TPU v7x, 32 devices: a whole 2x2x4 slice. The times are simulated.
32 devices in a mesh: gx: 4 (over y, x), gy: 4 (over z), gz: 2 (over core).
Axes of the slice: x: 2, y: 2, z: 4, core: 2. Of those that a mesh axis runs over, the one named last changes fastest.
Arguments:
- layer_east: float32 [16, 512, 512], P('gz', 'gy', 'gx'), may hold values from -6 to 6
- layer_north: float32 [16, 512, 512], P('gz', 'gy', 'gx'), may hold values from -6 to 6
- layer_press: float32 [16, 512, 512], P('gz', 'gy', 'gx'), may hold values from -6 to 6
- surface: float32 [512, 512], P('gy', 'gx'), may hold values from -3 to 3
- land_sea: int32 [512, 512], P('gy', 'gx'), may hold values 0 or 1
- bottom_level: int32 [512, 512], P('gy', 'gx'), may hold values from 12 to 16
- coriolis: float32 [512, 512], P('gy', 'gx'), may hold values from -1 to 1
- level_thick: float32 [16], P('gz'), may hold values from 0.25 to 0.3
Outputs:
- surface_next: float32 [512, 512], P('gy', 'gx')
- east_next: float32 [16, 512, 512], P('gz', 'gy', 'gx')
- north_next: float32 [16, 512, 512], P('gz', 'gy', 'gx')
All inputs are finite; a program needn't handle non-finite values. No bound on the sum of `land_sea` on one device may be relied on, other than what follows from the above.
Results may differ from a plain program's by a relative error of at most 0.00002.
Values sent between devices are 32-bit elements; how exact they have to be, the bound alone decides.
No kernel may reach another device: no remote copies, remote signals or barrier semaphores. Data moves between devices by JAX's collectives and lax.ppermute only.
A program may use at most 64 MiB of HBM per device.

v0:
```python
import jax
import jax.numpy as jnp
from jax import lax
from jax.sharding import PartitionSpec as P

SUBSTEPS = 4


COURANT = 0.25
VISCOSITY = 0.1


def extended(block, sides, width):
    for axis, dim in sides:
        count = lax.axis_size(axis)
        forward = [(i, i + 1) for i in range(count - 1)]
        forward.append((count - 1, 0))
        backward = [(target, source) for source, target in forward]
        low = lax.ppermute(
            lax.slice_in_dim(block, block.shape[dim] - width, None, axis=dim), axis, forward
        )
        high = lax.ppermute(lax.slice_in_dim(block, 0, width, axis=dim), axis, backward)
        block = jnp.concatenate([low, block, high], axis=dim)
    return block


def layer_terms(centre, east, west, north, south, coriolis):
    vel_east, vel_north, press, active = centre
    grad_x = 0.5 * (east[3] * (east[2] - press) + west[3] * (press - west[2]))
    grad_y = 0.5 * (north[3] * (north[2] - press) + south[3] * (press - south[2]))

    def friction(slot, value):
        return (
            east[3] * (east[slot] - value)
            + west[3] * (west[slot] - value)
            + north[3] * (north[slot] - value)
            + south[3] * (south[slot] - value)
        )

    tend_east = active * (-grad_x + coriolis * vel_north + VISCOSITY * friction(0, vel_east))
    tend_north = active * (-grad_y - coriolis * vel_east + VISCOSITY * friction(1, vel_north))
    return (tend_east, tend_north)


def surface_step(
    height, trans_east, trans_north, ocean_mid, depth, coriolis, force_east, force_north
):
    spread = 0.5 * (trans_east[1:-1, 2:] - trans_east[1:-1, :-2]) + 0.5 * (
        trans_north[2:, 1:-1] - trans_north[:-2, 1:-1]
    )
    height_mid = ocean_mid * (height[1:-1, 1:-1] - COURANT * spread)
    slope_x = 0.5 * (height_mid[1:-1, 2:] - height_mid[1:-1, :-2])
    slope_y = 0.5 * (height_mid[2:, 1:-1] - height_mid[:-2, 1:-1])
    ocean_core = ocean_mid[1:-1, 1:-1]
    old_east = trans_east[2:-2, 2:-2]
    old_north = trans_north[2:-2, 2:-2]
    new_east = ocean_core * (
        old_east + COURANT * (-depth * slope_x + coriolis * old_north + force_east)
    )
    new_north = ocean_core * (
        old_north + COURANT * (-depth * slope_y - coriolis * old_east + force_north)
    )
    return (height_mid, new_east, new_north)


def cropped(field, margin):
    return field[..., margin : field.shape[-2] - margin, margin : field.shape[-1] - margin]


def on_device(
    layer_east, layer_north, layer_press, surface, land_sea, bottom_level, coriolis, level_thick
):
    levels = layer_east.shape[0]
    ocean = land_sea.astype(jnp.float32)
    deepest = ocean * bottom_level.astype(jnp.float32)
    stacked = jnp.concatenate([layer_east, layer_north, layer_press, deepest[None]], axis=0)
    widened = extended(stacked, (("gx", 2), ("gy", 1)), 1)
    indices = (lax.axis_index("gz") * levels + jnp.arange(levels)).astype(jnp.float32)[
        :, None, None
    ]
    wide_deepest = widened[3 * levels]
    wide_active = (indices < wide_deepest[None]).astype(jnp.float32)
    fields = (
        widened[:levels],
        widened[levels : 2 * levels],
        widened[2 * levels : 3 * levels],
        wide_active,
    )
    centre = tuple((item[:, 1:-1, 1:-1] for item in fields))
    east = tuple((item[:, 1:-1, 2:] for item in fields))
    west = tuple((item[:, 1:-1, :-2] for item in fields))
    north = tuple((item[:, 2:, 1:-1] for item in fields))
    south = tuple((item[:, :-2, 1:-1] for item in fields))
    active = centre[3]
    tend_east, tend_north = layer_terms(centre, east, west, north, south, coriolis)
    thick = level_thick[:, None, None]
    masked_east = active * layer_east
    masked_north = active * layer_north
    partial_sums = jnp.stack(
        [
            jnp.sum(thick * tend_east, axis=0),
            jnp.sum(thick * tend_north, axis=0),
            jnp.sum(thick * masked_east, axis=0),
            jnp.sum(thick * masked_north, axis=0),
            jnp.sum(thick * active, axis=0),
        ]
    )
    totals = lax.psum(partial_sums, "gz")
    force_east, force_north, sum_east, sum_north, depth = (
        totals[0],
        totals[1],
        totals[2],
        totals[3],
        totals[4],
    )
    reach = 2 * SUBSTEPS
    state = jnp.stack(
        [surface, sum_east, sum_north, force_east, force_north, depth, coriolis, ocean]
    )
    region = extended(state, (("gx", 2), ("gy", 1)), reach)
    height, trans_east, trans_north = (region[0], region[1], region[2])
    for step in range(SUBSTEPS):
        ocean_mid = cropped(region[7], 2 * step + 1)
        statics = cropped(region[3:7], 2 * step + 2)
        height_mid, trans_east, trans_north = surface_step(
            height,
            trans_east,
            trans_north,
            ocean_mid,
            statics[2],
            statics[3],
            statics[0],
            statics[1],
        )
        height = height_mid[1:-1, 1:-1]
    timestep = SUBSTEPS * COURANT
    floor_depth = depth + (1.0 - ocean)
    east_next = active * (
        masked_east
        + timestep * tend_east
        + (trans_east - sum_east - timestep * force_east) / floor_depth
    )
    north_next = active * (
        masked_north
        + timestep * tend_north
        + (trans_north - sum_north - timestep * force_north) / floor_depth
    )
    return (height, east_next, north_next)


def solution(mesh):
    return jax.shard_map(
        on_device,
        mesh=mesh,
        in_specs=(
            P("gz", "gy", "gx"),
            P("gz", "gy", "gx"),
            P("gz", "gy", "gx"),
            P("gy", "gx"),
            P("gy", "gx"),
            P("gy", "gx"),
            P("gy", "gx"),
            P("gz"),
        ),
        out_specs=(P("gy", "gx"), P("gz", "gy", "gx"), P("gz", "gy", "gx")),
        check_vma=False,
    )
```

profile of v0, /device:TPU:0, one launch (start us, length us, event | category | flops | bytes accessed | tf_op | source)
XLA Modules:
  0.0 103.9 jit_solution(7889305889869582953)
XLA Ops:
  7.2 0.9 multiply_bitcast_fusion
  8.1 1.5 %pad_maximum_fusion = f32[25,128,128]{2,1,0:T(8,128)S(1)} fusion(f32[1,128,128]{2,1,0:T(8,128)S(1)} %multiply_bitcast_fusion, f32[8,128,128]{2,1,0:T(8,128)} %param.10, f32[8,128,128]{2,1,0:T(8,128)} %param.9, f32[8,128,128]{2,1,0:T(8,128)} %param.8), kind=kLoop, calls=%fused_computation.2 | loop fusion | flops 1228800 | bytes 3276800 | tf_op jit(solution)/shard_map/concatenate | solution.py:76
  9.6 0.6 fusion.122
  10.2 0.6 copy.40
  10.8 3.0 %collective-permute-start = (f32[25,128,1]{1,0,2:T(8,128)S(1)}, f32[25,128,1]{1,0,2:T(8,128)S(1)}, u32[]{:S(2)}, u32[]{:S(2)}) collective-permute-start(f32[25,128,1]{1,0,2:T(8,128)S(1)} %copy.40), channel_id=1, source_target_pairs={{0,8},{8,16},{16,24},{24,0},{1,9},{9,17},{17,25},{25,1},{2,10},{10... | collective-permute-start | bytes 38408 | tf_op jit(solution)/shard_map/ppermute | solution.py:19
  13.8 0.6 copy.41
  14.4 1.0 collective-permute-start.1
  15.4 1.1 %collective-permute-done = f32[25,128,1]{1,0,2:T(8,128)S(1)} collective-permute-done((f32[25,128,1]{1,0,2:T(8,128)S(1)}, f32[25,128,1]{1,0,2:T(8,128)S(1)}, u32[]{:S(2)}, u32[]{:S(2)}) %collective-permute-start) | collective-permute-done | bytes 12832 | tf_op jit(solution)/shard_map/ppermute | solution.py:19
  16.4 0.5 copy.42
  17.0 1.2 %collective-permute-done.1 = f32[25,128,1]{1,0,2:T(8,128)S(1)} collective-permute-done((f32[25,128,1]{1,0,2:T(8,128)S(1)}, f32[25,128,1]{1,0,2:T(8,128)S(1)}, u32[]{:S(2)}, u32[]{:S(2)}) %collective-permute-start.1) | collective-permute-done | bytes 12832 | tf_op jit(solution)/shard_map/ppermute | solution.py:22
  18.1 0.5 copy.43
  18.7 1.2 %pad_maximum_fusion.35 = (f32[25,1,130]{2,1,0:T(1,128)S(1)}, f32[25,1,130]{2,1,0:T(1,128)S(1)}) fusion(f32[25,128,1]{2,1,0:T(8,128)S(1)} %copy.43, f32[25,128,1]{2,1,0:T(8,128)S(1)} %copy.42, f32[1,128,128]{2,1,0:T(8,128)S(1)} %multiply_bitcast_fusion, f32[8,128,128]{2,1,0:T(8,128)} %param.10, f32[8,128,128]{2,1,0:T(8,128)} %param.9, f32[8,128,128]{2,1,0:T(8,128)} %param.8), kind=kLoop, calls=%fused_computation.225 | loop fusion | flops 32500 | bytes 1690000 | tf_op jit(solution)/shard_map/slice | solution.py:20
  19.9 1.6 %collective-permute-start.2 = (f32[25,1,130]{2,1,0:T(1,128)S(1)}, f32[25,1,130]{2,1,0:T(1,128)S(1)}, u32[]{:S(2)}, u32[]{:S(2)}) collective-permute-start(f32[25,1,130]{2,1,0:T(1,128)S(1)} %get-tuple-element.13), channel_id=1, source_target_pairs={{0,2},{2,4},{4,6},{6,0},{1,3},{3,5},{5,7},{7,1},{8,10},{10,12},{12... | collective-permute-start | bytes 39008 | tf_op jit(solution)/shard_map/ppermute | solution.py:19
  21.5 2.2 %collective-permute-start.3 = (f32[25,1,130]{2,1,0:T(1,128)S(1)}, f32[25,1,130]{2,1,0:T(1,128)S(1)}, u32[]{:S(2)}, u32[]{:S(2)}) collective-permute-start(f32[25,1,130]{2,1,0:T(1,128)S(1)} %get-tuple-element.14), channel_id=1, source_target_pairs={{2,0},{4,2},{6,4},{0,6},{3,1},{5,3},{7,5},{1,7},{10,8},{12,10},{14... | collective-permute-start | bytes 39008 | tf_op jit(solution)/shard_map/ppermute | solution.py:22
  23.8 1.9 %collective-permute-done.2 = f32[25,1,130]{2,1,0:T(1,128)S(1)} collective-permute-done((f32[25,1,130]{2,1,0:T(1,128)S(1)}, f32[25,1,130]{2,1,0:T(1,128)S(1)}, u32[]{:S(2)}, u32[]{:S(2)}) %collective-permute-start.2) | collective-permute-done | bytes 13032 | tf_op jit(solution)/shard_map/ppermute | solution.py:19
  26.0 7.8 %multiply_reduce_fusion = (f32[128,128]{1,0:T(8,128)S(1)}, f32[128,128]{1,0:T(8,128)S(1)}, f32[128,128]{1,0:T(8,128)S(1)}, f32[128,128]{1,0:T(8,128)S(1)}, f32[1...) fusion(f32[8,130,130]{2,1,0:T(8,128)S(1)} %compare_convert_fusion, f32[8]{0:T(128)S(1)} %copy-done.13, ...), kind=kLoop, calls=%fused_computation.71 | loop fusion | flops 15384576 | bytes 5753264 | tf_op jit(solution)/shard_map/reduce_sum | solution.py:105
  33.9 0.7 copy-done.11
  34.7 19.8 %all-reduce.2.cloned.1.call-done = f32[5,128,128]{2,1,0:T(8,128)} async-done(((f32[5,128,128]{2,1,0:T(8,128)}), f32[5,128,128]{2,1,0:T(8,128)}) %all-reduce.2.cloned.1.call-update) | async-done | bytes 327696 | tf_op jit(solution)/shard_map/psum | solution.py:108
  54.5 0.9 slice_dynamic-update-slice_fusion.1
  55.4 0.9 slice_dynamic-update-slice_fusion
  56.3 0.8 slice_dynamic-update-slice_fusion.2
  57.4 1.8 %collective-permute-start.4 = (f32[8,128,8]{2,1,0:T(8,128)S(1)}, f32[8,128,8]{2,1,0:T(8,128)S(1)}, u32[]{:S(2)}, u32[]{:S(2)}) collective-permute-start(f32[8,128,8]{2,1,0:T(8,128)S(1)} %get-tuple-element.33), channel_id=1, source_target_pairs={{0,8},{8,16},{16,24},{24,0},{1,9},{9,17},{17,25},{25,1},{2,10},{10... | collective-permute-start | bytes 98312 | tf_op jit(solution)/shard_map/ppermute | solution.py:19
  59.2 1.2 %collective-permute-start.5 = (f32[8,128,8]{2,1,0:T(8,128)S(1)}, f32[8,128,8]{2,1,0:T(8,128)S(1)}, u32[]{:S(2)}, u32[]{:S(2)}) collective-permute-start(f32[8,128,8]{2,1,0:T(8,128)S(1)} %get-tuple-element.34), channel_id=1, source_target_pairs={{8,0},{16,8},{24,16},{0,24},{9,1},{17,9},{25,17},{1,25},{10,2},{18... | collective-permute-start | bytes 98312 | tf_op jit(solution)/shard_map/ppermute | solution.py:22
  60.4 12.8 %collective-permute-done.4 = f32[8,128,8]{2,1,0:T(8,128)S(1)} collective-permute-done((f32[8,128,8]{2,1,0:T(8,128)S(1)}, f32[8,128,8]{2,1,0:T(8,128)S(1)}, u32[]{:S(2)}, u32[]{:S(2)}) %collective-permute-start.4) | collective-permute-done | bytes 32800 | tf_op jit(solution)/shard_map/ppermute | solution.py:19
  73.2 10.8 %collective-permute-done.5 = f32[8,128,8]{2,1,0:T(8,128)S(1)} collective-permute-done((f32[8,128,8]{2,1,0:T(8,128)S(1)}, f32[8,128,8]{2,1,0:T(8,128)S(1)}, u32[]{:S(2)}, u32[]{:S(2)}) %collective-permute-start.5) | collective-permute-done | bytes 32800 | tf_op jit(solution)/shard_map/ppermute | solution.py:22
  84.1 1.5 %collective-permute-start.6 = (f32[8,8,144]{2,1,0:T(8,128)S(1)}, f32[8,8,144]{2,1,0:T(8,128)S(1)}, u32[]{:S(2)}, u32[]{:S(2)}) collective-permute-start(f32[8,8,144]{2,1,0:T(8,128)S(1)} %get-tuple-element.23), channel_id=1, source_target_pairs={{0,2},{2,4},{4,6},{6,0},{1,3},{3,5},{5,7},{7,1},{8,10},{10,12},{12... | collective-permute-start | bytes 110600 | tf_op jit(solution)/shard_map/ppermute | solution.py:19
  85.6 2.3 %collective-permute-start.7 = (f32[8,8,144]{2,1,0:T(8,128)S(1)}, f32[8,8,144]{2,1,0:T(8,128)S(1)}, u32[]{:S(2)}, u32[]{:S(2)}) collective-permute-start(f32[8,8,144]{2,1,0:T(8,128)S(1)} %get-tuple-element.24), channel_id=1, source_target_pairs={{2,0},{4,2},{6,4},{0,6},{3,1},{5,3},{7,5},{1,7},{10,8},{12,10},{14... | collective-permute-start | bytes 110600 | tf_op jit(solution)/shard_map/ppermute | solution.py:22
  88.0 2.7 %collective-permute-done.6 = f32[8,8,144]{2,1,0:T(8,128)S(1)} collective-permute-done((f32[8,8,144]{2,1,0:T(8,128)S(1)}, f32[8,8,144]{2,1,0:T(8,128)S(1)}, u32[]{:S(2)}, u32[]{:S(2)}) %collective-permute-start.6) | collective-permute-done | bytes 36896 | tf_op jit(solution)/shard_map/ppermute | solution.py:19
  90.7 0.5 pad_maximum_fusion.1
  91.5 0.5 fusion.50
  93.7 0.8 fusion.102
  94.5 2.5 %add_multiply_fusion = (f32[8,128,128]{2,1,0:T(8,128)}, f32[8,128,128]{2,1,0:T(8,128)}) fusion(f32[8,128,128]{2,1,0:T(8,128)S(1)} %copy-done.7, f32[8,130,130]{2,1,0:T(8,128)} %copy-done, f32[128,128]{1,0:T(8,128)S(1)} %get-tuple-element.31, f32[8,128,128]{2,1,0:T(8,128)S(1)} %copy-done.2, f32[128,128]{1,0:T(8,128)S(1)} %get-tuple-element.32, ...), kind=kLoop, calls=%fused_computation.69 | loop fusion | flops 1048576 | bytes 3801088 | tf_op jit(solution)/shard_map/mul | solution.py:143
  (51 shorter events, 2.7 us)
Async XLA Ops:
  7.2 47.3 %all-reduce.2.cloned.1.call-start = ((), (), s32[]{:S(2)}) async-start(), calls=%async_computation | async-start | bytes 655360 | tf_op jit(solution)/shard_map/psum | solution.py:108
  10.8 5.7 %collective-permute-start = (f32[25,128,1]{1,0,2:T(8,128)S(1)}, f32[25,128,1]{1,0,2:T(8,128)S(1)}, u32[]{:S(2)}, u32[]{:S(2)}) collective-permute-start(f32[25,128,1]{1,0,2:T(8,128)S(1)} %copy.40), channel_id=1, source_target_pairs={{0,8},{8,16},{16,24},{24,0},{1,9},{9,17},{17,25},{25,1},{2,10},{10... | collective-permute-start | bytes 38408 | tf_op jit(solution)/shard_map/ppermute | solution.py:19
  14.4 3.8 %collective-permute-start.1 = (f32[25,128,1]{1,0,2:T(8,128)S(1)}, f32[25,128,1]{1,0,2:T(8,128)S(1)}, u32[]{:S(2)}, u32[]{:S(2)}) collective-permute-start(f32[25,128,1]{1,0,2:T(8,128)S(1)} %copy.41), channel_id=1, source_target_pairs={{8,0},{16,8},{24,16},{0,24},{9,1},{17,9},{25,17},{1,25},{10,2},{18... | collective-permute-start | bytes 38408 | tf_op jit(solution)/shard_map/ppermute | solution.py:22
  18.7 7.0 %copy-start.1 = (f32[8,128,128]{2,1,0:T(8,128)S(1)}, f32[8,128,128]{2,1,0:T(8,128)}, u32[]{:S(2)}) copy-start(f32[8,128,128]{2,1,0:T(8,128)} %param.9) | copy-start | bytes 1572868
  18.7 7.0 %copy-start.3 = (f32[8,128,128]{2,1,0:T(8,128)S(1)}, f32[8,128,128]{2,1,0:T(8,128)}, u32[]{:S(2)}) copy-start(f32[8,128,128]{2,1,0:T(8,128)} %param.8) | copy-start | bytes 1572868
  18.7 7.0 %copy-start.5 = (f32[8,128,128]{2,1,0:T(8,128)S(1)}, f32[8,128,128]{2,1,0:T(8,128)}, u32[]{:S(2)}) copy-start(f32[8,128,128]{2,1,0:T(8,128)} %param.10) | copy-start | bytes 1572868
  19.9 5.7 %collective-permute-start.2 = (f32[25,1,130]{2,1,0:T(1,128)S(1)}, f32[25,1,130]{2,1,0:T(1,128)S(1)}, u32[]{:S(2)}, u32[]{:S(2)}) collective-permute-start(f32[25,1,130]{2,1,0:T(1,128)S(1)} %get-tuple-element.13), channel_id=1, source_target_pairs={{0,2},{2,4},{4,6},{6,0},{1,3},{3,5},{5,7},{7,1},{8,10},{10,12},{12... | collective-permute-start | bytes 39008 | tf_op jit(solution)/shard_map/ppermute | solution.py:19
  21.5 4.1 %collective-permute-start.3 = (f32[25,1,130]{2,1,0:T(1,128)S(1)}, f32[25,1,130]{2,1,0:T(1,128)S(1)}, u32[]{:S(2)}, u32[]{:S(2)}) collective-permute-start(f32[25,1,130]{2,1,0:T(1,128)S(1)} %get-tuple-element.14), channel_id=1, source_target_pairs={{2,0},{4,2},{6,4},{0,6},{3,1},{5,3},{7,5},{1,7},{10,8},{12,10},{14... | collective-permute-start | bytes 39008 | tf_op jit(solution)/shard_map/ppermute | solution.py:22
  23.8 2.2 %copy-start.9 = (f32[128,128]{1,0:T(8,128)S(1)}, f32[128,128]{1,0:T(8,128)}, u32[]{:S(2)}) copy-start(f32[128,128]{1,0:T(8,128)} %param.14) | copy-start | bytes 196612
  23.8 2.2 %copy-start.13 = (f32[8]{0:T(128)S(1)}, f32[8]{0:T(128)}, u32[]{:S(2)}) copy-start(f32[8]{0:T(128)} %param.15) | copy-start | bytes 100
  25.9 7.9 %copy-start = (f32[8,130,130]{2,1,0:T(8,128)}, f32[8,130,130]{2,1,0:T(8,128)S(1)}, u32[]{:S(2)}) copy-start(f32[8,130,130]{2,1,0:T(8,128)S(1)} %compare_convert_fusion) | copy-start | bytes 1622404
  26.0 8.7 %copy-start.12 = (f32[128,128]{1,0:T(8,128)S(1)}, f32[128,128]{1,0:T(8,128)}, u32[]{:S(2)}) copy-start(f32[128,128]{1,0:T(8,128)} %param.11) | copy-start | bytes 196612
  33.8 23.4 %copy-start.10 = (s32[128,128]{1,0:T(8,128)S(1)}, s32[128,128]{1,0:T(8,128)}, u32[]{:S(2)}) copy-start(s32[128,128]{1,0:T(8,128)} %param.12) | copy-start | bytes 196612
  33.9 0.7 copy-start.11
  57.4 15.7 %collective-permute-start.4 = (f32[8,128,8]{2,1,0:T(8,128)S(1)}, f32[8,128,8]{2,1,0:T(8,128)S(1)}, u32[]{:S(2)}, u32[]{:S(2)}) collective-permute-start(f32[8,128,8]{2,1,0:T(8,128)S(1)} %get-tuple-element.33), channel_id=1, source_target_pairs={{0,8},{8,16},{16,24},{24,0},{1,9},{9,17},{17,25},{25,1},{2,10},{10... | collective-permute-start | bytes 98312 | tf_op jit(solution)/shard_map/ppermute | solution.py:19
  59.2 24.8 %collective-permute-start.5 = (f32[8,128,8]{2,1,0:T(8,128)S(1)}, f32[8,128,8]{2,1,0:T(8,128)S(1)}, u32[]{:S(2)}, u32[]{:S(2)}) collective-permute-start(f32[8,128,8]{2,1,0:T(8,128)S(1)} %get-tuple-element.34), channel_id=1, source_target_pairs={{8,0},{16,8},{24,16},{0,24},{9,1},{17,9},{25,17},{1,25},{10,2},{18... | collective-permute-start | bytes 98312 | tf_op jit(solution)/shard_map/ppermute | solution.py:22
  84.1 6.6 %collective-permute-start.6 = (f32[8,8,144]{2,1,0:T(8,128)S(1)}, f32[8,8,144]{2,1,0:T(8,128)S(1)}, u32[]{:S(2)}, u32[]{:S(2)}) collective-permute-start(f32[8,8,144]{2,1,0:T(8,128)S(1)} %get-tuple-element.23), channel_id=1, source_target_pairs={{0,2},{2,4},{4,6},{6,0},{1,3},{3,5},{5,7},{7,1},{8,10},{10,12},{12... | collective-permute-start | bytes 110600 | tf_op jit(solution)/shard_map/ppermute | solution.py:19
  85.6 5.1 %collective-permute-start.7 = (f32[8,8,144]{2,1,0:T(8,128)S(1)}, f32[8,8,144]{2,1,0:T(8,128)S(1)}, u32[]{:S(2)}, u32[]{:S(2)}) collective-permute-start(f32[8,8,144]{2,1,0:T(8,128)S(1)} %get-tuple-element.24), channel_id=1, source_target_pairs={{2,0},{4,2},{6,4},{0,6},{3,1},{5,3},{7,5},{1,7},{10,8},{12,10},{14... | collective-permute-start | bytes 110600 | tf_op jit(solution)/shard_map/ppermute | solution.py:22
  92.7 1.0 copy-start.8
  92.9 1.6 %copy-start.2 = (f32[8,128,128]{2,1,0:T(8,128)S(1)}, f32[8,128,128]{2,1,0:T(8,128)}, u32[]{:S(2)}) copy-start(f32[8,128,128]{2,1,0:T(8,128)} %param.9) | copy-start | bytes 1572868
  93.0 1.6 %copy-start.4 = (f32[8,128,128]{2,1,0:T(8,128)S(1)}, f32[8,128,128]{2,1,0:T(8,128)}, u32[]{:S(2)}) copy-start(f32[8,128,128]{2,1,0:T(8,128)} %param.8) | copy-start | bytes 1572868
  93.0 1.6 %copy-start.6 = (f32[8,128,128]{2,1,0:T(8,128)S(1)}, f32[8,128,128]{2,1,0:T(8,128)}, u32[]{:S(2)}) copy-start(f32[8,128,128]{2,1,0:T(8,128)} %get-tuple-element.11) | copy-start | bytes 1572868
  93.0 1.6 %copy-start.7 = (f32[8,128,128]{2,1,0:T(8,128)S(1)}, f32[8,128,128]{2,1,0:T(8,128)}, u32[]{:S(2)}) copy-start(f32[8,128,128]{2,1,0:T(8,128)} %get-tuple-element.12) | copy-start | bytes 1572868
Sparse Core Ops, SparseCore 0:
  34.8 19.6 all-reduce.1
where the time goes:
time: 104 us
  waiting for transfers between devices  50.2 us (48%)
  other arithmetic  17.9 us (17%)
  starting transfers between devices  14.7 us (14%)
  between operations  14.4 us (14%)
  local copies, waits for them, and re-layouts  6.62 us (6%)
    psum x1, waiting for transfers between devices, on_device(): totals = lax.psum(partial_sums, 'gz')  19.8 us
    ppermute x4, waiting for transfers between devices, extended(): lax.ppermute(lax.slice_in_dim(block, block.shape[dim] - width, None, axis...  18.4 us
    ppermute x4, waiting for transfers between devices, extended(): lax.ppermute(lax.slice_in_dim(block, 0, width, axis=dim), axis, backward)  12 us
    ppermute x4, starting transfers between devices, extended(): lax.ppermute(lax.slice_in_dim(block, block.shape[dim] - width, None, axis...  7.97 us
    reduce_sum x1, other arithmetic, on_device(): jnp.sum(thick * active, axis=0)  7.85 us
    ppermute x4, starting transfers between devices, extended(): lax.ppermute(lax.slice_in_dim(block, 0, width, axis=dim), axis, backward)  6.73 us
    unnamed x37, local copies, waits for them, and re-layouts  3.52 us
    mul x1, other arithmetic, on_device(): active * (masked_north + timestep * tend_north + (trans_north - sum_north...  2.49 us
  transfers between devices with their start and end apart: 9, of which 7 were waited for; matrix products, arithmetic and copies ran while one was open for 1% of the time, Pallas kernels for 0%

commit v1 on v0

v1 whole, which is shorter than its diff:
```python
import functools

import jax
import jax.numpy as jnp
from jax import lax
from jax.experimental import pallas as pl
from jax.experimental.pallas import tpu as pltpu
from jax.sharding import PartitionSpec as P

SUBSTEPS = 4
COURANT = 0.25
VISCOSITY = 0.1
REACH = 2 * SUBSTEPS
TIMESTEP = SUBSTEPS * COURANT
CHUNK = 2 * REACH

F32 = jnp.float32


class Sizes:
    def __init__(self, levels, rows, cols):
        self.levels = levels
        self.rows = rows
        self.cols = cols
        self.top = 2 * REACH
        self.tall = rows + 4 * REACH
        self.wide = rows + 2 * REACH
        self.slots = cols // REACH
        self.half = cols // 2
        self.planes = 3 * levels + 3
        assert 2 * levels * REACH == cols
        assert rows % CHUNK == 0


def turned(value, shift):
    lanes = value.shape[-1]
    shift = shift % lanes
    if shift == 0:
        return value
    return pltpu.roll(value, shift, axis=1)


def lane_ids(rows, cols):
    return lax.broadcasted_iota(jnp.int32, (rows, cols), 1)


def pack_edges(size, load, rows):
    lane = lane_ids(rows, size.cols)
    slot_of = lane // REACH
    results = []
    for first, count in ((0, 2 * size.levels), (2 * size.levels, size.levels + 3)):
        low = jnp.zeros((rows, size.cols), F32)
        high = jnp.zeros((rows, size.cols), F32)
        for slot in range(count):
            value = turned(load(first + slot), slot * REACH)
            low = jnp.where(slot_of == slot, value, low)
            high = jnp.where(slot_of == (slot - 1) % size.slots, value, high)
        results.append((low, turned(high, REACH)))
    return results


def pack_columns(
    size, east, north, press, surface, land, bottom, coriolis,
    ext, low_out, high_out, whole, sems,
):
    levels, top, rows = size.levels, size.top, size.rows
    span = pl.ds(top, rows)
    copies = []
    for slot, field in enumerate((east, north, press)):
        target = ext.at[pl.ds(slot * levels, levels), span, :]
        copies.append(pltpu.make_async_copy(field, target, sems.at[slot]))
    copies.append(pltpu.make_async_copy(surface, ext.at[3 * levels, span, :], sems.at[3]))
    copies.append(pltpu.make_async_copy(coriolis, ext.at[3 * levels + 2, span, :], sems.at[4]))
    copies.append(pltpu.make_async_copy(land, whole.at[0], sems.at[5]))
    copies.append(pltpu.make_async_copy(bottom, whole.at[1], sems.at[6]))
    for copy in copies:
        copy.start()
    for copy in copies[3:]:
        copy.wait()
    ext[3 * levels + 1, top : top + rows, :] = whole[0].astype(F32) * whole[1].astype(F32)
    for copy in copies[:3]:
        copy.wait()

    @pl.loop(0, rows // CHUNK)
    def _(step):
        start = pl.multiple_of(step * CHUNK, CHUNK)
        packed = pack_edges(size, lambda plane: ext[plane, pl.ds(top + start, CHUNK), :], CHUNK)
        for index, (low, high) in enumerate(packed):
            low_out[index, pl.ds(start, CHUNK), :] = low
            high_out[index, pl.ds(start, CHUNK), :] = high


def pack_rows(size, ext, west, east, south_out, north_out):
    planes, top, rows = size.planes, size.top, size.rows
    south_out[:planes] = ext[:, top : top + REACH, :]
    north_out[:planes] = ext[:, top + rows - REACH : top + rows, :]
    for index, strip in enumerate((west, east)):
        at = planes + 2 * index
        south_out[at : at + 2] = strip[:, :REACH, :]
        north_out[at : at + 2] = strip[:, rows - REACH :, :]


def spread_slot(size, value, slot):
    lane = lane_ids(value.shape[0], size.cols)
    value = jnp.where(lane // REACH == slot, value, 0.0)
    shift = REACH
    while shift < size.cols:
        value = value + turned(value, shift)
        shift *= 2
    return value


def layer_kernel(
    size, thick, ext_in, low, high, west, east, south, north,
    ext, base, sums, statics, strips, own,
):
    del ext_in
    levels, top, rows, cols = size.levels, size.top, size.rows, size.cols
    planes, half = size.planes, size.half
    first_level = (lax.axis_index("gz") * levels).astype(F32)
    below, above = top - REACH, top + rows

    ext[:, below:top, :] = south[:planes]
    ext[:, above : above + REACH, :] = north[:planes]
    VAL, PRS, XVAL, XPRS, CNT, XCNT, COR, RAW = range(8)
    for side, strip in enumerate((west, east)):
        at = planes + 2 * side
        for index, plane in ((0, VAL), (1, RAW)):
            strips[side, plane, below:top, :] = south[at + index]
            strips[side, plane, top:above, :] = strip[index]
            strips[side, plane, above : above + REACH, :] = north[at + index]
    for side, packed in enumerate((low, high)):
        for index in range(2):
            own[side, index, top:above, :] = packed[index]
    for start in (below, above):
        packed = pack_edges(size, lambda plane: ext[plane, start : start + REACH, :], REACH)
        for index in range(2):
            for side in range(2):
                own[side, index, start : start + REACH, :] = packed[index][side]

    @pl.loop(0, size.wide // CHUNK)
    def _(step):
        start = pl.multiple_of(below + step * CHUNK, REACH)
        here = pl.ds(start, CHUNK)
        lane = lane_ids(CHUNK, cols)
        inner = lane % REACH
        for side in range(2):
            edge, toward = ((REACH - 1, -1), (0, 1))[side]
            value, raw = strips[side, VAL, here, :], strips[side, RAW, here, :]

            def beside(array, index):
                mine = turned(own[side, index, here, :], edge if side == 0 else -(REACH - 1))
                return jnp.where(inner == edge, mine, turned(array, toward))

            x_value, x_raw = beside(value, 0), beside(raw, 1)

            def both(array):
                array = jnp.where(lane < half, array, 0.0)
                return array + turned(array, half)

            strips[side, PRS, here, :] = both(raw)
            strips[side, XVAL, here, :] = x_value
            strips[side, XPRS, here, :] = both(x_raw)
            strips[side, CNT, here, :] = spread_slot(size, raw, levels + 1)
            strips[side, XCNT, here, :] = spread_slot(size, jnp.minimum(raw, x_raw), levels + 1)
            strips[side, COR, here, :] = spread_slot(size, raw, levels + 2)
        place = pl.ds(step * CHUNK, CHUNK)
        for index in range(3):
            slot = levels + index
            left = turned(strips[0, RAW, here, :], (size.slots - 1 - slot) * REACH)
            right = turned(strips[1, RAW, here, :], -slot * REACH)
            statics[index, place, :] = jnp.where(
                lane >= cols - REACH, left, jnp.where(lane < REACH, right, 0.0)
            )

    @pl.loop(0, size.wide // CHUNK)
    def _(step):
        start = pl.multiple_of(below + step * CHUNK, REACH)
        here, over, under = (pl.ds(start + move, CHUNK) for move in (0, 1, -1))
        place = pl.ds(step * CHUNK, CHUNK)
        lane = lane_ids(CHUNK, cols)
        slot_of, inner = lane // REACH, lane % REACH
        level_of = (slot_of % levels).astype(F32) + first_level
        eastward = lane < half
        weight = jnp.zeros((CHUNK, cols), F32)
        for k in range(levels):
            weight = jnp.where(slot_of % levels == k, thick[k], weight)

        merged, wet_sides, faces = [], [], []
        for side in range(2):
            value, prs = strips[side, VAL, here, :], strips[side, PRS, here, :]
            cnt, cor = strips[side, CNT, here, :], strips[side, COR, here, :]
            x_value, x_prs = strips[side, XVAL, here, :], strips[side, XPRS, here, :]
            x_wet = level_of < strips[side, XCNT, here, :]
            change = VISCOSITY * (x_value - value)
            push = jnp.where(eastward, 0.5 * (x_prs - prs), 0.0)
            if side == 1:
                change, push = -change, -push
            ahead = jnp.where(x_wet, change - push, 0.0)
            behind = jnp.where(x_wet, change + push, 0.0)
            if side == 0:
                faces.append(behind)
                tend = ahead - turned(behind, 1)
            else:
                faces.append(ahead)
                tend = turned(ahead, -1) - behind
            wet = level_of < cnt
            n_wet = level_of < jnp.minimum(cnt, strips[side, CNT, over, :])
            s_wet = level_of < jnp.minimum(cnt, strips[side, CNT, under, :])
            n_val = jnp.where(n_wet, strips[side, VAL, over, :] - value, 0.0)
            s_val = jnp.where(s_wet, strips[side, VAL, under, :] - value, 0.0)
            n_prs = jnp.where(n_wet, strips[side, PRS, over, :] - prs, 0.0)
            s_prs = jnp.where(s_wet, prs - strips[side, PRS, under, :], 0.0)
            turn = cor * turned(value, half)
            turn = jnp.where(wet, jnp.where(eastward, turn, -turn), 0.0)
            tend = tend + VISCOSITY * (n_val + s_val) + turn
            tend = tend - jnp.where(eastward, 0.0, 0.5 * (n_prs + s_prs))
            force = weight * tend
            total = weight * jnp.where(wet, value, 0.0)
            quarter = half // 2
            force = force + turned(force, quarter)
            total = total + turned(total, -quarter)
            both = jnp.where(lane % half >= quarter, force, total)
            shift = quarter // 2
            while shift >= REACH:
                both = both + turned(both, shift)
                shift //= 2
            merged.append(both)
            wet_sides.append(jnp.where(wet, weight, 0.0))
        deep = jnp.where(eastward, wet_sides[0], wet_sides[1])
        shift = half // 2
        while shift >= REACH:
            deep = deep + turned(deep, shift)
            shift //= 2
        quarter_slots = size.slots // 4
        which = slot_of % quarter_slots
        sums[5, place, :] = jnp.where(
            which == quarter_slots - 1,
            merged[0],
            jnp.where(
                which == quarter_slots - 2,
                turned(merged[1], -REACH),
                turned(deep, -2 * REACH),
            ),
        )
        sides = jnp.where(inner == REACH - 1, faces[0], turned(faces[1], REACH - 2))

        cnt = ext[3 * levels + 1, here, :]
        cor = ext[3 * levels + 2, here, :]
        cnt_x = jnp.minimum(cnt, turned(cnt, -1))
        cnt_n = jnp.minimum(cnt, ext[3 * levels + 1, over, :])
        cnt_s = jnp.minimum(cnt, ext[3 * levels + 1, under, :])
        at_low, at_high = lane == 0, lane == cols - 1
        force_e = force_n = sum_e = sum_n = depth = jnp.zeros((CHUNK, cols), F32)
        for k in range(levels):
            level = first_level + k
            wet, wet_x, wet_n, wet_s = (level < c for c in (cnt, cnt_x, cnt_n, cnt_s))
            u, v, p = (ext[slot * levels + k, here, :] for slot in range(3))
            change_u = jnp.where(wet_x, turned(u, -1) - u, 0.0) * VISCOSITY
            change_v = jnp.where(wet_x, turned(v, -1) - v, 0.0) * VISCOSITY
            push = jnp.where(wet_x, turned(p, -1) - p, 0.0) * 0.5
            side_u = turned(sides, -(k * REACH + REACH - 1))
            side_v = turned(sides, -((levels + k) * REACH + REACH - 1))
            ahead_u = jnp.where(at_high, side_u, change_u - push)
            ahead_v = jnp.where(at_high, side_v, change_v)
            behind_u = jnp.where(at_low, side_u, turned(change_u + push, 1))
            behind_v = jnp.where(at_low, side_v, turned(change_v, 1))

            def vertical(slot, value):
                plane = slot * levels + k
                return (
                    jnp.where(wet_n, ext[plane, over, :] - value, 0.0),
                    jnp.where(wet_s, ext[plane, under, :] - value, 0.0),
                )

            n_u, s_u = vertical(0, u)
            n_v, s_v = vertical(1, v)
            n_p, s_p = vertical(2, p)
            wet_u, wet_v = jnp.where(wet, u, 0.0), jnp.where(wet, v, 0.0)
            tend_e = (ahead_u - behind_u) + cor * wet_v + VISCOSITY * (n_u + s_u)
            tend_n = (
                (ahead_v - behind_v) - cor * wet_u + VISCOSITY * (n_v + s_v) - 0.5 * (n_p - s_p)
            )
            base[0, k, place, :] = wet_u + TIMESTEP * tend_e
            base[1, k, place, :] = wet_v + TIMESTEP * tend_n
            force_e = force_e + thick[k] * tend_e
            force_n = force_n + thick[k] * tend_n
            sum_e = sum_e + thick[k] * wet_u
            sum_n = sum_n + thick[k] * wet_v
            depth = depth + jnp.where(wet, thick[k], 0.0)
        for index, total in enumerate((force_e, force_n, sum_e, sum_n, depth)):
            sums[index, place, :] = total


def surface_kernel(
    size, ext, base, statics, mine, other,
    height_out, east_out, north_out,
    state, fixed, drive, result, sems,
):
    levels, rows, cols, wide = size.levels, size.rows, size.cols, size.wide
    top = size.top
    first_level = (lax.axis_index("gz") * levels).astype(F32)
    lane = lane_ids(CHUNK, cols)
    H, TE, TN = range(3)
    OC, DP, CO, FE, FN = range(5)
    chunks = [REACH + at for at in range(0, wide, CHUNK)]

    @pl.loop(0, wide // CHUNK)
    def _(step):
        place = pl.ds(pl.multiple_of(step * CHUNK, CHUNK), CHUNK)
        here = pl.ds(pl.multiple_of(REACH + step * CHUNK, REACH), CHUNK)
        wider = pl.ds(pl.multiple_of(top - REACH + step * CHUNK, REACH), CHUNK)
        total = [mine[index, place, :] + other[index, place, :] for index in range(6)]
        strip = total[5]
        last = size.slots - 1
        quarter = size.slots // 4

        def outer(left, right):
            return jnp.where(
                lane >= cols - REACH,
                turned(strip, (last - left) * REACH),
                jnp.where(lane < REACH, turned(strip, -right * REACH), 0.0),
            )

        fixed[0, FE, here, :] = total[0]
        fixed[0, FN, here, :] = total[1]
        state[0, TE, here, :] = total[2]
        state[0, TN, here, :] = total[3]
        drive[0, place, :] = total[2] + TIMESTEP * total[0]
        drive[1, place, :] = total[3] + TIMESTEP * total[1]
        fixed[0, DP, here, :] = total[4]
        fixed[1, FE, here, :] = outer(2 * quarter - 1, 2 * quarter - 2)
        fixed[1, FN, here, :] = outer(4 * quarter - 1, 4 * quarter - 2)
        state[1, TE, here, :] = outer(quarter - 1, quarter - 2)
        state[1, TN, here, :] = outer(3 * quarter - 1, 3 * quarter - 2)
        fixed[1, DP, here, :] = outer(2 * quarter - 3, 4 * quarter - 3)
        state[0, H, here, :] = ext[3 * levels, wider, :]
        state[1, H, here, :] = statics[0, place, :]
        fixed[0, OC, here, :] = jnp.where(ext[3 * levels + 1, wider, :] > 0, 1.0, 0.0)
        fixed[1, OC, here, :] = jnp.where(statics[1, place, :] > 0, 1.0, 0.0)
        fixed[0, CO, here, :] = ext[3 * levels + 2, wider, :]
        fixed[1, CO, here, :] = statics[2, place, :]

    def difference_x(field, here):
        inside, outside = state[0, field, here, :], state[1, field, here, :]
        in_e, out_e = turned(inside, -1), turned(outside, -1)
        in_w, out_w = turned(inside, 1), turned(outside, 1)
        at_high, at_low = lane == cols - 1, lane == 0
        return (
            0.5 * (jnp.where(at_high, out_e, in_e) - jnp.where(at_low, out_w, in_w)),
            0.5 * (jnp.where(at_high, in_e, out_e) - jnp.where(at_low, in_w, out_w)),
        )

    def difference_y(part, field, start):
        above = state[part, field, start + 1 : start + 1 + CHUNK, :]
        return 0.5 * (above - state[part, field, start - 1 : start - 1 + CHUNK, :])

    for _ in range(SUBSTEPS):
        for start in chunks:
            here = slice(start, start + CHUNK)
            across = difference_x(TE, here)
            for part in range(2):
                spread = across[part] + difference_y(part, TN, start)
                height = state[part, H, here, :] - COURANT * spread
                state[part, H, here, :] = fixed[part, OC, here, :] * height
        for start in chunks:
            here = slice(start, start + CHUNK)
            across = difference_x(H, here)
            for part in range(2):
                slope_y = difference_y(part, H, start)
                te, tn = state[part, TE, here, :], state[part, TN, here, :]
                oc, dp, co, fe, fn = (fixed[part, index, here, :] for index in range(5))
                state[part, TE, here, :] = oc * (
                    te + COURANT * (-dp * across[part] + co * tn + fe)
                )
                state[part, TN, here, :] = oc * (tn + COURANT * (-dp * slope_y - co * te + fn))

    height_copy = pltpu.make_async_copy(
        state.at[0, H, pl.ds(top, rows), :], height_out, sems.at[0]
    )
    height_copy.start()
    inner = slice(top, top + rows)
    floor_depth = fixed[0, DP, inner, :] + (1.0 - fixed[0, OC, inner, :])
    for index, field in enumerate((TE, TN)):
        gain = state[0, field, inner, :] - drive[index, REACH : REACH + rows, :]
        drive[index, REACH : REACH + rows, :] = gain / floor_depth
    copies = [height_copy]
    for k in range(levels):
        wet = first_level + k < ext[3 * levels + 1, top : top + rows, :]
        for index, out in enumerate((east_out, north_out)):
            change = jnp.where(wet, drive[index, REACH : REACH + rows, :], 0.0)
            result[index, k] = base[index, k, REACH : REACH + rows, :] + change
            copy = pltpu.make_async_copy(
                result.at[index, k], out.at[k], sems.at[1 + 2 * k + index]
            )
            copy.start()
            copies.append(copy)
    for copy in copies:
        copy.wait()


VMEM = pl.BlockSpec(memory_space=pltpu.VMEM)
SMEM = pl.BlockSpec(memory_space=pltpu.SMEM)
HBM = pl.BlockSpec(memory_space=pltpu.HBM)
PARAMS = pltpu.CompilerParams(vmem_limit_bytes=24 * 1024 * 1024)


def shaped(*shape):
    return jax.ShapeDtypeStruct(shape, F32)


def ring(axis):
    count = lax.axis_size(axis)
    forward = [(i, (i + 1) % count) for i in range(count)]
    return forward, [(target, source) for source, target in forward]


def on_device(
    layer_east, layer_north, layer_press, surface, land_sea, bottom_level, coriolis, level_thick
):
    size = Sizes(*layer_east.shape)
    levels, rows, cols = layer_east.shape
    tall, wide = size.tall, size.wide
    ext, low, high = pl.pallas_call(
        functools.partial(pack_columns, size),
        in_specs=[HBM] * 7,
        out_specs=[VMEM] * 3,
        out_shape=[
            shaped(size.planes, tall, cols), shaped(2, rows, cols), shaped(2, rows, cols)
        ],
        scratch_shapes=[
            pltpu.VMEM((2, rows, cols), jnp.int32), pltpu.SemaphoreType.DMA((7,))
        ],
        compiler_params=PARAMS,
        name="pack_columns",
    )(
        *(
            pltpu.with_memory_space_constraint(array, pltpu.HBM)
            for array in (
                layer_east, layer_north, layer_press, surface, land_sea, bottom_level, coriolis
            )
        )
    )
    forward, backward = ring("gx")
    west = lax.ppermute(high, "gx", forward)
    east = lax.ppermute(low, "gx", backward)
    south_out, north_out = pl.pallas_call(
        functools.partial(pack_rows, size),
        in_specs=[VMEM] * 3,
        out_specs=[VMEM] * 2,
        out_shape=[shaped(size.planes + 4, REACH, cols)] * 2,
        compiler_params=PARAMS,
        name="pack_rows",
    )(ext, west, east)
    forward, backward = ring("gy")
    south = lax.ppermute(north_out, "gy", forward)
    north = lax.ppermute(south_out, "gy", backward)
    ext, base, sums, statics = pl.pallas_call(
        functools.partial(layer_kernel, size),
        in_specs=[SMEM] + [VMEM] * 7,
        out_specs=[VMEM] * 4,
        out_shape=[
            shaped(size.planes, tall, cols),
            shaped(2, levels, wide, cols),
            shaped(6, wide, cols),
            shaped(3, wide, cols),
        ],
        scratch_shapes=[
            pltpu.VMEM((2, 8, tall, cols), F32), pltpu.VMEM((2, 2, tall, cols), F32)
        ],
        input_output_aliases={1: 0},
        compiler_params=PARAMS,
        name="layer_terms",
    )(level_thick, ext, low, high, west, east, south, north)
    others = lax.ppermute(sums, "gz", ring("gz")[0])
    height, east_next, north_next = pl.pallas_call(
        functools.partial(surface_kernel, size),
        in_specs=[VMEM] * 5,
        out_specs=[HBM] * 3,
        out_shape=[shaped(rows, cols), shaped(levels, rows, cols), shaped(levels, rows, cols)],
        scratch_shapes=[
            pltpu.VMEM((2, 3, tall, cols), F32),
            pltpu.VMEM((2, 5, tall, cols), F32),
            pltpu.VMEM((2, wide, cols), F32),
            pltpu.VMEM((2, levels, rows, cols), F32),
            pltpu.SemaphoreType.DMA((1 + 2 * levels,)),
        ],
        compiler_params=PARAMS,
        name="surface_steps",
    )(ext, base, statics, sums, others)
    return (height, east_next, north_next)


def solution(mesh):
    return jax.shard_map(
        on_device,
        mesh=mesh,
        in_specs=(
            P("gz", "gy", "gx"),
            P("gz", "gy", "gx"),
            P("gz", "gy", "gx"),
            P("gy", "gx"),
            P("gy", "gx"),
            P("gy", "gx"),
            P("gy", "gx"),
            P("gz"),
        ),
        out_specs=(P("gy", "gx"), P("gz", "gy", "gx"), P("gz", "gy", "gx")),
        check_vma=False,
    )
```

time: 104 us -> 35.5 us (0.34)
  waiting for transfers between devices: 50.2 us -> 13.2 us
  other arithmetic: 17.9 us -> 0 us
  between operations: 14.4 us -> 0.67 us
  Pallas kernels: 0 us -> 13.6 us
  starting transfers between devices: 14.7 us -> 7.92 us
  local copies, waits for them, and re-layouts: 6.62 us -> 0.01 us
    psum x1 -> x0, waiting for transfers between devices: 19.8 us -> none  [on_device(): totals = lax.psum(partial_sums, 'gz')]
    ppermute x8 -> x5, waiting for transfers between devices: 30.4 us -> 13.2 us  [the longest x1 4.22 us: on_device(): south = lax.ppermute(north_out, 'gy', forward)]
    pallas_call x0 -> x4, Pallas kernels: none -> 13.6 us  [the longest x1 7.83 us: on_device(): pl.pallas_call(functools.partial(layer_kernel, size), in_specs=[SMEM] + [...]
    reduce_sum x1 -> x0, other arithmetic: 7.85 us -> none  [on_device(): jnp.sum(thick * active, axis=0)]
    ppermute x8 -> x5, starting transfers between devices: 14.7 us -> 7.92 us  [the longest x1 3.97 us: on_device(): east = lax.ppermute(low, 'gx', backward)]
    mul x8 -> x0, other arithmetic: 4.85 us -> none  [the longest x1 2.49 us: on_device(): active * (masked_north + timestep * tend_north + (trans_north - sum_north...]
    unnamed x37 -> x2, local copies, waits for them, and re-layouts: 3.52 us -> 0.01 us
    slice x4 -> x0, local copies, waits for them, and re-layouts: 2.01 us -> none  [the longest x3 1.39 us: extended(): lax.slice_in_dim(block, block.shape[dim] - width, None, axis=dim)]
  transfers between devices with their start and end apart: 9 -> 5, of which waited for: 7 -> 5; matrix products, arithmetic and copies ran while one was open for 1% -> 0% of each run, Pallas kernels for 0% -> 0%
where the time goes in v1:
time: 35.5 us; the launch traced here: 35.4 us
  Pallas kernels  13.6 us (38%)
  waiting for transfers between devices  13.2 us (37%)
  starting transfers between devices  7.92 us (22%)
  between operations  0.67 us (2%)
    pallas_call x1, Pallas kernels, on_device(): pl.pallas_call(functools.partial(layer_kernel, size), in_specs=[SMEM] + [...  7.83 us
    ppermute x1, waiting for transfers between devices, on_device(): south = lax.ppermute(north_out, 'gy', forward)  4.22 us
    ppermute x1, starting transfers between devices, on_device(): east = lax.ppermute(low, 'gx', backward)  3.97 us
    ppermute x1, waiting for transfers between devices, on_device(): east = lax.ppermute(low, 'gx', backward)  3.88 us
    pallas_call x1, Pallas kernels, on_device(): pl.pallas_call(functools.partial(pack_columns, size), in_specs=[HBM] * 7,...  2.96 us
    pallas_call x1, Pallas kernels, on_device(): pl.pallas_call(functools.partial(surface_kernel, size), in_specs=[VMEM] *...  2.76 us
    ppermute x1, waiting for transfers between devices, on_device(): west = lax.ppermute(high, 'gx', forward)  2.67 us
    ppermute x1, starting transfers between devices, on_device(): north = lax.ppermute(south_out, 'gy', backward)  2.25 us
  transfers between devices with their start and end apart: 5, of which 5 were waited for; matrix products, arithmetic and copies ran while one was open for 0% of the time, Pallas kernels for 0%

profile of v1, /device:TPU:0, one launch (start us, length us, event | category | flops | bytes accessed | tf_op | source)
XLA Modules:
  0.0 35.4 jit_solution(2555718174873876618)
XLA Ops:
  0.6 0.0 copy-start
  0.6 3.0 %pack_columns.1 = (f32[27,160,128]{2,1,0:T(8,128)S(1)}, f32[2,128,128]{2,1,0:T(8,128)S(1)}, f32[2,128,128]{2,1,0:T(8,128)S(1)}) custom-call(f32[8,128,128]{2,1,0:T(8,128)} %east.1, f32[8,128,128]{2,1,0:T(8,128)} %north.1, f32[8,128,128]{2,1,0:T(8,128)} %press.1, f32[128,128]{1,0:T(8,128)} %surface.1, s32[128,128]{1,0:T(8,128)} %land.1, s32[128,128]{1,0:T(8,128)} %bottom.1, ...), custom_call_target="tpu_custom_call" | custom-call | tf_op jit(solution)/shard_map/pack_columns/pallas_call | solution.py:424
  3.6 4.0 %collective-permute-start.1 = (f32[2,128,128]{2,1,0:T(8,128)S(1)}, f32[2,128,128]{2,1,0:T(8,128)S(1)}, u32[]{:S(2)}, u32[]{:S(2)}) collective-permute-start(f32[2,128,128]{2,1,0:T(8,128)S(1)} %get-tuple-element.13.low), channel_id=1, source_target_pairs={{8,0},{16,8},{24,16},{0,24},{9,1},{17,9},{25,17},{1,25},{10,2},{18... | collective-permute-start | bytes 393224 | tf_op jit(solution)/shard_map/ppermute | solution.py:446
  7.6 0.0 collective-permute-start
  7.6 3.9 %collective-permute-done.1.east = f32[2,128,128]{2,1,0:T(8,128)S(1)} collective-permute-done((f32[2,128,128]{2,1,0:T(8,128)S(1)}, f32[2,128,128]{2,1,0:T(8,128)S(1)}, u32[]{:S(2)}, u32[]{:S(2)}) %collective-permute-start.1) | collective-permute-done | bytes 131104 | tf_op jit(solution)/shard_map/ppermute | solution.py:446
  11.5 2.7 %collective-permute-done.west = f32[2,128,128]{2,1,0:T(8,128)S(1)} collective-permute-done((f32[2,128,128]{2,1,0:T(8,128)S(1)}, f32[2,128,128]{2,1,0:T(8,128)S(1)}, u32[]{:S(2)}, u32[]{:S(2)}) %collective-permute-start) | collective-permute-done | bytes 131104 | tf_op jit(solution)/shard_map/ppermute | solution.py:445
  14.2 1.6 %collective-permute-start.2 = (f32[31,8,128]{2,1,0:T(8,128)S(1)}, f32[31,8,128]{2,1,0:T(8,128)S(1)}, u32[]{:S(2)}, u32[]{:S(2)}) collective-permute-start(f32[31,8,128]{2,1,0:T(8,128)S(1)} %get-tuple-element.15), channel_id=1, source_target_pairs={{0,2},{2,4},{4,6},{6,0},{1,3},{3,5},{5,7},{7,1},{8,10},{10,12},{12... | collective-permute-start | bytes 380936 | tf_op jit(solution)/shard_map/ppermute | solution.py:456
  15.8 2.2 %collective-permute-start.3 = (f32[31,8,128]{2,1,0:T(8,128)S(1)}, f32[31,8,128]{2,1,0:T(8,128)S(1)}, u32[]{:S(2)}, u32[]{:S(2)}) collective-permute-start(f32[31,8,128]{2,1,0:T(8,128)S(1)} %get-tuple-element.16), channel_id=1, source_target_pairs={{2,0},{4,2},{6,4},{0,6},{3,1},{5,3},{7,5},{1,7},{10,8},{12,10},{14... | collective-permute-start | bytes 380936 | tf_op jit(solution)/shard_map/ppermute | solution.py:457
  18.0 4.2 %collective-permute-done.2.south = f32[31,8,128]{2,1,0:T(8,128)S(1)} collective-permute-done((f32[31,8,128]{2,1,0:T(8,128)S(1)}, f32[31,8,128]{2,1,0:T(8,128)S(1)}, u32[]{:S(2)}, u32[]{:S(2)}) %collective-permute-start.2) | collective-permute-done | bytes 127008 | tf_op jit(solution)/shard_map/ppermute | solution.py:456
  22.3 0.7 %collective-permute-done.3.north = f32[31,8,128]{2,1,0:T(8,128)S(1)} collective-permute-done((f32[31,8,128]{2,1,0:T(8,128)S(1)}, f32[31,8,128]{2,1,0:T(8,128)S(1)}, u32[]{:S(2)}, u32[]{:S(2)}) %collective-permute-start.3) | collective-permute-done | bytes 127008 | tf_op jit(solution)/shard_map/ppermute | solution.py:457
  22.9 0.0 copy-done
  22.9 7.8 %layer_terms.1 = (f32[27,160,128]{2,1,0:T(8,128)S(1)}, f32[2,8,144,128]{3,2,1,0:T(8,128)S(1)}, f32[6,144,128]{2,1,0:T(8,128)S(1)}, f32[3,144,128]{2,1,0:T(8,128)S(1)}) custom-call(f32[8]{0:T(128)S(1)} %copy-done, f32[27,160,128]{2,1,0:T(8,128)S(1)} %get-tuple-element.12.ext.ext_in, ...), custom_call_target="tpu_custom_call", output_to_operand_aliasing={{0}: (1, {})} | custom-call | tf_op jit(solution)/shard_map/layer_terms/pallas_call | solution.py:458
  30.8 0.1 collective-permute-start.4
  30.9 1.8 %collective-permute-done.4.other = f32[6,144,128]{2,1,0:T(8,128)S(1)} collective-permute-done((f32[6,144,128]{2,1,0:T(8,128)S(1)}, f32[6,144,128]{2,1,0:T(8,128)S(1)}, u32[]{:S(2)}, u32[]{:S(2)}) %collective-permute-start.4) | collective-permute-done | bytes 442400 | tf_op jit(solution)/shard_map/ppermute | solution.py:475
  32.6 2.8 %surface_steps.1 = (f32[128,128]{1,0:T(8,128)}, f32[8,128,128]{2,1,0:T(8,128)}, f32[8,128,128]{2,1,0:T(8,128)}) custom-call(f32[27,160,128]{2,1,0:T(8,128)S(1)} %get-tuple-element.17.ext, f32[2,8,144,128]{3,2,1,0:T(8,128)S(1)} %get-tuple-element.18.base, f32[3,144,128]{2,1,0:T(8,128)S(1)} %get-tuple-element.19.statics, ...), custom_call_target="tpu_custom_call" | custom-call | tf_op jit(solution)/shard_map/surface_steps/pallas_call | solution.py:476
  (1 shorter events, 0.0 us)
Async XLA Ops:
  0.6 22.3 %copy-start = (f32[8]{0:T(128)S(1)}, f32[8]{0:T(128)}, u32[]{:S(2)}) copy-start(f32[8]{0:T(128)} %thick.1) | copy-start | bytes 100
  3.6 7.9 %collective-permute-start.1 = (f32[2,128,128]{2,1,0:T(8,128)S(1)}, f32[2,128,128]{2,1,0:T(8,128)S(1)}, u32[]{:S(2)}, u32[]{:S(2)}) collective-permute-start(f32[2,128,128]{2,1,0:T(8,128)S(1)} %get-tuple-element.13.low), channel_id=1, source_target_pairs={{8,0},{16,8},{24,16},{0,24},{9,1},{17,9},{25,17},{1,25},{10,2},{18... | collective-permute-start | bytes 393224 | tf_op jit(solution)/shard_map/ppermute | solution.py:446
  7.6 6.6 %collective-permute-start = (f32[2,128,128]{2,1,0:T(8,128)S(1)}, f32[2,128,128]{2,1,0:T(8,128)S(1)}, u32[]{:S(2)}, u32[]{:S(2)}) collective-permute-start(f32[2,128,128]{2,1,0:T(8,128)S(1)} %get-tuple-element.14.high), channel_id=1, source_target_pairs={{0,8},{8,16},{16,24},{24,0},{1,9},{9,17},{17,25},{25,1},{2,10},{10... | collective-permute-start | bytes 393224 | tf_op jit(solution)/shard_map/ppermute | solution.py:445
  14.2 8.1 %collective-permute-start.2 = (f32[31,8,128]{2,1,0:T(8,128)S(1)}, f32[31,8,128]{2,1,0:T(8,128)S(1)}, u32[]{:S(2)}, u32[]{:S(2)}) collective-permute-start(f32[31,8,128]{2,1,0:T(8,128)S(1)} %get-tuple-element.15), channel_id=1, source_target_pairs={{0,2},{2,4},{4,6},{6,0},{1,3},{3,5},{5,7},{7,1},{8,10},{10,12},{12... | collective-permute-start | bytes 380936 | tf_op jit(solution)/shard_map/ppermute | solution.py:456
  15.8 7.2 %collective-permute-start.3 = (f32[31,8,128]{2,1,0:T(8,128)S(1)}, f32[31,8,128]{2,1,0:T(8,128)S(1)}, u32[]{:S(2)}, u32[]{:S(2)}) collective-permute-start(f32[31,8,128]{2,1,0:T(8,128)S(1)} %get-tuple-element.16), channel_id=1, source_target_pairs={{2,0},{4,2},{6,4},{0,6},{3,1},{5,3},{7,5},{1,7},{10,8},{12,10},{14... | collective-permute-start | bytes 380936 | tf_op jit(solution)/shard_map/ppermute | solution.py:457
  30.8 1.9 %collective-permute-start.4 = (f32[6,144,128]{2,1,0:T(8,128)S(1)}, f32[6,144,128]{2,1,0:T(8,128)S(1)}, u32[]{:S(2)}, u32[]{:S(2)}) collective-permute-start(f32[6,144,128]{2,1,0:T(8,128)S(1)} %get-tuple-element.20.mine), channel_id=1, source_target_pairs={{0,1},{1,0},{2,3},{3,2},{4,5},{5,4},{6,7},{7,6},{8,9},{9,8},{10,11... | collective-permute-start | bytes 1327112 | tf_op jit(solution)/shard_map/ppermute | solution.py:475

commit v2 on v1

v2 whole, which is shorter than its diff:
```python
import functools

import jax
import jax.numpy as jnp
from jax import lax
from jax.experimental import pallas as pl
from jax.experimental.pallas import tpu as pltpu
from jax.sharding import PartitionSpec as P


SUBSTEPS = 4
COURANT = 0.25
VISCOSITY = 0.1
REACH = 2 * SUBSTEPS
TIMESTEP = SUBSTEPS * COURANT
CHUNK = 2 * REACH
SIDE_PARTS = 1

F32 = jnp.float32


class Sizes:
    def __init__(self, levels, rows, cols):
        self.levels = levels
        self.rows = rows
        self.cols = cols
        self.wide = rows + 2 * REACH
        self.slots = cols // REACH
        self.half = cols // 2
        self.planes = 3 * levels + 3
        assert 2 * levels * REACH == cols
        assert rows % CHUNK == 0


def turned(value, shift):
    shift = shift % value.shape[-1]
    if shift == 0:
        return value
    return pltpu.roll(value, shift, axis=1)


def repeated(count):
    def run(body):
        for step in range(count):
            body(step)

    return run


def lane_ids(rows, cols):
    return lax.broadcasted_iota(jnp.int32, (rows, cols), 1)


def gathered(value, source):
    return jnp.take_along_axis(value, source, axis=1, mode="promise_in_bounds")


def pairing(axis):
    count = lax.axis_size(axis)
    steps = [(i, (i + 1) % count) for i in range(count)]
    if count % 2:
        return steps, [(target, source) for source, target in steps]
    swaps = [[], []]
    for source, target in steps:
        swaps[source % 2] += [(source, target), (target, source)]
    return swaps


def roles(axis):
    if lax.axis_size(axis) % 2:
        return True, False
    even = lax.axis_index(axis) % 2 == 0
    return even, even


def either(flag, first, second):
    if flag is True:
        return first
    if flag is False:
        return second
    return jnp.where(flag, first, second)


def pack_edges(size, load, rows):
    lane = lane_ids(rows, size.cols)
    slot_of = lane // REACH
    results = []
    for first, count in ((0, 2 * size.levels), (2 * size.levels, size.levels + 3)):
        low = jnp.zeros((rows, size.cols), F32)
        high = jnp.zeros((rows, size.cols), F32)
        for slot in range(count):
            value = turned(load(first + slot), slot * REACH)
            low = jnp.where(slot_of == slot, value, low)
            high = jnp.where(slot_of == (slot - 1) % size.slots, value, high)
        results.append((low, turned(high, REACH)))
    return results


def pack_kernel(
    size, east, north, press, surface, land, bottom, coriolis,
    tile, x_first, x_second, y_first, y_second, whole, sems,
):
    levels, rows = size.levels, size.rows
    copies = []
    for slot, field in enumerate((east, north, press)):
        target = tile.at[pl.ds(slot * levels, levels)]
        copies.append(pltpu.make_async_copy(field, target, sems.at[slot]))
    copies.append(pltpu.make_async_copy(surface, tile.at[3 * levels], sems.at[3]))
    copies.append(pltpu.make_async_copy(coriolis, tile.at[3 * levels + 2], sems.at[4]))
    copies.append(pltpu.make_async_copy(land, whole.at[0], sems.at[5]))
    copies.append(pltpu.make_async_copy(bottom, whole.at[1], sems.at[6]))
    for copy in copies:
        copy.start()
    for copy in copies[3:]:
        copy.wait()
    tile[3 * levels + 1] = whole[0].astype(F32) * whole[1].astype(F32)
    for copy in copies[:3]:
        copy.wait()
    x_flag, _ = roles("gx")
    y_flag, _ = roles("gy")

    def pack(first, second):
        @repeated(rows // CHUNK)
        def _(step):
            here = pl.ds(step * CHUNK, CHUNK)
            packed = pack_edges(size, lambda plane: tile[plane, here, :], CHUNK)
            for index, (low, high) in enumerate(packed):
                first[index, here, :] = either(x_flag, high, low)
                second[index, here, :] = either(x_flag, low, high)

    pack(x_first, x_second)
    low, high = tile[:, :REACH, :], tile[:, rows - REACH :, :]
    y_first[...] = either(y_flag, high, low)
    y_second[...] = either(y_flag, low, high)


def corner_kernel(size, y_first, y_second, base, first, second):
    del base
    x_flag, _ = roles("gx")
    _, north_first = roles("gy")

    def rows_of(plane):
        a, b = y_first[plane], y_second[plane]
        south, north = either(north_first, b, a), either(north_first, a, b)
        return jnp.concatenate([south, north])

    for index, (low, high) in enumerate(pack_edges(size, rows_of, 2 * REACH)):
        first[index] = either(x_flag, high, low)
        second[index] = either(x_flag, low, high)


class Strips:
    def __init__(self, size, thick, rows):
        self.size = size
        self.first_level = (lax.axis_index("gz") * size.levels).astype(F32)
        lane = lane_ids(rows, size.cols)
        self.lane = lane
        self.slot_of, self.inner = lane // REACH, lane % REACH
        self.level_of = (self.slot_of % size.levels).astype(F32) + self.first_level
        self.eastward = lane < size.half
        weight = jnp.zeros((rows, size.cols), F32)
        for k in range(size.levels):
            weight = jnp.where(self.slot_of % size.levels == k, thick[k], weight)
        self.weight = weight

    def slot(self, index):
        return index * REACH + self.inner

    def prepare(self, raw):
        size = self.size
        lane = lane_ids(*raw.shape)
        slot = (size.levels + 1) * REACH + lane % REACH
        return gathered(raw, lane % size.half), gathered(raw, slot)

    def chunk(self, value, raw, own_value, own_raw, around):
        size = self.size
        half, levels = size.half, size.levels
        merged, wet_sides, faces = [], [], []
        for side in range(2):
            edge, toward = ((REACH - 1, -1), (0, 1))[side]

            def beside(array, mine):
                mine = turned(mine, edge if side == 0 else -(REACH - 1))
                return jnp.where(self.inner == edge, mine, turned(array, toward))

            x_value = beside(value[side], own_value[side])
            x_raw = beside(raw[side], own_raw[side])
            x_prs = gathered(x_raw, self.lane % half)
            x_cnt = gathered(jnp.minimum(raw[side], x_raw), self.slot(levels + 1))
            cor = gathered(raw[side], self.slot(levels + 2))
            (val, prs, cnt), over, under = around(side)
            x_wet = self.level_of < x_cnt
            change = VISCOSITY * (x_value - val)
            push = jnp.where(self.eastward, 0.5 * (x_prs - prs), 0.0)
            if side == 1:
                change, push = -change, -push
            ahead = jnp.where(x_wet, change - push, 0.0)
            behind = jnp.where(x_wet, change + push, 0.0)
            if side == 0:
                faces.append(-behind)
                tend = ahead - turned(behind, 1)
            else:
                faces.append(ahead)
                tend = turned(ahead, -1) - behind
            wet = self.level_of < cnt
            n_wet = self.level_of < jnp.minimum(cnt, over[2])
            s_wet = self.level_of < jnp.minimum(cnt, under[2])
            n_val = jnp.where(n_wet, over[0] - val, 0.0)
            s_val = jnp.where(s_wet, under[0] - val, 0.0)
            n_prs = jnp.where(n_wet, over[1] - prs, 0.0)
            s_prs = jnp.where(s_wet, prs - under[1], 0.0)
            turn = cor * turned(val, half)
            turn = jnp.where(wet, jnp.where(self.eastward, turn, -turn), 0.0)
            tend = tend + VISCOSITY * (n_val + s_val) + turn
            tend = tend - jnp.where(self.eastward, 0.0, 0.5 * (n_prs + s_prs))
            force = self.weight * tend
            total = self.weight * jnp.where(wet, val, 0.0)
            quarter = half // 2
            force = force + turned(force, quarter)
            total = total + turned(total, -quarter)
            both = jnp.where(self.lane % half >= quarter, force, total)
            merged.append(self.summed(both, quarter // 2))
            wet_sides.append(jnp.where(wet, self.weight, 0.0))
        deep = self.summed(jnp.where(self.eastward, *wet_sides), half // 2)
        quarter_slots = size.slots // 4
        which = self.slot_of % quarter_slots
        plane = jnp.where(
            which == quarter_slots - 1,
            merged[0],
            jnp.where(
                which == quarter_slots - 2,
                turned(merged[1], -REACH),
                turned(deep, -2 * REACH),
            ),
        )
        sides = jnp.where(self.inner == REACH - 1, faces[0], turned(faces[1], REACH - 2))
        return plane, sides

    def summed(self, value, shift):
        while shift >= REACH:
            value = value + turned(value, shift)
            shift //= 2
        return value

    def at_sides(self, sides, slot):
        rolled = turned(sides, -(slot * REACH + REACH - 1))
        ends = (self.lane == 0) | (self.lane == self.size.cols - 1)
        return jnp.where(ends, rolled, 0.0)

    def side_forces(self, sides):
        levels = self.size.levels
        total = self.summed(self.weight * sides, self.size.half // 2)
        return self.at_sides(total, levels - 1), self.at_sides(total, 2 * levels - 1)

    def statics(self, raw):
        size, results = self.size, []
        for index in range(3):
            slot = size.levels + index
            lane = lane_ids(*raw[0].shape)
            left = turned(raw[0], (size.slots - 1 - slot) * REACH)
            right = turned(raw[1], -slot * REACH)
            results.append(
                jnp.where(
                    lane >= size.cols - REACH, left, jnp.where(lane < REACH, right, 0.0)
                )
            )
        return results


def core_chunk(size, thick, first_level, here, over, under, gains, write):
    levels, cols = size.levels, size.cols
    count = 3 * levels + 1
    cnt, cor = here(count), here(count + 1)
    lane = lane_ids(*cnt.shape)
    cnt_e = jnp.where(lane == cols - 1, -1.0, jnp.minimum(cnt, turned(cnt, -1)))
    cnt_w = jnp.where(lane == 0, -1.0, jnp.minimum(cnt, turned(cnt, 1)))
    cnt_n, cnt_s = jnp.minimum(cnt, over(count)), jnp.minimum(cnt, under(count))
    totals = [jnp.zeros(cnt.shape, F32)] * 5
    for k in range(levels):
        level = first_level + k
        wet, wet_e, wet_w, wet_n, wet_s = (
            level < c for c in (cnt, cnt_e, cnt_w, cnt_n, cnt_s)
        )
        u, v, p = here(k), here(levels + k), here(2 * levels + k)
        slow_u, slow_v, push = VISCOSITY * u, VISCOSITY * v, 0.5 * p
        u_less, u_more = slow_u - push, slow_u + push
        gain_e = jnp.where(wet_e, turned(u_less, -1) - u_less, 0.0)
        gain_e = gain_e + jnp.where(wet_w, turned(u_more, 1) - u_more, 0.0)
        gain_n = jnp.where(wet_e, turned(slow_v, -1) - slow_v, 0.0)
        gain_n = gain_n + jnp.where(wet_w, turned(slow_v, 1) - slow_v, 0.0)
        n_u, s_u = over(k) - u, under(k) - u
        n_v, s_v = over(levels + k) - v, under(levels + k) - v
        n_p, s_p = over(2 * levels + k) - p, p - under(2 * levels + k)
        gain_e = gain_e + VISCOSITY * (jnp.where(wet_n, n_u, 0.0) + jnp.where(wet_s, s_u, 0.0))
        gain_n = gain_n + jnp.where(wet_n, VISCOSITY * n_v - 0.5 * n_p, 0.0)
        gain_n = gain_n + jnp.where(wet_s, VISCOSITY * s_v - 0.5 * s_p, 0.0)
        if gains is not None:
            gain_e, gain_n = gain_e + gains(k), gain_n + gains(levels + k)
        wet_u, wet_v = jnp.where(wet, u, 0.0), jnp.where(wet, v, 0.0)
        tend_e, tend_n = gain_e + cor * wet_v, gain_n - cor * wet_u
        write(0, k, wet_u + TIMESTEP * tend_e)
        write(1, k, wet_v + TIMESTEP * tend_n)
        weight = thick[k]
        parts = (weight * tend_e, weight * tend_n, weight * wet_u, weight * wet_v)
        parts += (jnp.where(wet, weight, 0.0),)
        totals = [total + part for total, part in zip(totals, parts)]
    return totals


def middle_kernel(size, thick, tile, base, sums):
    rows = size.rows
    first_level = (lax.axis_index("gz") * size.levels).astype(F32)

    @repeated((rows - CHUNK) // CHUNK)
    def _(step):
        start = REACH + step * CHUNK

        def load(move):
            return lambda plane: tile[plane, pl.ds(start + move, CHUNK), :]

        def write(field, k, value):
            base[field, k, pl.ds(start, CHUNK), :] = value

        totals = core_chunk(size, thick, first_level, load(0), load(1), load(-1), None, write)
        for index, total in enumerate(totals):
            sums[index, pl.ds(REACH + start, CHUNK), :] = total


def side_kernel(
    size, thick, tile, own_first, own_second, got_first, got_second, sums_in,
    sums, statics, sides_out, work,
):
    rows = size.rows
    high_first, _ = roles("gx")
    _, east_first = roles("gx")
    count = (rows - CHUNK) // SIDE_PARTS
    strips = Strips(size, thick, count)

    def got(index, at):
        a, b = got_first[index, at, :], got_second[index, at, :]
        return either(east_first, b, a), either(east_first, a, b)

    def own(index, at):
        a, b = own_first[index, at, :], own_second[index, at, :]
        return either(high_first, b, a), either(high_first, a, b)

    everything = slice(0, rows)
    value, raw = got(0, everything), got(1, everything)
    place = slice(REACH, REACH + rows)
    for side in range(2):
        work[side, 0] = value[side]
        work[side, 1], work[side, 2] = strips.prepare(raw[side])
    for index, plane in enumerate(strips.statics(raw)):
        statics[index, place, :] = plane
        statics[3 + index, place, :] = tile[3 * size.levels + index]

    for start in range(REACH, rows - REACH, count):
        at, place = slice(start, start + count), slice(start + REACH, start + REACH + count)

        def around(side):
            return [
                [work[side, plane, start + move : start + move + count, :] for plane in range(3)]
                for move in (0, 1, -1)
            ]

        plane, sides = strips.chunk(got(0, at), got(1, at), own(0, at), own(1, at), around)
        sums[5, place, :] = plane
        sides_out[at, :] = sides
        for index, gain in enumerate(strips.side_forces(sides)):
            sums[index, place, :] = sums_in[index, place, :] + gain
        for index in range(2, 5):
            sums[index, place, :] = sums_in[index, place, :]


def outer_kernel(
    size, thick, tile, own_first, own_second, got_first, got_second,
    y_first, y_second, c_first, c_second, c_got_first, c_got_second,
    base_in, sums_in, statics_in,
    base, sums, statics, rows_of, strip_of, own_of,
):
    del base_in, sums_in, statics_in
    rows, planes = size.rows, size.planes
    high_first, east_first = roles("gx")
    _, north_first = roles("gy")
    strips = Strips(size, thick, 2 * CHUNK)
    window = 4 * REACH
    near = (slice(0, CHUNK), slice(rows - CHUNK, rows))
    mine = (slice(CHUNK, window), slice(window, window + CHUNK))
    halo = (slice(REACH, CHUNK), slice(window + CHUNK, window + CHUNK + REACH))

    def outer(plane):
        a, b = y_first[plane], y_second[plane]
        return either(north_first, b, a), either(north_first, a, b)

    def corner(first, second, flag, index):
        a, b = first[index], second[index]
        pair = either(flag, b, a), either(flag, a, b)
        return [(value[:REACH], value[REACH:]) for value in pair]

    def pair_of(first, second, flag, index, at):
        a, b = first[index, at, :], second[index, at, :]
        return either(flag, b, a), either(flag, a, b)

    def joined(ref, lead, move=0):
        return jnp.concatenate(
            [
                ref[(*lead, slice(at + move, at + move + CHUNK), slice(None))]
                for at in (REACH, window + REACH)
            ]
        )

    for plane in range(planes):
        halos = outer(plane)
        for part in range(2):
            rows_of[plane, mine[part], :] = tile[plane, near[part], :]
            rows_of[plane, halo[part], :] = halos[part]
    for index in range(2):
        halos = corner(c_got_first, c_got_second, east_first, index)
        own_halos = corner(c_first, c_second, high_first, index)
        for part in range(2):
            got = pair_of(got_first, got_second, east_first, index, near[part])
            own = pair_of(own_first, own_second, high_first, index, near[part])
            for side in range(2):
                strip_of[side, index, mine[part], :] = got[side]
                strip_of[side, index, halo[part], :] = halos[side][part]
                own_of[side, index, mine[part], :] = own[side]
                own_of[side, index, halo[part], :] = own_halos[side][part]
    for side in range(2):
        strip_of[side, 2], strip_of[side, 3] = strips.prepare(strip_of[side, 1])

    def around(side):
        return [
            [joined(strip_of, (side, plane), move) for plane in (0, 2, 3)] for move in (0, 1, -1)
        ]

    value, raw, own_value, own_raw = (
        [joined(ref, (side, index)) for side in range(2)]
        for ref, index in ((strip_of, 0), (strip_of, 1), (own_of, 0), (own_of, 1))
    )
    places = (slice(0, CHUNK), slice(rows, rows + CHUNK))
    tiles = (slice(0, REACH), slice(rows - REACH, rows))
    kept = (slice(REACH, CHUNK), slice(CHUNK, CHUNK + REACH))

    def store(ref, index, value):
        ref[index, places[0], :] = value[:CHUNK]
        ref[index, places[1], :] = value[CHUNK:]

    plane, sides = strips.chunk(value, raw, own_value, own_raw, around)
    store(sums, 5, plane)
    for index, plane in enumerate(strips.statics(raw)):
        store(statics, index, plane)

    def load(move):
        return lambda plane: joined(rows_of, (plane,), move)

    def write(field, k, value):
        for part in range(2):
            base[field, k, tiles[part], :] = value[kept[part]]

    totals = core_chunk(
        size, thick, strips.first_level, load(0), load(1), load(-1),
        lambda slot: strips.at_sides(sides, slot), write,
    )
    for index, total in enumerate(totals):
        store(sums, index, total)
    for index in range(3):
        store(statics, 3 + index, load(0)(3 * size.levels + index))


def finish_kernel(size, thick, sides_in, base_in, base):
    levels, rows = size.levels, size.rows
    strips = Strips(size, thick, CHUNK)

    @repeated((rows - CHUNK) // CHUNK)
    def _(step):
        at = pl.ds(REACH + step * CHUNK, CHUNK)
        sides = sides_in[at, :]
        for field in range(2):
            for k in range(levels):
                gain = strips.at_sides(sides, field * levels + k)
                base[field, k, at, :] = base_in[field, k, at, :] + TIMESTEP * gain


def surface_kernel(
    size, tile, base, statics, mine, other,
    height_out, east_out, north_out,
    state, fixed, drive, result, sems,
):
    levels, rows, cols, wide = size.levels, size.rows, size.cols, size.wide
    top = 2 * REACH
    first_level = (lax.axis_index("gz") * levels).astype(F32)
    lane = lane_ids(CHUNK, cols)
    H, TE, TN = range(3)
    OC, DP, CO, FE, FN = range(5)
    chunks = [REACH + at for at in range(0, wide, CHUNK)]

    @repeated(wide // CHUNK)
    def _(step):
        place = pl.ds(step * CHUNK, CHUNK)
        here = pl.ds(REACH + step * CHUNK, CHUNK)
        total = [mine[index, place, :] + other[index, place, :] for index in range(6)]
        strip = total[5]
        last = size.slots - 1
        quarter = size.slots // 4

        def outer(left, right):
            return jnp.where(
                lane >= cols - REACH,
                turned(strip, (last - left) * REACH),
                jnp.where(lane < REACH, turned(strip, -right * REACH), 0.0),
            )

        fixed[0, FE, here, :] = total[0]
        fixed[0, FN, here, :] = total[1]
        state[0, TE, here, :] = total[2]
        state[0, TN, here, :] = total[3]
        drive[0, place, :] = total[2] + TIMESTEP * total[0]
        drive[1, place, :] = total[3] + TIMESTEP * total[1]
        fixed[0, DP, here, :] = total[4]
        fixed[1, FE, here, :] = outer(2 * quarter - 1, 2 * quarter - 2)
        fixed[1, FN, here, :] = outer(4 * quarter - 1, 4 * quarter - 2)
        state[1, TE, here, :] = outer(quarter - 1, quarter - 2)
        state[1, TN, here, :] = outer(3 * quarter - 1, 3 * quarter - 2)
        fixed[1, DP, here, :] = outer(2 * quarter - 3, 4 * quarter - 3)
        state[0, H, here, :] = statics[3, place, :]
        state[1, H, here, :] = statics[0, place, :]
        fixed[0, OC, here, :] = jnp.where(statics[4, place, :] > 0, 1.0, 0.0)
        fixed[1, OC, here, :] = jnp.where(statics[1, place, :] > 0, 1.0, 0.0)
        fixed[0, CO, here, :] = statics[5, place, :]
        fixed[1, CO, here, :] = statics[2, place, :]

    def difference_x(field, here):
        inside, outside = state[0, field, here, :], state[1, field, here, :]
        in_e, out_e = turned(inside, -1), turned(outside, -1)
        in_w, out_w = turned(inside, 1), turned(outside, 1)
        at_high, at_low = lane == cols - 1, lane == 0
        return (
            0.5 * (jnp.where(at_high, out_e, in_e) - jnp.where(at_low, out_w, in_w)),
            0.5 * (jnp.where(at_high, in_e, out_e) - jnp.where(at_low, in_w, out_w)),
        )

    def difference_y(part, field, start):
        above = state[part, field, start + 1 : start + 1 + CHUNK, :]
        return 0.5 * (above - state[part, field, start - 1 : start - 1 + CHUNK, :])

    for _ in range(SUBSTEPS):
        for start in chunks:
            here = slice(start, start + CHUNK)
            across = difference_x(TE, here)
            for part in range(2):
                spread = across[part] + difference_y(part, TN, start)
                height = state[part, H, here, :] - COURANT * spread
                state[part, H, here, :] = fixed[part, OC, here, :] * height
        for start in chunks:
            here = slice(start, start + CHUNK)
            across = difference_x(H, here)
            for part in range(2):
                slope_y = difference_y(part, H, start)
                te, tn = state[part, TE, here, :], state[part, TN, here, :]
                oc, dp, co, fe, fn = (fixed[part, index, here, :] for index in range(5))
                state[part, TE, here, :] = oc * (
                    te + COURANT * (-dp * across[part] + co * tn + fe)
                )
                state[part, TN, here, :] = oc * (tn + COURANT * (-dp * slope_y - co * te + fn))

    height_copy = pltpu.make_async_copy(
        state.at[0, H, pl.ds(top, rows), :], height_out, sems.at[0]
    )
    height_copy.start()
    inner = slice(top, top + rows)
    floor_depth = fixed[0, DP, inner, :] + (1.0 - fixed[0, OC, inner, :])
    for index, field in enumerate((TE, TN)):
        gain = state[0, field, inner, :] - drive[index, REACH : REACH + rows, :]
        drive[index, REACH : REACH + rows, :] = gain / floor_depth
    copies = [height_copy]
    for k in range(levels):
        wet = first_level + k < tile[3 * levels + 1]
        for index, out in enumerate((east_out, north_out)):
            change = jnp.where(wet, drive[index, REACH : REACH + rows, :], 0.0)
            result[index, k] = base[index, k] + change
            copy = pltpu.make_async_copy(
                result.at[index, k], out.at[k], sems.at[1 + 2 * k + index]
            )
            copy.start()
            copies.append(copy)
    for copy in copies:
        copy.wait()


VMEM = pl.BlockSpec(memory_space=pltpu.VMEM)
SMEM = pl.BlockSpec(memory_space=pltpu.SMEM)
HBM = pl.BlockSpec(memory_space=pltpu.HBM)


def shaped(*shape):
    return jax.ShapeDtypeStruct(shape, F32)


def call(body, size, ins, outs, shapes, scratch=(), aliases=None, flops=0):
    return pl.pallas_call(
        functools.partial(body, size),
        in_specs=ins,
        out_specs=outs,
        out_shape=shapes,
        scratch_shapes=scratch,
        input_output_aliases=aliases or {},
        compiler_params=pltpu.CompilerParams(vmem_limit_bytes=24 * 1024 * 1024),
        cost_estimate=pl.CostEstimate(flops=flops, bytes_accessed=0, transcendentals=0),
    )


def swapped(axis, first, second):
    pairs = pairing(axis)
    first = lax.ppermute(first, axis, pairs[0])
    second = lax.ppermute(second, axis, pairs[1])
    return first, second


def on_device(
    layer_east, layer_north, layer_press, surface, land_sea, bottom_level, coriolis, level_thick
):
    size = Sizes(*layer_east.shape)
    levels, rows, cols = layer_east.shape
    wide, planes = size.wide, size.planes
    tile, x_first, x_second, y_first, y_second = call(
        pack_kernel,
        size,
        [HBM] * 7,
        [VMEM] * 5,
        [shaped(planes, rows, cols)]
        + [shaped(2, rows, cols)] * 2
        + [shaped(planes, REACH, cols)] * 2,
        [pltpu.VMEM((2, rows, cols), jnp.int32), pltpu.SemaphoreType.DMA((7,))],
    )(
        *(
            pltpu.with_memory_space_constraint(array, pltpu.HBM)
            for array in (
                layer_east, layer_north, layer_press, surface, land_sea, bottom_level, coriolis
            )
        )
    )
    own = x_first, x_second
    got_y = swapped("gy", y_first, y_second)
    got = swapped("gx", *own)
    base, sums = call(
        middle_kernel,
        size,
        [SMEM, VMEM],
        [VMEM] * 2,
        [shaped(2, levels, rows, cols), shaped(6, wide, cols)],
        flops=10**7,
    )(level_thick, tile)
    corners = call(
        corner_kernel, size, [VMEM] * 3, [VMEM] * 2, [shaped(2, 2 * REACH, cols)] * 2
    )(*got_y, base)
    got_corners = swapped("gx", *corners)
    sums, statics, sides = call(
        side_kernel,
        size,
        [SMEM] + [VMEM] * 6,
        [VMEM] * 3,
        [shaped(6, wide, cols), shaped(6, wide, cols), shaped(rows, cols)],
        [pltpu.VMEM((2, 3, rows, cols), F32)],
        {6: 0},
        flops=10**7,
    )(level_thick, tile, *own, *got, sums)
    base, sums, statics = call(
        outer_kernel,
        size,
        [SMEM] + [VMEM] * 14,
        [VMEM] * 3,
        [shaped(2, levels, rows, cols), shaped(6, wide, cols), shaped(6, wide, cols)],
        [
            pltpu.VMEM((planes, 8 * REACH, cols), F32),
            pltpu.VMEM((2, 4, 8 * REACH, cols), F32),
            pltpu.VMEM((2, 2, 8 * REACH, cols), F32),
        ],
        {12: 0, 13: 1, 14: 2},
    )(level_thick, tile, *own, *got, *got_y, *corners, *got_corners, base, sums, statics)
    others = lax.ppermute(sums, "gz", pairing("gz")[0])
    base = call(
        finish_kernel,
        size,
        [SMEM] + [VMEM] * 2,
        [VMEM],
        [shaped(2, levels, rows, cols)],
        aliases={2: 0},
        flops=10**7,
    )(level_thick, sides, base)[0]
    height, east_next, north_next = call(
        surface_kernel,
        size,
        [VMEM] * 5,
        [HBM] * 3,
        [shaped(rows, cols), shaped(levels, rows, cols), shaped(levels, rows, cols)],
        [
            pltpu.VMEM((2, 3, wide + 2 * REACH, cols), F32),
            pltpu.VMEM((2, 5, wide + 2 * REACH, cols), F32),
            pltpu.VMEM((2, wide, cols), F32),
            pltpu.VMEM((2, levels, rows, cols), F32),
            pltpu.SemaphoreType.DMA((1 + 2 * levels,)),
        ],
    )(tile, base, statics, sums, others)
    return (height, east_next, north_next)


def solution(mesh):
    return jax.shard_map(
        on_device,
        mesh=mesh,
        in_specs=(
            P("gz", "gy", "gx"),
            P("gz", "gy", "gx"),
            P("gz", "gy", "gx"),
            P("gy", "gx"),
            P("gy", "gx"),
            P("gy", "gx"),
            P("gy", "gx"),
            P("gz"),
        ),
        out_specs=(P("gy", "gx"), P("gz", "gy", "gx"), P("gz", "gy", "gx")),
        check_vma=False,
    )
```

time: 35.5 us -> 28.5 us (0.80)
  waiting for transfers between devices: 13.2 us -> 6.01 us
  starting transfers between devices: 7.92 us -> 10.6 us
  Pallas kernels: 13.6 us -> 11 us
    ppermute x5 -> x7, waiting for transfers between devices: 13.2 us -> 6.01 us  [the longest x3 5.2 us: swapped(): second = lax.ppermute(second, axis, pairs[1])]
    ppermute x5 -> x7, starting transfers between devices: 7.92 us -> 10.6 us  [the longest x3 6.11 us: swapped(): first = lax.ppermute(first, axis, pairs[0])]
    pallas_call x4 -> x7, Pallas kernels: 13.6 us -> 11 us  [the longest x1 2.8 us: on_device(): call(pack_kernel, size, [HBM] * 7, [VMEM] * 5, [shaped(planes, rows, cols...]
  transfers between devices with their start and end apart: 5 -> 7, of which waited for: 5 -> 3; matrix products, arithmetic and copies ran while one was open for 0% -> 0% of each run, Pallas kernels for 0% -> 17%
where the time goes in v2:
time: 28.5 us; the launch traced here: 28.4 us
  Pallas kernels  11 us (39%)
  starting transfers between devices  10.6 us (37%)
  waiting for transfers between devices  6.01 us (21%)
  between operations  0.7 us (2%)
    ppermute x3, starting transfers between devices, swapped(): first = lax.ppermute(first, axis, pairs[0])  6.11 us
    ppermute x3, waiting for transfers between devices, swapped(): second = lax.ppermute(second, axis, pairs[1])  5.2 us
    ppermute x3, starting transfers between devices, swapped(): second = lax.ppermute(second, axis, pairs[1])  4.44 us
    pallas_call x1, Pallas kernels, on_device(): call(pack_kernel, size, [HBM] * 7, [VMEM] * 5, [shaped(planes, rows, cols...  2.8 us
    pallas_call x1, Pallas kernels, on_device(): call(surface_kernel, size, [VMEM] * 5, [HBM] * 3, [shaped(rows, cols), sh...  2.23 us
    pallas_call x1, Pallas kernels, on_device(): call(side_kernel, size, [SMEM] + [VMEM] * 6, [VMEM] * 3, [shaped(6, wide,...  2.07 us
    pallas_call x1, Pallas kernels, on_device(): call(middle_kernel, size, [SMEM, VMEM], [VMEM] * 2, [shaped(2, levels, ro...  1.53 us
    pallas_call x1, Pallas kernels, on_device(): call(outer_kernel, size, [SMEM] + [VMEM] * 14, [VMEM] * 3, [shaped(2, lev...  1.24 us
  transfers between devices with their start and end apart: 7, of which 3 were waited for; matrix products, arithmetic and copies ran while one was open for 0% of the time, Pallas kernels for 17%

profile of v2, /device:TPU:0, one launch (start us, length us, event | category | flops | bytes accessed | tf_op | source)
XLA Modules:
  0.0 28.4 jit_solution(17735575187045371773)
XLA Ops:
  0.6 0.0 copy-start
  0.6 2.8 %shard_map.103 = (f32[27,128,128]{2,1,0:T(8,128)S(1)}, f32[2,128,128]{2,1,0:T(8,128)S(1)}, f32[2,128,128]{2,1,0:T(8,128)S(1)}, f32[27,8,128]{2,1,0:T(8,128)S(1)}, f32[27,8,128]{2,1,0:T(8,128)S(1)}) custom-call(f32[8,128,128]{2,1,0:T(8,128)} %east.1, f32[8,128,128]{2,1,0:T(8,128)} %north.1, f32[8,128,128]{2,1,0:T(8,128)} %press.1, f32[128,128]{1,0:T(8,128)} %surface.1, ...), custom_call_target="tpu_custom_call" | custom-call | tf_op jit(solution)/shard_map/pallas_call | solution.py:625
  3.5 3.0 %collective-permute-start = (f32[2,128,128]{2,1,0:T(8,128)S(1)}, f32[2,128,128]{2,1,0:T(8,128)S(1)}, u32[]{:S(2)}, u32[]{:S(2)}) collective-permute-start(f32[2,128,128]{2,1,0:T(8,128)S(1)} %get-tuple-element.19.own_first), channel_id=1, source_target_pairs={{0,8},{8,0},{16,24},{24,16},{1,9},{9,1},{17,25},{25,17},{2,10},{10... | collective-permute-start | bytes 393224 | tf_op jit(solution)/shard_map/ppermute | solution.py:614
  6.5 1.5 %collective-permute-start.1 = (f32[2,128,128]{2,1,0:T(8,128)S(1)}, f32[2,128,128]{2,1,0:T(8,128)S(1)}, u32[]{:S(2)}, u32[]{:S(2)}) collective-permute-start(f32[2,128,128]{2,1,0:T(8,128)S(1)} %get-tuple-element.20.own_second), channel_id=1, source_target_pairs={{8,16},{16,8},{24,0},{0,24},{9,17},{17,9},{25,1},{1,25},{10,18},{1... | collective-permute-start | bytes 393224 | tf_op jit(solution)/shard_map/ppermute | solution.py:615
  8.0 1.6 %collective-permute-start.2 = (f32[27,8,128]{2,1,0:T(8,128)S(1)}, f32[27,8,128]{2,1,0:T(8,128)S(1)}, u32[]{:S(2)}, u32[]{:S(2)}) collective-permute-start(f32[27,8,128]{2,1,0:T(8,128)S(1)} %get-tuple-element.23), channel_id=1, source_target_pairs={{0,2},{2,0},{4,6},{6,4},{1,3},{3,1},{5,7},{7,5},{8,10},{10,8},{12,... | collective-permute-start | bytes 331784 | tf_op jit(solution)/shard_map/ppermute | solution.py:614
  9.6 2.5 %collective-permute-start.3 = (f32[27,8,128]{2,1,0:T(8,128)S(1)}, f32[27,8,128]{2,1,0:T(8,128)S(1)}, u32[]{:S(2)}, u32[]{:S(2)}) collective-permute-start(f32[27,8,128]{2,1,0:T(8,128)S(1)} %get-tuple-element.24), channel_id=1, source_target_pairs={{2,4},{4,2},{6,0},{0,6},{3,5},{5,3},{7,1},{1,7},{10,12},{12,10},{1... | collective-permute-start | bytes 331784 | tf_op jit(solution)/shard_map/ppermute | solution.py:615
  12.0 0.0 copy-done
  12.0 1.5 %shard_map.104 = (f32[2,8,128,128]{3,2,1,0:T(8,128)S(1)}, f32[6,144,128]{2,1,0:T(8,128)S(1)}) custom-call(f32[8]{0:T(128)S(1)} %copy-done, f32[27,128,128]{2,1,0:T(8,128)S(1)} %get-tuple-element.18.tile), custom_call_target="tpu_custom_call" | custom-call | flops 10000000 | tf_op jit(solution)/shard_map/pallas_call | solution.py:645
  13.6 0.0 collective-permute-done.2.y_first
  13.6 3.1 %collective-permute-done.3.y_second = f32[27,8,128]{2,1,0:T(8,128)S(1)} collective-permute-done((f32[27,8,128]{2,1,0:T(8,128)S(1)}, f32[27,8,128]{2,1,0:T(8,128)S(1)}, u32[]{:S(2)}, u32[]{:S(2)}) %collective-permute-start.3) | collective-permute-done | bytes 110624 | tf_op jit(solution)/shard_map/ppermute | solution.py:615
  16.7 0.2 shard_map.106
  16.9 1.5 %collective-permute-start.4 = (f32[2,16,128]{2,1,0:T(8,128)S(1)}, f32[2,16,128]{2,1,0:T(8,128)S(1)}, u32[]{:S(2)}, u32[]{:S(2)}) collective-permute-start(f32[2,16,128]{2,1,0:T(8,128)S(1)} %get-tuple-element.26.c_first), channel_id=1, source_target_pairs={{0,8},{8,0},{16,24},{24,16},{1,9},{9,1},{17,25},{25,17},{2,10},{10... | collective-permute-start | bytes 49160 | tf_op jit(solution)/shard_map/ppermute | solution.py:614
  18.4 0.5 %collective-permute-start.5 = (f32[2,16,128]{2,1,0:T(8,128)S(1)}, f32[2,16,128]{2,1,0:T(8,128)S(1)}, u32[]{:S(2)}, u32[]{:S(2)}) collective-permute-start(f32[2,16,128]{2,1,0:T(8,128)S(1)} %get-tuple-element.27.c_second), channel_id=1, source_target_pairs={{8,16},{16,8},{24,0},{0,24},{9,17},{17,9},{25,1},{1,25},{10,18},{1... | collective-permute-start | bytes 49160 | tf_op jit(solution)/shard_map/ppermute | solution.py:615
  18.9 0.0 collective-permute-done.got_first
  18.9 0.0 collective-permute-done.1.got_second
  18.9 2.1 %shard_map.105 = (f32[6,144,128]{2,1,0:T(8,128)S(1)}, f32[6,144,128]{2,1,0:T(8,128)S(1)}, f32[128,128]{1,0:T(8,128)S(1)}) custom-call(f32[8]{0:T(128)S(1)} %copy-done, f32[27,128,128]{2,1,0:T(8,128)S(1)} %get-tuple-element.18.tile, f32[2,128,128]{2,1,0:T(8,128)S(1)} %get-tuple-element.19.own_first, ...), custom_call_target="tpu_custom_call", output_to_operand_aliasing={{0}: (6, {})} | custom-call | flops 10000000 | tf_op jit(solution)/shard_map/pallas_call | solution.py:657
  21.0 0.0 collective-permute-done.4.c_got_first
  21.0 2.1 %collective-permute-done.5.c_got_second = f32[2,16,128]{2,1,0:T(8,128)S(1)} collective-permute-done((f32[2,16,128]{2,1,0:T(8,128)S(1)}, f32[2,16,128]{2,1,0:T(8,128)S(1)}, u32[]{:S(2)}, u32[]{:S(2)}) %collective-permute-start.5) | collective-permute-done | bytes 16416 | tf_op jit(solution)/shard_map/ppermute | solution.py:615
  23.0 1.2 %shard_map.107 = (f32[2,8,128,128]{3,2,1,0:T(8,128)S(1)}, f32[6,144,128]{2,1,0:T(8,128)S(1)}, f32[6,144,128]{2,1,0:T(8,128)S(1)}) custom-call(f32[8]{0:T(128)S(1)} %copy-done, f32[27,128,128]{2,1,0:T(8,128)S(1)} %get-tuple-element.18.tile, ...), custom_call_target="tpu_custom_call", output_to_operand_aliasing={{0}: (12, {}), {1}: (13, {}), {2}: (14, {})} | custom-call | tf_op jit(solution)/shard_map/pallas_call | solution.py:667
  24.3 0.1 collective-permute-start.6
  24.4 1.0 %shard_map.108.base = f32[2,8,128,128]{3,2,1,0:T(8,128)S(1)} custom-call(f32[8]{0:T(128)S(1)} %copy-done, f32[128,128]{1,0:T(8,128)S(1)} %get-tuple-element.22.sides_in, f32[2,8,128,128]{3,2,1,0:T(8,128)S(1)} %get-tuple-element.30.base_in), custom_call_target="tpu_custom_call", output_to_operand_aliasing={{}: (2, {})} | custom-call | flops 10000000 | tf_op jit(solution)/shard_map/pallas_call | solution.py:681
  25.3 0.8 %collective-permute-done.6.other = f32[6,144,128]{2,1,0:T(8,128)S(1)} collective-permute-done((f32[6,144,128]{2,1,0:T(8,128)S(1)}, f32[6,144,128]{2,1,0:T(8,128)S(1)}, u32[]{:S(2)}, u32[]{:S(2)}) %collective-permute-start.6) | collective-permute-done | bytes 442400 | tf_op jit(solution)/shard_map/ppermute | solution.py:680
  26.1 2.2 %shard_map.109 = (f32[128,128]{1,0:T(8,128)}, f32[8,128,128]{2,1,0:T(8,128)}, f32[8,128,128]{2,1,0:T(8,128)}) custom-call(f32[27,128,128]{2,1,0:T(8,128)S(1)} %get-tuple-element.18.tile, f32[2,8,128,128]{3,2,1,0:T(8,128)S(1)} %shard_map.108.base, f32[6,144,128]{2,1,0:T(8,128)S(1)} %get-tuple-element.31.statics, f32[6,144,128]{2,1,0:T(8,128)S(1)} %get-tuple-element.32.mine, ...), custom_call_target="tpu_custom_call" | custom-call | tf_op jit(solution)/shard_map/pallas_call | solution.py:690
Async XLA Ops:
  0.6 11.4 %copy-start = (f32[8]{0:T(128)S(1)}, f32[8]{0:T(128)}, u32[]{:S(2)}) copy-start(f32[8]{0:T(128)} %thick.7) | copy-start | bytes 100
  3.5 15.4 %collective-permute-start = (f32[2,128,128]{2,1,0:T(8,128)S(1)}, f32[2,128,128]{2,1,0:T(8,128)S(1)}, u32[]{:S(2)}, u32[]{:S(2)}) collective-permute-start(f32[2,128,128]{2,1,0:T(8,128)S(1)} %get-tuple-element.19.own_first), channel_id=1, source_target_pairs={{0,8},{8,0},{16,24},{24,16},{1,9},{9,1},{17,25},{25,17},{2,10},{10... | collective-permute-start | bytes 393224 | tf_op jit(solution)/shard_map/ppermute | solution.py:614
  6.5 12.4 %collective-permute-start.1 = (f32[2,128,128]{2,1,0:T(8,128)S(1)}, f32[2,128,128]{2,1,0:T(8,128)S(1)}, u32[]{:S(2)}, u32[]{:S(2)}) collective-permute-start(f32[2,128,128]{2,1,0:T(8,128)S(1)} %get-tuple-element.20.own_second), channel_id=1, source_target_pairs={{8,16},{16,8},{24,0},{0,24},{9,17},{17,9},{25,1},{1,25},{10,18},{1... | collective-permute-start | bytes 393224 | tf_op jit(solution)/shard_map/ppermute | solution.py:615
  8.0 5.6 %collective-permute-start.2 = (f32[27,8,128]{2,1,0:T(8,128)S(1)}, f32[27,8,128]{2,1,0:T(8,128)S(1)}, u32[]{:S(2)}, u32[]{:S(2)}) collective-permute-start(f32[27,8,128]{2,1,0:T(8,128)S(1)} %get-tuple-element.23), channel_id=1, source_target_pairs={{0,2},{2,0},{4,6},{6,4},{1,3},{3,1},{5,7},{7,5},{8,10},{10,8},{12,... | collective-permute-start | bytes 331784 | tf_op jit(solution)/shard_map/ppermute | solution.py:614
  9.6 7.2 %collective-permute-start.3 = (f32[27,8,128]{2,1,0:T(8,128)S(1)}, f32[27,8,128]{2,1,0:T(8,128)S(1)}, u32[]{:S(2)}, u32[]{:S(2)}) collective-permute-start(f32[27,8,128]{2,1,0:T(8,128)S(1)} %get-tuple-element.24), channel_id=1, source_target_pairs={{2,4},{4,2},{6,0},{0,6},{3,5},{5,3},{7,1},{1,7},{10,12},{12,10},{1... | collective-permute-start | bytes 331784 | tf_op jit(solution)/shard_map/ppermute | solution.py:615
  16.9 4.1 %collective-permute-start.4 = (f32[2,16,128]{2,1,0:T(8,128)S(1)}, f32[2,16,128]{2,1,0:T(8,128)S(1)}, u32[]{:S(2)}, u32[]{:S(2)}) collective-permute-start(f32[2,16,128]{2,1,0:T(8,128)S(1)} %get-tuple-element.26.c_first), channel_id=1, source_target_pairs={{0,8},{8,0},{16,24},{24,16},{1,9},{9,1},{17,25},{25,17},{2,10},{10... | collective-permute-start | bytes 49160 | tf_op jit(solution)/shard_map/ppermute | solution.py:614
  18.4 4.6 %collective-permute-start.5 = (f32[2,16,128]{2,1,0:T(8,128)S(1)}, f32[2,16,128]{2,1,0:T(8,128)S(1)}, u32[]{:S(2)}, u32[]{:S(2)}) collective-permute-start(f32[2,16,128]{2,1,0:T(8,128)S(1)} %get-tuple-element.27.c_second), channel_id=1, source_target_pairs={{8,16},{16,8},{24,0},{0,24},{9,17},{17,9},{25,1},{1,25},{10,18},{1... | collective-permute-start | bytes 49160 | tf_op jit(solution)/shard_map/ppermute | solution.py:615
  24.3 1.9 %collective-permute-start.6 = (f32[6,144,128]{2,1,0:T(8,128)S(1)}, f32[6,144,128]{2,1,0:T(8,128)S(1)}, u32[]{:S(2)}, u32[]{:S(2)}) collective-permute-start(f32[6,144,128]{2,1,0:T(8,128)S(1)} %get-tuple-element.32.mine), channel_id=1, source_target_pairs={{0,1},{1,0},{2,3},{3,2},{4,5},{5,4},{6,7},{7,6},{8,9},{9,8},{10,11... | collective-permute-start | bytes 1327112 | tf_op jit(solution)/shard_map/ppermute | solution.py:680

commit v3 on v0

v3 whole, which is shorter than its diff:
```python
import functools

import jax
import jax.numpy as jnp
from jax import lax
from jax.experimental import pallas as pl
from jax.experimental.pallas import tpu as pltpu
from jax.sharding import PartitionSpec as P


SUBSTEPS = 4
COURANT = 0.25
VISCOSITY = 0.1
REACH = 2 * SUBSTEPS
TIMESTEP = SUBSTEPS * COURANT
CHUNK = 2 * REACH

F32 = jnp.float32

FIELDS = 8
SURFACE, COUNT, CORIOLIS = 5, 6, 7
SUMS = 5


class Sizes:
    def __init__(self, levels, rows, cols):
        self.levels = levels
        self.rows = rows
        self.cols = cols
        self.wide = rows + 2 * REACH
        self.slots = cols // REACH
        self.half = cols // 2
        assert levels == REACH and self.slots == 2 * FIELDS
        assert rows % CHUNK == 0


def turned(value, shift):
    shift = shift % value.shape[-1]
    if shift == 0:
        return value
    return pltpu.roll(value, shift, axis=1)


def repeated(count):
    def run(body):
        for step in range(count):
            body(step)

    return run


def lane_ids(rows, cols):
    return lax.broadcasted_iota(jnp.int32, (rows, cols), 1)


def gathered(value, source):
    return jnp.take_along_axis(value, source, axis=1, mode="promise_in_bounds")


def pairing(axis):
    count = lax.axis_size(axis)
    steps = [(i, (i + 1) % count) for i in range(count)]
    if count % 2:
        return steps, [(target, source) for source, target in steps]
    swaps = [[], []]
    for source, target in steps:
        swaps[1 - source % 2] += [(source, target), (target, source)]
    return swaps


def roles(axis):
    if lax.axis_size(axis) % 2:
        return True, False
    odd = lax.axis_index(axis) % 2 == 1
    return odd, odd


def either(flag, first, second):
    if flag is True:
        return first
    if flag is False:
        return second
    return jnp.where(flag, first, second)


def pack_lines(size, load, like):
    cols, lane = size.cols, lane_ids(*like)
    low = high = jnp.zeros(like, F32)
    for plane in range(3 * size.levels):
        at = plane // size.levels * 2 * REACH + plane % size.levels
        value = turned(load(plane), at)
        low = jnp.where(lane == at, value, low)
        high = jnp.where(lane == (at - 1) % cols, value, high)
    return low, turned(high, REACH + 1)


def pack_columns(load, lines, like):
    slot_of = lane_ids(*like) // REACH
    low, high = lines
    for index in range(FIELDS):
        value = turned(load(index), (2 * index + 1) * REACH)
        low = jnp.where(slot_of == 2 * index + 1, value, low)
        high = jnp.where(slot_of == 2 * index, value, high)
    return low, high


def shifted_rows(value, shift):
    return pltpu.roll(value, shift % value.shape[0], axis=0)


def row_ids(rows, cols):
    return lax.broadcasted_iota(jnp.int32, (rows, cols), 0)


def split(flag, first, second):
    return either(flag, second, first), either(flag, first, second)


def by_level(thick, index):
    weight = jnp.zeros(index.shape, F32)
    for k in range(REACH):
        weight = jnp.where(index == k, thick[k], weight)
    return weight


def core_chunk(size, thick, first_level, row, here, over, under, cor, write):
    levels, cols = size.levels, size.cols
    count = 3 * levels
    cnt = here(count)
    lane = lane_ids(*cnt.shape)
    cnt_e = jnp.where(lane == cols - 1, -1.0, jnp.minimum(cnt, turned(cnt, -1)))
    cnt_w = jnp.where(lane == 0, -1.0, jnp.minimum(cnt, turned(cnt, 1)))
    cnt_n = jnp.where(row == size.rows - 1, -1.0, jnp.minimum(cnt, over(count)))
    cnt_s = jnp.where(row == 0, -1.0, jnp.minimum(cnt, under(count)))
    totals = [jnp.zeros(cnt.shape, F32)] * 5
    for k in range(levels):
        level = first_level + k
        wet, wet_e, wet_w, wet_n, wet_s = (
            level < c for c in (cnt, cnt_e, cnt_w, cnt_n, cnt_s)
        )
        u, v, p = here(k), here(levels + k), here(2 * levels + k)
        slow_u, slow_v, push = VISCOSITY * u, VISCOSITY * v, 0.5 * p
        u_less, u_more = slow_u - push, slow_u + push
        gain_e = jnp.where(wet_e, turned(u_less, -1) - u_less, 0.0)
        gain_e = gain_e + jnp.where(wet_w, turned(u_more, 1) - u_more, 0.0)
        gain_n = jnp.where(wet_e, turned(slow_v, -1) - slow_v, 0.0)
        gain_n = gain_n + jnp.where(wet_w, turned(slow_v, 1) - slow_v, 0.0)
        n_u, s_u = over(k) - u, under(k) - u
        n_v, s_v = over(levels + k) - v, under(levels + k) - v
        n_p, s_p = over(2 * levels + k) - p, p - under(2 * levels + k)
        gain_e = gain_e + VISCOSITY * (jnp.where(wet_n, n_u, 0.0) + jnp.where(wet_s, s_u, 0.0))
        gain_n = gain_n + jnp.where(wet_n, VISCOSITY * n_v - 0.5 * n_p, 0.0)
        gain_n = gain_n + jnp.where(wet_s, VISCOSITY * s_v - 0.5 * s_p, 0.0)
        wet_u, wet_v = jnp.where(wet, u, 0.0), jnp.where(wet, v, 0.0)
        tend_e, tend_n = gain_e + cor * wet_v, gain_n - cor * wet_u
        if write is not None:
            write(0, k, wet_u + TIMESTEP * tend_e)
            write(1, k, wet_v + TIMESTEP * tend_n)
        weight = thick[k]
        parts = (weight * tend_e, weight * tend_n, weight * wet_u, weight * wet_v)
        parts += (jnp.where(wet, weight, 0.0),)
        totals = [total + part for total, part in zip(totals, parts)]
    return totals


def edge_kernel(
    size, thick_hbm, east, north, press, surface, land, bottom, coriolis,
    y_first, y_second, weights, thick, levels_of, flat, whole, sems,
):
    levels, rows, cols = size.levels, size.rows, size.cols
    first_level = (lax.axis_index("gz") * levels).astype(F32)
    copies = [pltpu.make_async_copy(thick_hbm, thick, sems.at[0])]
    ends = ((0, REACH), (rows - CHUNK, 4 * REACH))
    for part, (source, target) in enumerate(ends):
        span = pl.ds(source, CHUNK)
        for index, array in enumerate((land, bottom)):
            at = whole.at[index, pl.ds(part * CHUNK, CHUNK), :]
            copies.append(pltpu.make_async_copy(array.at[span, :], at, sems.at[len(copies)]))
        for index, array in enumerate((surface, coriolis)):
            at = flat.at[index, pl.ds(target, CHUNK), :]
            copies.append(pltpu.make_async_copy(array.at[span, :], at, sems.at[len(copies)]))
        for slot, array in enumerate((east, north, press)):
            at = levels_of.at[pl.ds(slot * levels, levels), pl.ds(target, CHUNK), :]
            copies.append(pltpu.make_async_copy(array.at[:, span, :], at, sems.at[len(copies)]))
    for copy in copies:
        copy.start()
    for copy in copies:
        copy.wait()
    weights[0] = by_level(thick, row_ids(REACH, cols))
    weights[1] = by_level(thick, lane_ids(REACH, cols) % REACH)
    for part, (_, target) in enumerate(ends):
        span = slice(part * CHUNK, part * CHUNK + CHUNK)
        count = whole[0, span, :].astype(F32) * whole[1, span, :].astype(F32)
        levels_of[3 * levels, target : target + CHUNK, :] = count

    starts = (REACH, 4 * REACH + REACH)

    def joined(ref, plane, move=0):
        return jnp.concatenate([ref[plane, at + move : at + move + REACH, :] for at in starts])

    def load(move):
        return lambda plane: joined(levels_of, plane, move)

    like = (CHUNK, cols)
    row = row_ids(*like)
    row = jnp.where(row < REACH, row, row + rows - CHUNK)
    cor = joined(flat, 1)
    fields = core_chunk(
        size, thick, first_level, row, load(0), load(1), load(-1), cor, None
    )
    fields += [joined(flat, 0), load(0)(3 * levels), cor]
    low, high = pack_lines(size, load(0), like)
    fields.append(low + high)
    y_flag, _ = roles("gy")

    def store(index, south, north):
        y_first[index] = either(y_flag, north, south)
        y_second[index] = either(y_flag, south, north)

    for index, value in enumerate(fields):
        store(index, value[:REACH], value[REACH:])
    for slot in range(3):
        planes = slice(slot * levels, (slot + 1) * levels)
        store(
            FIELDS + 1 + slot,
            *(levels_of[planes, at, :] for at in (REACH, 4 * REACH + CHUNK - 1)),
        )


def tile_kernel(
    size, thick, east, north, press, surface, land, bottom, coriolis, after,
    base, sums, statics, x_first, x_second,
):
    del after
    levels, rows, cols = size.levels, size.rows, size.cols
    first_level = (lax.axis_index("gz") * levels).astype(F32)
    span = slice(REACH, REACH + rows)
    statics[0, span, :] = surface[...]
    statics[1, span, :] = land[...].astype(F32) * bottom[...].astype(F32)
    statics[2, span, :] = coriolis[...]
    fields = (east, north, press)
    x_flag, _ = roles("gx")
    like = (CHUNK, cols)
    for start in range(0, rows, CHUNK):

        def load(move):
            at = start + move

            def value(plane):
                if plane == 3 * levels:
                    return statics[1, REACH + at : REACH + at + CHUNK, :]
                ref, level = fields[plane // levels], plane % levels
                if 0 <= at <= rows - CHUNK:
                    return ref[level, at : at + CHUNK, :]
                return shifted_rows(ref[level, start : start + CHUNK, :], -move)

            return value

        here, place = slice(start, start + CHUNK), slice(start + REACH, start + REACH + CHUNK)

        def write(field, k, value):
            base[field, k, here, :] = value

        totals = core_chunk(
            size, thick, first_level, start + row_ids(*like), load(0), load(1), load(-1),
            statics[2, place, :], write,
        )
        for index, total in enumerate(totals):
            sums[index, place, :] = total
        totals += [statics[index, place, :] for index in range(3)]
        low, high = pack_columns(lambda index: totals[index], pack_lines(size, load(0), like), like)
        x_first[place, :] = either(x_flag, high, low)
        x_second[place, :] = either(x_flag, low, high)


def row_kernel(
    size, weights, own_first, own_second, got_first, got_second,
    sums_in, statics_in, x_first_in, x_second_in,
    sums, statics, x_first, x_second, flux,
):
    del sums_in, statics_in, x_first_in, x_second_in
    levels, rows, cols = size.levels, size.rows, size.cols
    first_level = (lax.axis_index("gz") * levels).astype(F32)
    high_first, north_first = roles("gy")
    x_flag, _ = roles("gx")
    top = REACH + rows
    halo = [split(north_first, got_first[i], got_second[i]) for i in range(FIELDS + 4)]
    mine = [split(high_first, own_first[i], own_second[i]) for i in range(FIELDS + 4)]
    row = row_ids(REACH, cols)
    weight, level_of = weights[0], row.astype(F32) + first_level
    end = REACH - 1
    blocks = [
        [pair[part] for pair in pairs[:FIELDS]]
        for pairs, part in ((halo, 0), (mine, 0), (mine, 1), (halo, 1))
    ]
    lines = [
        pairs[FIELDS][part] for pairs, part in ((halo, 0), (mine, 0), (mine, 1), (halo, 1))
    ]
    for side in range(2):
        south = [(halo[i][0], mine[i][1])[side] for i in range(FIELDS + 4)]
        north = [(mine[i][0], halo[i][1])[side] for i in range(FIELDS + 4)]
        counts = jnp.minimum(south[COUNT][end:, :], north[COUNT][:1, :])
        wet = level_of < jnp.broadcast_to(counts, (REACH, cols))
        change_u, change_v, push = (
            jnp.where(wet, north[FIELDS + 1 + slot] - south[FIELDS + 1 + slot], 0.0)
            for slot in range(3)
        )
        change_u, change_v, push = VISCOSITY * change_u, VISCOSITY * change_v, 0.5 * push
        to_north = (-change_u, -change_v - push)
        to_south = (change_u, change_v - push)
        for field in range(2):
            flux[side, field] = (to_north, to_south)[side][field]
            for block, line, value in (
                (2 * side, end, to_south[field]), (2 * side + 1, 0, to_north[field])
            ):
                gain = jnp.sum(weight * value, axis=0, keepdims=True)
                gain = jnp.where(row == line, jnp.broadcast_to(gain, (REACH, cols)), 0.0)
                blocks[block][field] = blocks[block][field] + gain
    slot_of = lane_ids(REACH, cols) // REACH
    for block, start in enumerate((0, REACH, top - REACH, top)):
        place = slice(start, start + REACH)
        for index in range(SUMS):
            sums[index, place, :] = blocks[block][index]
        for index in range(3):
            statics[index, place, :] = blocks[block][SUMS + index]
        low_line = jnp.where((slot_of < 6) & (slot_of % 2 == 0), lines[block], 0.0)
        high_line = jnp.where((slot_of < 6) & (slot_of % 2 == 1), lines[block], 0.0)
        low, high = pack_columns(
            lambda index: blocks[block][index], (low_line, high_line), (REACH, cols)
        )
        x_first[place, :] = either(x_flag, high, low)
        x_second[place, :] = either(x_flag, low, high)


def column_kernel(
    size, weights, own_first, own_second, got_first, got_second, sums_in,
    sums, flux,
):
    levels, wide, cols = size.levels, size.wide, size.cols
    first_level = (lax.axis_index("gz") * levels).astype(F32)
    high_first, east_first = roles("gx")
    west, east = split(east_first, got_first[...], got_second[...])
    low, high = split(high_first, own_first[...], own_second[...])
    left, right = jnp.concatenate([west, high]), jnp.concatenate([low, east])
    lane = lane_ids(2 * wide, cols)
    slot_of, place = lane // REACH, lane % REACH
    change = turned(right, REACH) - left
    push = turned(change, -4 * REACH)
    counts = jnp.minimum(
        gathered(left, jnp.full_like(lane, (2 * COUNT + 1) * REACH - 1)),
        gathered(right, jnp.full_like(lane, (2 * COUNT + 1) * REACH)),
    )
    wet = (place.astype(F32) + first_level < counts) & ((slot_of == 1) | (slot_of == 3))
    change = jnp.where(wet, VISCOSITY * change, 0.0)
    push = jnp.where(wet & (slot_of == 1), 0.5 * push, 0.0)
    to_east, to_west = -change - push, change - push
    flux[0], flux[1] = to_east[:wide], to_west[wide:]
    weight = jnp.concatenate([weights[1]] * (2 * wide // REACH))
    total = weight * to_east + turned(weight * to_west, size.half)
    for shift in (1, 2, 4):
        total = total + turned(total, shift)
    end = REACH - 1
    at_west, at_east = total[:wide], total[wide:]
    lane = lane_ids(wide, cols)
    for index in range(2):
        source = (2 * index + 1) * REACH + end
        gain = jnp.where(lane == 0, turned(at_west, -source), 0.0)
        gain = gain + jnp.where(
            lane == cols - 1, turned(at_east, cols - 1 - size.half - source), 0.0
        )
        sums[index] = sums_in[index] + gain
    slot_of, place = lane // REACH, lane % REACH
    outer_west = (slot_of == 0) | (slot_of == 2)
    outer_east = (slot_of == 1) | (slot_of == 3)
    gain = jnp.where(
        outer_west & (place == end), turned(at_west, -size.half - REACH), 0.0
    ) + jnp.where(outer_east & (place == 0), turned(at_east, -end), 0.0)
    sums[SUMS] = jnp.where(slot_of % 2 == 0, west, east) + gain


def finish_kernel(size, column_flux, row_flux, base_in, base):
    levels, rows, cols = size.levels, size.rows, size.cols
    lane = lane_ids(CHUNK, cols)
    for start in range(0, rows, CHUNK):
        at = slice(start, start + CHUNK)
        wider = slice(start + REACH, start + REACH + CHUNK)
        west, east = column_flux[0, wider, :], column_flux[1, wider, :]
        for field in range(2):
            for k in range(levels):
                source = (2 * field + 1) * REACH + k
                gain = jnp.where(lane == 0, turned(west, -source), 0.0)
                gain = gain + jnp.where(
                    lane == cols - 1, turned(east, cols - 1 - source), 0.0
                )
                base[field, k, at, :] = base_in[field, k, at, :] + TIMESTEP * gain
    for field in range(2):
        for side, at in enumerate((0, rows - 1)):
            for k in range(levels):
                line = slice(at, at + 1)
                gain = row_flux[side, field, k : k + 1, :]
                base[field, k, line, :] = base[field, k, line, :] + TIMESTEP * gain


def surface_kernel(
    size, base, statics, mine, other,
    height_out, east_out, north_out,
    state, fixed, drive, result, sems,
):
    levels, rows, cols, wide = size.levels, size.rows, size.cols, size.wide
    top = 2 * REACH
    first_level = (lax.axis_index("gz") * levels).astype(F32)
    lane = lane_ids(CHUNK, cols)
    H, TE, TN = range(3)
    OC, DP, CO, FE, FN = range(5)
    chunks = [REACH + at for at in range(0, wide, CHUNK)]

    @repeated(wide // CHUNK)
    def _(step):
        place = pl.ds(step * CHUNK, CHUNK)
        here = pl.ds(REACH + step * CHUNK, CHUNK)
        total = [mine[index, place, :] + other[index, place, :] for index in range(SUMS)]
        strip = mine[SUMS, place, :]
        strip = jnp.where(
            lane < 2 * SUMS * REACH, strip + other[SUMS, place, :], strip
        )

        def outer(index):
            moved = turned(strip, (size.slots - 1 - 2 * index) * REACH)
            return jnp.where((lane < REACH) | (lane >= cols - REACH), moved, 0.0)

        fixed[0, FE, here, :] = total[0]
        fixed[0, FN, here, :] = total[1]
        state[0, TE, here, :] = total[2]
        state[0, TN, here, :] = total[3]
        drive[0, place, :] = total[2] + TIMESTEP * total[0]
        drive[1, place, :] = total[3] + TIMESTEP * total[1]
        fixed[0, DP, here, :] = total[4]
        fixed[1, FE, here, :] = outer(0)
        fixed[1, FN, here, :] = outer(1)
        state[1, TE, here, :] = outer(2)
        state[1, TN, here, :] = outer(3)
        fixed[1, DP, here, :] = outer(4)
        state[0, H, here, :] = statics[0, place, :]
        state[1, H, here, :] = outer(SURFACE)
        fixed[0, OC, here, :] = jnp.where(statics[1, place, :] > 0, 1.0, 0.0)
        fixed[1, OC, here, :] = jnp.where(outer(COUNT) > 0, 1.0, 0.0)
        fixed[0, CO, here, :] = statics[2, place, :]
        fixed[1, CO, here, :] = outer(CORIOLIS)

    def difference_x(field, here):
        inside, outside = state[0, field, here, :], state[1, field, here, :]
        in_e, out_e = turned(inside, -1), turned(outside, -1)
        in_w, out_w = turned(inside, 1), turned(outside, 1)
        at_high, at_low = lane == cols - 1, lane == 0
        return (
            0.5 * (jnp.where(at_high, out_e, in_e) - jnp.where(at_low, out_w, in_w)),
            0.5 * (jnp.where(at_high, in_e, out_e) - jnp.where(at_low, in_w, out_w)),
        )

    def difference_y(part, field, start):
        above = state[part, field, start + 1 : start + 1 + CHUNK, :]
        return 0.5 * (above - state[part, field, start - 1 : start - 1 + CHUNK, :])

    for _ in range(SUBSTEPS):
        for start in chunks:
            here = slice(start, start + CHUNK)
            across = difference_x(TE, here)
            for part in range(2):
                spread = across[part] + difference_y(part, TN, start)
                height = state[part, H, here, :] - COURANT * spread
                state[part, H, here, :] = fixed[part, OC, here, :] * height
        for start in chunks:
            here = slice(start, start + CHUNK)
            across = difference_x(H, here)
            for part in range(2):
                slope_y = difference_y(part, H, start)
                te, tn = state[part, TE, here, :], state[part, TN, here, :]
                oc, dp, co, fe, fn = (fixed[part, index, here, :] for index in range(5))
                state[part, TE, here, :] = oc * (
                    te + COURANT * (-dp * across[part] + co * tn + fe)
                )
                state[part, TN, here, :] = oc * (tn + COURANT * (-dp * slope_y - co * te + fn))

    height_copy = pltpu.make_async_copy(
        state.at[0, H, pl.ds(top, rows), :], height_out, sems.at[0]
    )
    height_copy.start()
    inner = slice(top, top + rows)
    floor_depth = fixed[0, DP, inner, :] + (1.0 - fixed[0, OC, inner, :])
    for index, field in enumerate((TE, TN)):
        gain = state[0, field, inner, :] - drive[index, REACH : REACH + rows, :]
        drive[index, REACH : REACH + rows, :] = gain / floor_depth
    copies = [height_copy]
    for k in range(levels):
        wet = first_level + k < statics[1, REACH : REACH + rows, :]
        for index, out in enumerate((east_out, north_out)):
            change = jnp.where(wet, drive[index, REACH : REACH + rows, :], 0.0)
            result[index, k] = base[index, k] + change
            copy = pltpu.make_async_copy(
                result.at[index, k], out.at[k], sems.at[1 + 2 * k + index]
            )
            copy.start()
            copies.append(copy)
    for copy in copies:
        copy.wait()


VMEM = pl.BlockSpec(memory_space=pltpu.VMEM)
SMEM = pl.BlockSpec(memory_space=pltpu.SMEM)
HBM = pl.BlockSpec(memory_space=pltpu.HBM)


def shaped(*shape):
    return jax.ShapeDtypeStruct(shape, F32)


def call(body, size, ins, outs, shapes, scratch=(), aliases=None, flops=0):
    return pl.pallas_call(
        functools.partial(body, size),
        in_specs=ins,
        out_specs=outs,
        out_shape=shapes,
        scratch_shapes=scratch,
        input_output_aliases=aliases or {},
        compiler_params=pltpu.CompilerParams(vmem_limit_bytes=24 * 1024 * 1024),
        cost_estimate=pl.CostEstimate(flops=flops, bytes_accessed=0, transcendentals=0),
    )


def swapped(axis, first, second):
    pairs = pairing(axis)
    first = lax.ppermute(first, axis, pairs[0])
    second = lax.ppermute(second, axis, pairs[1])
    return first, second


def on_device(
    layer_east, layer_north, layer_press, surface, land_sea, bottom_level, coriolis, level_thick
):
    size = Sizes(*layer_east.shape)
    levels, rows, cols = layer_east.shape
    wide = size.wide
    inputs = [
        pltpu.with_memory_space_constraint(array, pltpu.HBM)
        for array in (
            level_thick, layer_east, layer_north, layer_press,
            surface, land_sea, bottom_level, coriolis,
        )
    ]
    side = shaped(FIELDS + 4, REACH, cols)
    *own_y, weights = call(
        edge_kernel,
        size,
        [HBM] * 8,
        [VMEM] * 3,
        [side, side, shaped(2, REACH, cols)],
        [
            pltpu.SMEM((levels,), F32),
            pltpu.VMEM((3 * levels + 1, 7 * REACH, cols), F32),
            pltpu.VMEM((2, 7 * REACH, cols), F32),
            pltpu.VMEM((2, 2 * CHUNK, cols), jnp.int32),
            pltpu.SemaphoreType.DMA((15,)),
        ],
    )(*inputs)
    got_y = swapped("gy", *own_y)
    base, sums, statics, x_first, x_second = call(
        tile_kernel,
        size,
        [SMEM] + [VMEM] * 8,
        [VMEM] * 5,
        [
            shaped(2, levels, rows, cols),
            shaped(SUMS + 1, wide, cols),
            shaped(3, wide, cols),
            shaped(wide, cols),
            shaped(wide, cols),
        ],
        flops=10**7,
    )(
        level_thick, layer_east, layer_north, layer_press,
        surface, land_sea, bottom_level, coriolis, own_y[0],
    )
    sums, statics, x_first, x_second, row_flux = call(
        row_kernel,
        size,
        [VMEM] * 9,
        [VMEM] * 5,
        [
            shaped(SUMS + 1, wide, cols),
            shaped(3, wide, cols),
            shaped(wide, cols),
            shaped(wide, cols),
            shaped(2, 2, levels, cols),
        ],
        aliases={5: 0, 6: 1, 7: 2, 8: 3},
    )(weights, *own_y, *got_y, sums, statics, x_first, x_second)
    got_x = swapped("gx", x_first, x_second)
    sums, column_flux = call(
        column_kernel,
        size,
        [VMEM] * 6,
        [VMEM] * 2,
        [shaped(SUMS + 1, wide, cols), shaped(2, wide, cols)],
        aliases={5: 0},
    )(weights, x_first, x_second, *got_x, sums)
    others = lax.ppermute(sums, "gz", pairing("gz")[0])
    base = call(
        finish_kernel,
        size,
        [VMEM] * 3,
        [VMEM],
        [shaped(2, levels, rows, cols)],
        aliases={2: 0},
        flops=10**7,
    )(column_flux, row_flux, base)[0]
    height, east_next, north_next = call(
        surface_kernel,
        size,
        [VMEM] * 4,
        [HBM] * 3,
        [shaped(rows, cols), shaped(levels, rows, cols), shaped(levels, rows, cols)],
        [
            pltpu.VMEM((2, 3, wide + 2 * REACH, cols), F32),
            pltpu.VMEM((2, 5, wide + 2 * REACH, cols), F32),
            pltpu.VMEM((2, wide, cols), F32),
            pltpu.VMEM((2, levels, rows, cols), F32),
            pltpu.SemaphoreType.DMA((1 + 2 * levels,)),
        ],
    )(base, statics, sums, others)
    return (height, east_next, north_next)


def solution(mesh):
    return jax.shard_map(
        on_device,
        mesh=mesh,
        in_specs=(
            P("gz", "gy", "gx"),
            P("gz", "gy", "gx"),
            P("gz", "gy", "gx"),
            P("gy", "gx"),
            P("gy", "gx"),
            P("gy", "gx"),
            P("gy", "gx"),
            P("gz"),
        ),
        out_specs=(P("gy", "gx"), P("gz", "gy", "gx"), P("gz", "gy", "gx")),
        check_vma=False,
    )
```

time: 104 us -> 23.2 us (0.22)
  waiting for transfers between devices: 50.2 us -> 5.62 us
  other arithmetic: 17.9 us -> 0 us
  between operations: 14.4 us -> 0.79 us
  Pallas kernels: 0 us -> 7.85 us
  local copies, waits for them, and re-layouts: 6.62 us -> 0.04 us
  starting transfers between devices: 14.7 us -> 8.71 us
    ppermute x8 -> x5, waiting for transfers between devices: 30.4 us -> 5.62 us  [the longest x2 3.08 us: swapped(): first = lax.ppermute(first, axis, pairs[0])]
    psum x1 -> x0, waiting for transfers between devices: 19.8 us -> none  [on_device(): totals = lax.psum(partial_sums, 'gz')]
    pallas_call x0 -> x6, Pallas kernels: none -> 7.85 us  [the longest x1 2.53 us: on_device(): call(tile_kernel, size, [SMEM] + [VMEM] * 8, [VMEM] * 5, [shaped(2, level...]
    reduce_sum x1 -> x0, other arithmetic: 7.85 us -> none  [on_device(): jnp.sum(thick * active, axis=0)]
    ppermute x8 -> x5, starting transfers between devices: 14.7 us -> 8.71 us  [the longest x2 4.99 us: swapped(): first = lax.ppermute(first, axis, pairs[0])]
    mul x8 -> x0, other arithmetic: 4.85 us -> none  [the longest x1 2.49 us: on_device(): active * (masked_north + timestep * tend_north + (trans_north - sum_north...]
    unnamed x37 -> x16, local copies, waits for them, and re-layouts: 3.52 us -> 0.04 us
    slice x4 -> x0, local copies, waits for them, and re-layouts: 2.01 us -> none  [the longest x3 1.39 us: extended(): lax.slice_in_dim(block, block.shape[dim] - width, None, axis=dim)]
  transfers between devices with their start and end apart: 9 -> 5, of which waited for: 7 -> 4; matrix products, arithmetic and copies ran while one was open for 1% -> 0% of each run, Pallas kernels for 0% -> 14%
where the time goes in v3:
time: 23.2 us; the launch traced here: 23 us
  starting transfers between devices  8.71 us (38%)
  Pallas kernels  7.85 us (34%)
  waiting for transfers between devices  5.62 us (24%)
  between operations  0.79 us (3%)
    ppermute x2, starting transfers between devices, swapped(): first = lax.ppermute(first, axis, pairs[0])  4.99 us
    ppermute x2, starting transfers between devices, swapped(): second = lax.ppermute(second, axis, pairs[1])  3.65 us
    ppermute x2, waiting for transfers between devices, swapped(): first = lax.ppermute(first, axis, pairs[0])  3.08 us
    pallas_call x1, Pallas kernels, on_device(): call(tile_kernel, size, [SMEM] + [VMEM] * 8, [VMEM] * 5, [shaped(2, level...  2.53 us
    pallas_call x1, Pallas kernels, on_device(): call(surface_kernel, size, [VMEM] * 4, [HBM] * 3, [shaped(rows, cols), sh...  2.18 us
    pallas_call x1, Pallas kernels, on_device(): call(edge_kernel, size, [HBM] * 8, [VMEM] * 3, [side, side, shaped(2, REA...  1.56 us
    ppermute x2, waiting for transfers between devices, swapped(): second = lax.ppermute(second, axis, pairs[1])  1.55 us
    ppermute x1, waiting for transfers between devices, on_device(): others = lax.ppermute(sums, 'gz', pairing('gz')[0])  0.98 us
  transfers between devices with their start and end apart: 5, of which 4 were waited for; matrix products, arithmetic and copies ran while one was open for 0% of the time, Pallas kernels for 14%

profile of v3, /device:TPU:0, one launch (start us, length us, event | category | flops | bytes accessed | tf_op | source)
XLA Modules:
  0.0 23.0 jit_solution(3291089704432353039)
XLA Ops:
  0.6 0.0 copy-start.6
  0.6 0.0 copy-start.5
  0.7 0.0 copy-start.4
  0.7 0.0 copy-start.3
  0.7 0.0 copy-start.2
  0.7 0.0 copy-start.1
  0.7 0.0 copy-start
  0.7 1.6 %shard_map.103 = (f32[12,8,128]{2,1,0:T(8,128)S(1)}, f32[12,8,128]{2,1,0:T(8,128)S(1)}, f32[2,8,128]{2,1,0:T(8,128)S(1)}) custom-call(f32[8]{0:T(128)} %thick.1, f32[8,128,128]{2,1,0:T(8,128)} %east.3, f32[8,128,128]{2,1,0:T(8,128)} %north.3, f32[8,128,128]{2,1,0:T(8,128)} %press.3, f32[128,128]{1,0:T(8,128)} %surface.3, s32[128,128]{1,0:T(8,128)} %land.3, ...), custom_call_target="tpu_custom_call" | custom-call | tf_op jit(solution)/shard_map/pallas_call | solution.py:551
  2.3 0.0 copy-start.7
  2.3 3.1 %collective-permute-start.1 = (f32[12,8,128]{2,1,0:T(8,128)S(1)}, f32[12,8,128]{2,1,0:T(8,128)S(1)}, u32[]{:S(2)}, u32[]{:S(2)}) collective-permute-start(f32[12,8,128]{2,1,0:T(8,128)S(1)} %get-tuple-element.20.own_second), channel_id=1, source_target_pairs={{0,2},{2,0},{4,6},{6,4},{1,3},{3,1},{5,7},{7,5},{8,10},{10,8},{12,... | collective-permute-start | bytes 147464 | tf_op jit(solution)/shard_map/ppermute | solution.py:533
  5.4 2.5 %collective-permute-start = (f32[12,8,128]{2,1,0:T(8,128)S(1)}, f32[12,8,128]{2,1,0:T(8,128)S(1)}, u32[]{:S(2)}, u32[]{:S(2)}) collective-permute-start(f32[12,8,128]{2,1,0:T(8,128)S(1)} %get-tuple-element.19.after.own_first), channel_id=1, source_target_pairs={{2,4},{4,2},{6,0},{0,6},{3,5},{5,3},{7,1},{1,7},{10,12},{12,10},{1... | collective-permute-start | bytes 147464 | tf_op jit(solution)/shard_map/ppermute | solution.py:532
  7.9 0.0 copy-done.6
  7.9 0.0 copy-done.5
  7.9 0.0 copy-done.4
  7.9 0.0 copy-done.3
  7.9 0.0 copy-done.2
  7.9 0.0 copy-done.1
  7.9 0.0 copy-done
  7.9 0.0 copy-done.7
  7.9 2.5 %shard_map.104 = (f32[2,8,128,128]{3,2,1,0:T(8,128)S(1)}, f32[6,144,128]{2,1,0:T(8,128)S(1)}, f32[3,144,128]{2,1,0:T(8,128)S(1)}, f32[144,128]{1,0:T(8,128)S(1)}, f32[144,128]{1,0:T(8,128)S(1)}) custom-call(f32[8]{0:T(128)S(1)} %copy-done.7, f32[8,128,128]{2,1,0:T(8,128)S(1)} %copy-done, f32[8,128,128]{2,1,0:T(8,128)S(1)} %copy-done.1, ...), custom_call_target="tpu_custom_call" | custom-call | flops 10000000 | tf_op jit(solution)/shard_map/pallas_call | solution.py:566
  10.5 0.0 collective-permute-done.1.got_second
  10.5 0.8 %collective-permute-done.got_first = f32[12,8,128]{2,1,0:T(8,128)S(1)} collective-permute-done((f32[12,8,128]{2,1,0:T(8,128)S(1)}, f32[12,8,128]{2,1,0:T(8,128)S(1)}, u32[]{:S(2)}, u32[]{:S(2)}) %collective-permute-start) | collective-permute-done | bytes 49184 | tf_op jit(solution)/shard_map/ppermute | solution.py:532
  11.3 0.1 shard_map.105
  11.4 2.5 %collective-permute-start.2 = (f32[144,128]{1,0:T(8,128)S(1)}, f32[144,128]{1,0:T(8,128)S(1)}, u32[]{:S(2)}, u32[]{:S(2)}) collective-permute-start(f32[144,128]{1,0:T(8,128)S(1)} %get-tuple-element.25.own_first), channel_id=1, source_target_pairs={{8,16},{16,8},{24,0},{0,24},{9,17},{17,9},{25,1},{1,25},{10,18},{1... | collective-permute-start | bytes 221192 | tf_op jit(solution)/shard_map/ppermute | solution.py:532
  13.9 0.5 %collective-permute-start.3 = (f32[144,128]{1,0:T(8,128)S(1)}, f32[144,128]{1,0:T(8,128)S(1)}, u32[]{:S(2)}, u32[]{:S(2)}) collective-permute-start(f32[144,128]{1,0:T(8,128)S(1)} %get-tuple-element.26.own_second), channel_id=1, source_target_pairs={{0,8},{8,0},{16,24},{24,16},{1,9},{9,1},{17,25},{25,17},{2,10},{10... | collective-permute-start | bytes 221192 | tf_op jit(solution)/shard_map/ppermute | solution.py:533
  14.5 2.3 %collective-permute-done.2.got_first = f32[144,128]{1,0:T(8,128)S(1)} collective-permute-done((f32[144,128]{1,0:T(8,128)S(1)}, f32[144,128]{1,0:T(8,128)S(1)}, u32[]{:S(2)}, u32[]{:S(2)}) %collective-permute-start.2) | collective-permute-done | bytes 73760 | tf_op jit(solution)/shard_map/ppermute | solution.py:532
  16.7 1.5 %collective-permute-done.3.got_second = f32[144,128]{1,0:T(8,128)S(1)} collective-permute-done((f32[144,128]{1,0:T(8,128)S(1)}, f32[144,128]{1,0:T(8,128)S(1)}, u32[]{:S(2)}, u32[]{:S(2)}) %collective-permute-start.3) | collective-permute-done | bytes 73760 | tf_op jit(solution)/shard_map/ppermute | solution.py:533
  18.3 0.7 %shard_map.106 = (f32[6,144,128]{2,1,0:T(8,128)S(1)}, f32[2,144,128]{2,1,0:T(8,128)S(1)}) custom-call(f32[2,8,128]{2,1,0:T(8,128)S(1)} %get-tuple-element.18.weights, f32[144,128]{1,0:T(8,128)S(1)} %get-tuple-element.25.own_first, f32[144,128]{1,0:T(8,128)S(1)} %get-tuple-element.26.own_second, ...), custom_call_target="tpu_custom_call", output_to_operand_aliasing={{0}: (5, {})} | custom-call | tf_op jit(solution)/shard_map/pallas_call | solution.py:598
  19.0 0.1 collective-permute-start.4
  19.0 0.8 %shard_map.107.base = f32[2,8,128,128]{3,2,1,0:T(8,128)S(1)} custom-call(f32[2,144,128]{2,1,0:T(8,128)S(1)} %get-tuple-element.28.column_flux, f32[2,2,8,128]{3,2,1,0:T(8,128)S(1)} %get-tuple-element.29.row_flux, f32[2,8,128,128]{3,2,1,0:T(8,128)S(1)} %get-tuple-element.30.base_in), custom_call_target="tpu_custom_call", output_to_operand_aliasing={{}: (2, {})} | custom-call | flops 10000000 | tf_op jit(solution)/shard_map/pallas_call | solution.py:607
  19.8 1.0 %collective-permute-done.4.other = f32[6,144,128]{2,1,0:T(8,128)S(1)} collective-permute-done((f32[6,144,128]{2,1,0:T(8,128)S(1)}, f32[6,144,128]{2,1,0:T(8,128)S(1)}, u32[]{:S(2)}, u32[]{:S(2)}) %collective-permute-start.4) | collective-permute-done | bytes 442400 | tf_op jit(solution)/shard_map/ppermute | solution.py:606
  20.8 2.2 %shard_map.108 = (f32[128,128]{1,0:T(8,128)}, f32[8,128,128]{2,1,0:T(8,128)}, f32[8,128,128]{2,1,0:T(8,128)}) custom-call(f32[2,8,128,128]{3,2,1,0:T(8,128)S(1)} %shard_map.107.base, f32[3,144,128]{2,1,0:T(8,128)S(1)} %get-tuple-element.31.statics, f32[6,144,128]{2,1,0:T(8,128)S(1)} %get-tuple-element.32.mine, f32[6,144,128]{2,1,0:T(8,128)S(1)} %collective-permute-done.4.other), custom_call_target="tpu_custom_call" | custom-call | tf_op jit(solution)/shard_map/pallas_call | solution.py:616
Async XLA Ops:
  0.6 7.2 %copy-start.6 = (f32[128,128]{1,0:T(8,128)S(1)}, f32[128,128]{1,0:T(8,128)}, u32[]{:S(2)}) copy-start(f32[128,128]{1,0:T(8,128)} %coriolis.3) | copy-start | bytes 196612
  0.6 7.2 %copy-start.5 = (s32[128,128]{1,0:T(8,128)S(1)}, s32[128,128]{1,0:T(8,128)}, u32[]{:S(2)}) copy-start(s32[128,128]{1,0:T(8,128)} %bottom.3) | copy-start | bytes 196612
  0.7 7.2 %copy-start.4 = (s32[128,128]{1,0:T(8,128)S(1)}, s32[128,128]{1,0:T(8,128)}, u32[]{:S(2)}) copy-start(s32[128,128]{1,0:T(8,128)} %land.3) | copy-start | bytes 196612
  0.7 7.2 %copy-start.3 = (f32[128,128]{1,0:T(8,128)S(1)}, f32[128,128]{1,0:T(8,128)}, u32[]{:S(2)}) copy-start(f32[128,128]{1,0:T(8,128)} %surface.3) | copy-start | bytes 196612
  0.7 7.2 %copy-start.2 = (f32[8,128,128]{2,1,0:T(8,128)S(1)}, f32[8,128,128]{2,1,0:T(8,128)}, u32[]{:S(2)}) copy-start(f32[8,128,128]{2,1,0:T(8,128)} %press.3) | copy-start | bytes 1572868
  0.7 7.2 %copy-start.1 = (f32[8,128,128]{2,1,0:T(8,128)S(1)}, f32[8,128,128]{2,1,0:T(8,128)}, u32[]{:S(2)}) copy-start(f32[8,128,128]{2,1,0:T(8,128)} %north.3) | copy-start | bytes 1572868
  0.7 7.2 %copy-start = (f32[8,128,128]{2,1,0:T(8,128)S(1)}, f32[8,128,128]{2,1,0:T(8,128)}, u32[]{:S(2)}) copy-start(f32[8,128,128]{2,1,0:T(8,128)} %east.3) | copy-start | bytes 1572868
  2.3 5.7 %copy-start.7 = (f32[8]{0:T(128)S(1)}, f32[8]{0:T(128)}, u32[]{:S(2)}) copy-start(f32[8]{0:T(128)} %thick.1) | copy-start | bytes 100
  2.3 8.2 %collective-permute-start.1 = (f32[12,8,128]{2,1,0:T(8,128)S(1)}, f32[12,8,128]{2,1,0:T(8,128)S(1)}, u32[]{:S(2)}, u32[]{:S(2)}) collective-permute-start(f32[12,8,128]{2,1,0:T(8,128)S(1)} %get-tuple-element.20.own_second), channel_id=1, source_target_pairs={{0,2},{2,0},{4,6},{6,4},{1,3},{3,1},{5,7},{7,5},{8,10},{10,8},{12,... | collective-permute-start | bytes 147464 | tf_op jit(solution)/shard_map/ppermute | solution.py:533
  5.4 5.9 %collective-permute-start = (f32[12,8,128]{2,1,0:T(8,128)S(1)}, f32[12,8,128]{2,1,0:T(8,128)S(1)}, u32[]{:S(2)}, u32[]{:S(2)}) collective-permute-start(f32[12,8,128]{2,1,0:T(8,128)S(1)} %get-tuple-element.19.after.own_first), channel_id=1, source_target_pairs={{2,4},{4,2},{6,0},{0,6},{3,5},{5,3},{7,1},{1,7},{10,12},{12,10},{1... | collective-permute-start | bytes 147464 | tf_op jit(solution)/shard_map/ppermute | solution.py:532
  11.4 5.3 %collective-permute-start.2 = (f32[144,128]{1,0:T(8,128)S(1)}, f32[144,128]{1,0:T(8,128)S(1)}, u32[]{:S(2)}, u32[]{:S(2)}) collective-permute-start(f32[144,128]{1,0:T(8,128)S(1)} %get-tuple-element.25.own_first), channel_id=1, source_target_pairs={{8,16},{16,8},{24,0},{0,24},{9,17},{17,9},{25,1},{1,25},{10,18},{1... | collective-permute-start | bytes 221192 | tf_op jit(solution)/shard_map/ppermute | solution.py:532
  13.9 4.4 %collective-permute-start.3 = (f32[144,128]{1,0:T(8,128)S(1)}, f32[144,128]{1,0:T(8,128)S(1)}, u32[]{:S(2)}, u32[]{:S(2)}) collective-permute-start(f32[144,128]{1,0:T(8,128)S(1)} %get-tuple-element.26.own_second), channel_id=1, source_target_pairs={{0,8},{8,0},{16,24},{24,16},{1,9},{9,1},{17,25},{25,17},{2,10},{10... | collective-permute-start | bytes 221192 | tf_op jit(solution)/shard_map/ppermute | solution.py:533
  19.0 1.9 %collective-permute-start.4 = (f32[6,144,128]{2,1,0:T(8,128)S(1)}, f32[6,144,128]{2,1,0:T(8,128)S(1)}, u32[]{:S(2)}, u32[]{:S(2)}) collective-permute-start(f32[6,144,128]{2,1,0:T(8,128)S(1)} %get-tuple-element.32.mine), channel_id=1, source_target_pairs={{1,0},{0,1},{3,2},{2,3},{5,4},{4,5},{7,6},{6,7},{9,8},{8,9},{11,10... | collective-permute-start | bytes 1327112 | tf_op jit(solution)/shard_map/ppermute | solution.py:606

commit v4 on v3

--- a/solution.py
+++ b/solution.py
@@ -14,6 +14,7 @@
 REACH = 2 * SUBSTEPS
 TIMESTEP = SUBSTEPS * COURANT
 CHUNK = 2 * REACH
+WAVE = 16
 
 F32 = jnp.float32
 
@@ -41,14 +42,6 @@
     return pltpu.roll(value, shift, axis=1)
 
 
-def repeated(count):
-    def run(body):
-        for step in range(count):
-            body(step)
-
-    return run
-
-
 def lane_ids(rows, cols):
     return lax.broadcasted_iota(jnp.int32, (rows, cols), 1)
 
@@ -94,14 +87,21 @@
     return low, turned(high, REACH + 1)
 
 
-def pack_columns(load, lines, like):
+def pack_columns(fields, lines, like):
     slot_of = lane_ids(*like) // REACH
     low, high = lines
     for index in range(FIELDS):
-        value = turned(load(index), (2 * index + 1) * REACH)
+        value = turned(fields[index], (2 * index + 1) * REACH)
         low = jnp.where(slot_of == 2 * index + 1, value, low)
         high = jnp.where(slot_of == 2 * index, value, high)
     return low, high
+
+
+def among(slot_of, slots):
+    found = slot_of == slots[0]
+    for slot in slots[1:]:
+        found = found | (slot_of == slot)
+    return found
 
 
 def shifted_rows(value, shift):
@@ -123,7 +123,7 @@
     return weight
 
 
-def core_chunk(size, thick, first_level, row, here, over, under, cor, write):
+def core_chunk(size, weights, first_level, row, here, over, under, cor, write):
     levels, cols = size.levels, size.cols
     count = 3 * levels
     cnt = here(count)
@@ -156,7 +156,7 @@
         if write is not None:
             write(0, k, wet_u + TIMESTEP * tend_e)
             write(1, k, wet_v + TIMESTEP * tend_n)
-        weight = thick[k]
+        weight = weights[k]
         parts = (weight * tend_e, weight * tend_n, weight * wet_u, weight * wet_v)
         parts += (jnp.where(wet, weight, 0.0),)
         totals = [total + part for total, part in zip(totals, parts)]
@@ -171,6 +171,11 @@
     first_level = (lax.axis_index("gz") * levels).astype(F32)
     copies = [pltpu.make_async_copy(thick_hbm, thick, sems.at[0])]
     ends = ((0, REACH), (rows - CHUNK, 4 * REACH))
+    for source, target in ends:
+        span = pl.ds(source, CHUNK)
+        for slot, array in enumerate((east, north, press)):
+            at = levels_of.at[pl.ds(slot * levels, levels), pl.ds(target, CHUNK), :]
+            copies.append(pltpu.make_async_copy(array.at[:, span, :], at, sems.at[len(copies)]))
     for part, (source, target) in enumerate(ends):
         span = pl.ds(source, CHUNK)
         for index, array in enumerate((land, bottom)):
@@ -179,15 +184,14 @@
         for index, array in enumerate((surface, coriolis)):
             at = flat.at[index, pl.ds(target, CHUNK), :]
             copies.append(pltpu.make_async_copy(array.at[span, :], at, sems.at[len(copies)]))
-        for slot, array in enumerate((east, north, press)):
-            at = levels_of.at[pl.ds(slot * levels, levels), pl.ds(target, CHUNK), :]
-            copies.append(pltpu.make_async_copy(array.at[:, span, :], at, sems.at[len(copies)]))
     for copy in copies:
         copy.start()
     for copy in copies:
         copy.wait()
     weights[0] = by_level(thick, row_ids(REACH, cols))
     weights[1] = by_level(thick, lane_ids(REACH, cols) % REACH)
+    for k in range(levels):
+        weights[2 + k] = jnp.full((REACH, cols), thick[k])
     for part, (_, target) in enumerate(ends):
         span = slice(part * CHUNK, part * CHUNK + CHUNK)
         count = whole[0, span, :].astype(F32) * whole[1, span, :].astype(F32)
@@ -228,10 +232,9 @@
 
 
 def tile_kernel(
-    size, thick, east, north, press, surface, land, bottom, coriolis, after,
+    size, weights, east, north, press, surface, land, bottom, coriolis,
     base, sums, statics, x_first, x_second,
 ):
-    del after
     levels, rows, cols = size.levels, size.rows, size.cols
     first_level = (lax.axis_index("gz") * levels).astype(F32)
     span = slice(REACH, REACH + rows)
@@ -241,6 +244,7 @@
     fields = (east, north, press)
     x_flag, _ = roles("gx")
     like = (CHUNK, cols)
+    weight = [jnp.concatenate([weights[2 + k]] * (CHUNK // REACH)) for k in range(levels)]
     for start in range(0, rows, CHUNK):
 
         def load(move):
@@ -262,13 +266,13 @@
             base[field, k, here, :] = value
 
         totals = core_chunk(
-            size, thick, first_level, start + row_ids(*like), load(0), load(1), load(-1),
+            size, weight, first_level, start + row_ids(*like), load(0), load(1), load(-1),
             statics[2, place, :], write,
         )
         for index, total in enumerate(totals):
             sums[index, place, :] = total
         totals += [statics[index, place, :] for index in range(3)]
-        low, high = pack_columns(lambda index: totals[index], pack_lines(size, load(0), like), like)
+        low, high = pack_columns(totals, pack_lines(size, load(0), like), like)
         x_first[place, :] = either(x_flag, high, low)
         x_second[place, :] = either(x_flag, low, high)
 
@@ -325,57 +329,50 @@
             statics[index, place, :] = blocks[block][SUMS + index]
         low_line = jnp.where((slot_of < 6) & (slot_of % 2 == 0), lines[block], 0.0)
         high_line = jnp.where((slot_of < 6) & (slot_of % 2 == 1), lines[block], 0.0)
-        low, high = pack_columns(
-            lambda index: blocks[block][index], (low_line, high_line), (REACH, cols)
-        )
+        low, high = pack_columns(blocks[block], (low_line, high_line), (REACH, cols))
         x_first[place, :] = either(x_flag, high, low)
         x_second[place, :] = either(x_flag, low, high)
 
 
 def column_kernel(
-    size, weights, own_first, own_second, got_first, got_second, sums_in,
-    sums, flux,
+    size, weights, own_first, own_second, got_first, got_second, ends, flux,
 ):
-    levels, wide, cols = size.levels, size.wide, size.cols
-    first_level = (lax.axis_index("gz") * levels).astype(F32)
+    wide, cols, half = size.wide, size.cols, size.half
+    first_level = (lax.axis_index("gz") * size.levels).astype(F32)
     high_first, east_first = roles("gx")
     west, east = split(east_first, got_first[...], got_second[...])
     low, high = split(high_first, own_first[...], own_second[...])
-    left, right = jnp.concatenate([west, high]), jnp.concatenate([low, east])
-    lane = lane_ids(2 * wide, cols)
+    lane = lane_ids(wide, cols)
     slot_of, place = lane // REACH, lane % REACH
-    change = turned(right, REACH) - left
+    end = REACH - 1
+    change = jnp.where(
+        lane < half, turned(low, REACH) - west, turned(turned(east, REACH) - high, half)
+    )
+    count = 2 * COUNT * REACH + end
+    counts = jnp.where(
+        lane == count, jnp.minimum(west, turned(low, -1)), jnp.minimum(turned(high, 1), east)
+    )
+    counts = gathered(counts, jnp.where(lane < half, count, count + 1))
     push = turned(change, -4 * REACH)
-    counts = jnp.minimum(
-        gathered(left, jnp.full_like(lane, (2 * COUNT + 1) * REACH - 1)),
-        gathered(right, jnp.full_like(lane, (2 * COUNT + 1) * REACH)),
-    )
-    wet = (place.astype(F32) + first_level < counts) & ((slot_of == 1) | (slot_of == 3))
+    eastward = among(slot_of % FIELDS, (1,))
+    wet = (place.astype(F32) + first_level < counts) & among(slot_of % FIELDS, (1, 3))
     change = jnp.where(wet, VISCOSITY * change, 0.0)
-    push = jnp.where(wet & (slot_of == 1), 0.5 * push, 0.0)
+    push = jnp.where(wet & eastward, 0.5 * push, 0.0)
     to_east, to_west = -change - push, change - push
-    flux[0], flux[1] = to_east[:wide], to_west[wide:]
-    weight = jnp.concatenate([weights[1]] * (2 * wide // REACH))
-    total = weight * to_east + turned(weight * to_west, size.half)
+    flux[0], flux[1] = to_east, to_west
+    weight = jnp.concatenate([weights[1]] * (wide // REACH))
+    total = weight * to_east + turned(weight * to_west, 4 * REACH)
     for shift in (1, 2, 4):
         total = total + turned(total, shift)
-    end = REACH - 1
-    at_west, at_east = total[:wide], total[wide:]
-    lane = lane_ids(wide, cols)
-    for index in range(2):
-        source = (2 * index + 1) * REACH + end
-        gain = jnp.where(lane == 0, turned(at_west, -source), 0.0)
-        gain = gain + jnp.where(
-            lane == cols - 1, turned(at_east, cols - 1 - size.half - source), 0.0
-        )
-        sums[index] = sums_in[index] + gain
-    slot_of, place = lane // REACH, lane % REACH
-    outer_west = (slot_of == 0) | (slot_of == 2)
-    outer_east = (slot_of == 1) | (slot_of == 3)
-    gain = jnp.where(
-        outer_west & (place == end), turned(at_west, -size.half - REACH), 0.0
-    ) + jnp.where(outer_east & (place == 0), turned(at_east, -end), 0.0)
-    sums[SUMS] = jnp.where(slot_of % 2 == 0, west, east) + gain
+    sources = [(2 * index + 1) * REACH + end for index in range(2)]
+    ends[1] = jnp.where(
+        among(lane, sources), total, turned(total, -half - 4 * REACH - 1)
+    )
+    outer_west = among(lane, (end, 2 * REACH + end))
+    outer_east = among(lane, (REACH, 3 * REACH))
+    gain = jnp.where(outer_west, turned(total, -5 * REACH), 0.0)
+    gain = gain + jnp.where(outer_east, turned(total, -half - end), 0.0)
+    ends[0] = jnp.where(slot_of % 2 == 0, west, east) + gain
 
 
 def finish_kernel(size, column_flux, row_flux, base_in, base):
@@ -390,7 +387,7 @@
                 source = (2 * field + 1) * REACH + k
                 gain = jnp.where(lane == 0, turned(west, -source), 0.0)
                 gain = gain + jnp.where(
-                    lane == cols - 1, turned(east, cols - 1 - source), 0.0
+                    lane == cols - 1, turned(east, size.half - 1 - source), 0.0
                 )
                 base[field, k, at, :] = base_in[field, k, at, :] + TIMESTEP * gain
     for field in range(2):
@@ -401,92 +398,118 @@
                 base[field, k, line, :] = base[field, k, line, :] + TIMESTEP * gain
 
 
+H, TE, TN = range(3)
+STEP, SLOPE, TURN, PUSH_E, PUSH_N = range(5)
+
+
+def coefficients(ocean, depth, coriolis, force_east, force_north):
+    step = 0.5 * COURANT * ocean
+    twice = COURANT * ocean
+    return step, step * depth, twice * coriolis, twice * force_east, twice * force_north
+
+
+def strip_field(size, strips, index):
+    lane = lane_ids(*strips.shape)
+    moved = turned(strips, (size.slots - 1 - 2 * index) * REACH)
+    return jnp.where((lane < REACH) | (lane >= size.cols - REACH), moved, 0.0)
+
+
+def blend_kernel(size, mine, other, statics, ends, state, fixed, drive):
+    here = slice(REACH, REACH + size.wide)
+    total = [mine[index] + other[index] for index in range(SUMS)]
+    ocean = jnp.where(statics[1] > 0, 1.0, 0.0)
+    values = coefficients(ocean, total[4], statics[2], total[0], total[1])
+    for index, value in enumerate(values):
+        fixed[0, index, here, :] = value
+    for index, value in ((TE, total[2]), (TN, total[3]), (H, ocean * statics[0])):
+        state[0, index, here, :] = value
+    drive[0] = total[2] + TIMESTEP * total[0]
+    drive[1] = total[3] + TIMESTEP * total[1]
+    drive[2] = total[4] + (1.0 - ocean)
+    strips = ends[0]
+    ocean = jnp.where(strip_field(size, strips, COUNT) > 0, 1.0, 0.0)
+    fixed[1, STEP, here, :] = 0.5 * COURANT * ocean
+    fixed[1, TURN, here, :] = COURANT * ocean * strip_field(size, strips, CORIOLIS)
+    state[1, H, here, :] = ocean * strip_field(size, strips, SURFACE)
+
+
 def surface_kernel(
-    size, base, statics, mine, other,
-    height_out, east_out, north_out,
-    state, fixed, drive, result, sems,
+    size, base, statics, mine, other, state_in, fixed_in, drive_in,
+    height_out, east_out, north_out, state, fixed, drive,
+    result, sems,
 ):
+    del state_in, fixed_in, drive_in
     levels, rows, cols, wide = size.levels, size.rows, size.cols, size.wide
     top = 2 * REACH
     first_level = (lax.axis_index("gz") * levels).astype(F32)
-    lane = lane_ids(CHUNK, cols)
-    H, TE, TN = range(3)
-    OC, DP, CO, FE, FN = range(5)
-    chunks = [REACH + at for at in range(0, wide, CHUNK)]
-
-    @repeated(wide // CHUNK)
-    def _(step):
-        place = pl.ds(step * CHUNK, CHUNK)
-        here = pl.ds(REACH + step * CHUNK, CHUNK)
-        total = [mine[index, place, :] + other[index, place, :] for index in range(SUMS)]
-        strip = mine[SUMS, place, :]
-        strip = jnp.where(
-            lane < 2 * SUMS * REACH, strip + other[SUMS, place, :], strip
+
+    here, lane = slice(REACH, REACH + wide), lane_ids(wide, cols)
+    strips = mine[0] + other[0]
+    force_east, force_north, sum_east, sum_north, depth = (
+        strip_field(size, strips, index) for index in range(SUMS)
+    )
+    step = fixed[1, STEP, here, :]
+    fixed[1, SLOPE, here, :] = step * depth
+    fixed[1, PUSH_E, here, :] = 2.0 * step * force_east
+    fixed[1, PUSH_N, here, :] = 2.0 * step * force_north
+    state[1, TE, here, :] = sum_east
+    state[1, TN, here, :] = sum_north
+    gains = mine[1] + other[1]
+    for index, push in ((0, PUSH_E), (1, PUSH_N)):
+        gain = turned(gains, -((2 * index + 1) * REACH + REACH - 1))
+        gain = jnp.where((lane == 0) | (lane == cols - 1), gain, 0.0)
+        fixed[0, push, here, :] = (
+            fixed[0, push, here, :] + 2.0 * fixed[0, STEP, here, :] * gain
         )
-
-        def outer(index):
-            moved = turned(strip, (size.slots - 1 - 2 * index) * REACH)
-            return jnp.where((lane < REACH) | (lane >= cols - REACH), moved, 0.0)
-
-        fixed[0, FE, here, :] = total[0]
-        fixed[0, FN, here, :] = total[1]
-        state[0, TE, here, :] = total[2]
-        state[0, TN, here, :] = total[3]
-        drive[0, place, :] = total[2] + TIMESTEP * total[0]
-        drive[1, place, :] = total[3] + TIMESTEP * total[1]
-        fixed[0, DP, here, :] = total[4]
-        fixed[1, FE, here, :] = outer(0)
-        fixed[1, FN, here, :] = outer(1)
-        state[1, TE, here, :] = outer(2)
-        state[1, TN, here, :] = outer(3)
-        fixed[1, DP, here, :] = outer(4)
-        state[0, H, here, :] = statics[0, place, :]
-        state[1, H, here, :] = outer(SURFACE)
-        fixed[0, OC, here, :] = jnp.where(statics[1, place, :] > 0, 1.0, 0.0)
-        fixed[1, OC, here, :] = jnp.where(outer(COUNT) > 0, 1.0, 0.0)
-        fixed[0, CO, here, :] = statics[2, place, :]
-        fixed[1, CO, here, :] = outer(CORIOLIS)
+        drive[index] = drive[index] + TIMESTEP * gain
+    lane = lane_ids(WAVE, cols)
+    at_high, at_low = lane == cols - 1, lane == 0
 
     def difference_x(field, here):
         inside, outside = state[0, field, here, :], state[1, field, here, :]
         in_e, out_e = turned(inside, -1), turned(outside, -1)
         in_w, out_w = turned(inside, 1), turned(outside, 1)
-        at_high, at_low = lane == cols - 1, lane == 0
         return (
-            0.5 * (jnp.where(at_high, out_e, in_e) - jnp.where(at_low, out_w, in_w)),
-            0.5 * (jnp.where(at_high, in_e, out_e) - jnp.where(at_low, in_w, out_w)),
+            jnp.where(at_high, out_e, in_e) - jnp.where(at_low, out_w, in_w),
+            jnp.where(at_high, in_e, out_e) - jnp.where(at_low, in_w, out_w),
         )
 
     def difference_y(part, field, start):
-        above = state[part, field, start + 1 : start + 1 + CHUNK, :]
-        return 0.5 * (above - state[part, field, start - 1 : start - 1 + CHUNK, :])
+        above = state[part, field, start + 1 : start + 1 + WAVE, :]
+        return above - state[part, field, start - 1 : start - 1 + WAVE, :]
+
+    def height_part(start):
+        here = slice(start, start + WAVE)
+        across = difference_x(TE, here)
+        for part in range(2):
+            spread = across[part] + difference_y(part, TN, start)
+            state[part, H, here, :] = (
+                state[part, H, here, :] - fixed[part, STEP, here, :] * spread
+            )
+
+    def transport_part(start):
+        here = slice(start, start + WAVE)
+        across = difference_x(H, here)
+        for part in range(2):
+            slope_y = difference_y(part, H, start)
+            te, tn = state[part, TE, here, :], state[part, TN, here, :]
+            slope, turn, push_e, push_n = (
+                fixed[part, index, here, :] for index in (SLOPE, TURN, PUSH_E, PUSH_N)
+            )
+            state[part, TE, here, :] = te + (turn * tn + push_e - slope * across[part])
+            state[part, TN, here, :] = tn + (push_n - turn * te - slope * slope_y)
 
     for _ in range(SUBSTEPS):
-        for start in chunks:
-            here = slice(start, start + CHUNK)
-            across = difference_x(TE, here)
-            for part in range(2):
-                spread = across[part] + difference_y(part, TN, start)
-                height = state[part, H, here, :] - COURANT * spread
-                state[part, H, here, :] = fixed[part, OC, here, :] * height
-        for start in chunks:
-            here = slice(start, start + CHUNK)
-            across = difference_x(H, here)
-            for part in range(2):
-                slope_y = difference_y(part, H, start)
-                te, tn = state[part, TE, here, :], state[part, TN, here, :]
-                oc, dp, co, fe, fn = (fixed[part, index, here, :] for index in range(5))
-                state[part, TE, here, :] = oc * (
-                    te + COURANT * (-dp * across[part] + co * tn + fe)
-                )
-                state[part, TN, here, :] = oc * (tn + COURANT * (-dp * slope_y - co * te + fn))
+        for part in (height_part, transport_part):
+            for start in range(REACH, REACH + wide, WAVE):
+                part(start)
 
     height_copy = pltpu.make_async_copy(
         state.at[0, H, pl.ds(top, rows), :], height_out, sems.at[0]
     )
     height_copy.start()
     inner = slice(top, top + rows)
-    floor_depth = fixed[0, DP, inner, :] + (1.0 - fixed[0, OC, inner, :])
+    floor_depth = drive[2, REACH : REACH + rows, :]
     for index, field in enumerate((TE, TN)):
         gain = state[0, field, inner, :] - drive[index, REACH : REACH + rows, :]
         drive[index, REACH : REACH + rows, :] = gain / floor_depth
@@ -553,7 +576,7 @@
         size,
         [HBM] * 8,
         [VMEM] * 3,
-        [side, side, shaped(2, REACH, cols)],
+        [side, side, shaped(2 + levels, REACH, cols)],
         [
             pltpu.SMEM((levels,), F32),
             pltpu.VMEM((3 * levels + 1, 7 * REACH, cols), F32),
@@ -563,22 +586,23 @@
         ],
     )(*inputs)
     got_y = swapped("gy", *own_y)
+    packed = shaped(wide, cols)
     base, sums, statics, x_first, x_second = call(
         tile_kernel,
         size,
-        [SMEM] + [VMEM] * 8,
+        [VMEM] * 8,
         [VMEM] * 5,
         [
             shaped(2, levels, rows, cols),
-            shaped(SUMS + 1, wide, cols),
+            shaped(SUMS, wide, cols),
             shaped(3, wide, cols),
-            shaped(wide, cols),
-            shaped(wide, cols),
+            packed,
+            packed,
         ],
         flops=10**7,
     )(
-        level_thick, layer_east, layer_north, layer_press,
-        surface, land_sea, bottom_level, coriolis, own_y[0],
+        weights, layer_east, layer_north, layer_press,
+        surface, land_sea, bottom_level, coriolis,
     )
     sums, statics, x_first, x_second, row_flux = call(
         row_kernel,
@@ -586,24 +610,32 @@
         [VMEM] * 9,
         [VMEM] * 5,
         [
-            shaped(SUMS + 1, wide, cols),
+            shaped(SUMS, wide, cols),
             shaped(3, wide, cols),
-            shaped(wide, cols),
-            shaped(wide, cols),
+            packed,
+            packed,
             shaped(2, 2, levels, cols),
         ],
         aliases={5: 0, 6: 1, 7: 2, 8: 3},
     )(weights, *own_y, *got_y, sums, statics, x_first, x_second)
     got_x = swapped("gx", x_first, x_second)
-    sums, column_flux = call(
+    other_sums = lax.ppermute(sums, "gz", pairing("gz")[0])
+    scratch = [
+        shaped(2, 3, wide + 2 * REACH, cols),
+        shaped(2, 5, wide + 2 * REACH, cols),
+        shaped(3, wide, cols),
+    ]
+    ends, column_flux = call(
         column_kernel,
         size,
-        [VMEM] * 6,
+        [VMEM] * 5,
         [VMEM] * 2,
-        [shaped(SUMS + 1, wide, cols), shaped(2, wide, cols)],
-        aliases={5: 0},
-    )(weights, x_first, x_second, *got_x, sums)
-    others = lax.ppermute(sums, "gz", pairing("gz")[0])
+        [shaped(2, wide, cols), shaped(2, wide, cols)],
+    )(weights, x_first, x_second, *got_x)
+    other_ends = lax.ppermute(ends, "gz", pairing("gz")[0])
+    blended = call(blend_kernel, size, [VMEM] * 4, [VMEM] * 3, scratch, flops=10**6)(
+        sums, other_sums, statics, ends
+    )
     base = call(
         finish_kernel,
         size,
@@ -613,20 +645,19 @@
         aliases={2: 0},
         flops=10**7,
     )(column_flux, row_flux, base)[0]
-    height, east_next, north_next = call(
+    layers = shaped(levels, rows, cols)
+    height, east_next, north_next, *_ = call(
         surface_kernel,
         size,
-        [VMEM] * 4,
-        [HBM] * 3,
-        [shaped(rows, cols), shaped(levels, rows, cols), shaped(levels, rows, cols)],
+        [VMEM] * 7,
+        [HBM] * 3 + [VMEM] * 3,
+        [shaped(rows, cols), layers, layers, *scratch],
         [
-            pltpu.VMEM((2, 3, wide + 2 * REACH, cols), F32),
-            pltpu.VMEM((2, 5, wide + 2 * REACH, cols), F32),
-            pltpu.VMEM((2, wide, cols), F32),
             pltpu.VMEM((2, levels, rows, cols), F32),
             pltpu.SemaphoreType.DMA((1 + 2 * levels,)),
         ],
-    )(base, statics, sums, others)
+        aliases={4: 3, 5: 4, 6: 5},
+    )(base, statics, ends, other_ends, *blended)
     return (height, east_next, north_next)
 
 

time: 23.2 us -> 23.2 us (level)
  waiting for transfers between devices: 5.62 us -> 6.56 us
  Pallas kernels: 7.85 us -> 7.34 us
  starting transfers between devices: 8.71 us -> 8.33 us
    ppermute x2, starting transfers between devices: 3.65 us -> 0.54 us  [swapped(): second = lax.ppermute(second, axis, pairs[1])]
    ppermute x2, starting transfers between devices: 4.99 us -> 7.65 us  [swapped(): first = lax.ppermute(first, axis, pairs[0])]
    ppermute x2, waiting for transfers between devices: 1.55 us -> 3.08 us  [swapped(): second = lax.ppermute(second, axis, pairs[1])]
    ppermute x1 -> x2, waiting for transfers between devices: 0.98 us -> 0.4 us  [the longest x1 0.4 us: on_device(): other_ends = lax.ppermute(ends, 'gz', pairing('gz')[0])]
    pallas_call x5 -> x6, Pallas kernels: 7.06 us -> 6.55 us  [the longest x1 2.15 us: on_device(): call(surface_kernel, size, [VMEM] * 7, [HBM] * 3 + [VMEM] * 3, [shaped(ro...]
  transfers between devices with their start and end apart: 5 -> 6, of which waited for: 4 -> 5; matrix products, arithmetic and copies ran while one was open for 0% -> 0% of each run, Pallas kernels for 14% -> 15%
where the time goes in v4:
time: 23.2 us; the launch traced here: 23.1 us
  starting transfers between devices  8.33 us (36%)
  Pallas kernels  7.34 us (32%)
  waiting for transfers between devices  6.56 us (28%)
  between operations  0.81 us (3%)
    ppermute x2, starting transfers between devices, swapped(): first = lax.ppermute(first, axis, pairs[0])  7.65 us
    ppermute x2, waiting for transfers between devices, swapped(): second = lax.ppermute(second, axis, pairs[1])  3.08 us
    ppermute x2, waiting for transfers between devices, swapped(): first = lax.ppermute(first, axis, pairs[0])  3.08 us
    pallas_call x1, Pallas kernels, on_device(): call(surface_kernel, size, [VMEM] * 7, [HBM] * 3 + [VMEM] * 3, [shaped(ro...  2.15 us
    pallas_call x1, Pallas kernels, on_device(): call(tile_kernel, size, [VMEM] * 8, [VMEM] * 5, [shaped(2, levels, rows,...  2.02 us
    pallas_call x1, Pallas kernels, on_device(): call(edge_kernel, size, [HBM] * 8, [VMEM] * 3, [side, side, shaped(2 + le...  1.51 us
    pallas_call x1, Pallas kernels, on_device(): call(finish_kernel, size, [VMEM] * 3, [VMEM], [shaped(2, levels, rows, co...  0.79 us
    pallas_call x1, Pallas kernels, on_device(): call(column_kernel, size, [VMEM] * 5, [VMEM] * 2, [shaped(2, wide, cols),...  0.62 us
  transfers between devices with their start and end apart: 6, of which 5 were waited for; matrix products, arithmetic and copies ran while one was open for 0% of the time, Pallas kernels for 15%

profile of v4, /device:TPU:0, one launch (start us, length us, event | category | flops | bytes accessed | tf_op | source)
XLA Modules:
  0.0 23.1 jit_solution(344825566050824612)
XLA Ops:
  0.6 0.0 copy-start.6
  0.6 0.0 copy-start.5
  0.7 0.0 copy-start.4
  0.7 0.0 copy-start.3
  0.7 0.0 copy-start.2
  0.7 0.0 copy-start.1
  0.7 0.0 copy-start
  0.7 1.5 %shard_map.103 = (f32[12,8,128]{2,1,0:T(8,128)S(1)}, f32[12,8,128]{2,1,0:T(8,128)S(1)}, f32[10,8,128]{2,1,0:T(8,128)S(1)}) custom-call(f32[8]{0:T(128)} %thick_hbm.1, f32[8,128,128]{2,1,0:T(8,128)} %east.3, f32[8,128,128]{2,1,0:T(8,128)} %north.3, f32[8,128,128]{2,1,0:T(8,128)} %press.3, f32[128,128]{1,0:T(8,128)} %surface.3, s32[128,128]{1,0:T(8,128)} %land.3, ...), custom_call_target="tpu_custom_call" | custom-call | tf_op jit(solution)/shard_map/pallas_call | solution.py:574
  2.2 5.1 %collective-permute-start = (f32[12,8,128]{2,1,0:T(8,128)S(1)}, f32[12,8,128]{2,1,0:T(8,128)S(1)}, u32[]{:S(2)}, u32[]{:S(2)}) collective-permute-start(f32[12,8,128]{2,1,0:T(8,128)S(1)} %get-tuple-element.25.own_first), channel_id=1, source_target_pairs={{2,4},{4,2},{6,0},{0,6},{3,5},{5,3},{7,1},{1,7},{10,12},{12,10},{1... | collective-permute-start | bytes 147464 | tf_op jit(solution)/shard_map/ppermute | solution.py:555
  7.4 0.0 collective-permute-start.1
  7.4 0.0 copy-done.6
  7.4 0.0 copy-done.5
  7.4 0.0 copy-done.4
  7.4 0.0 copy-done.3
  7.4 0.0 copy-done.2
  7.4 0.0 copy-done.1
  7.4 2.0 %shard_map.104 = (f32[2,8,128,128]{3,2,1,0:T(8,128)S(1)}, f32[5,144,128]{2,1,0:T(8,128)S(1)}, f32[3,144,128]{2,1,0:T(8,128)S(1)}, f32[144,128]{1,0:T(8,128)S(1)}, f32[144,128]{1,0:T(8,128)S(1)}) custom-call(f32[10,8,128]{2,1,0:T(8,128)S(1)} %get-tuple-element.24.weights, f32[8,128,128]{2,1,0:T(8,128)S(1)} %copy-done, f32[8,128,128]{2,1,0:T(8,128)S(1)} %copy-done.1, ...), custom_call_target="tpu_custom_call" | custom-call | flops 10000000 | tf_op jit(solution)/shard_map/pallas_call | solution.py:590
  9.5 0.2 collective-permute-done.got_first
  9.6 1.8 %collective-permute-done.1.got_second = f32[12,8,128]{2,1,0:T(8,128)S(1)} collective-permute-done((f32[12,8,128]{2,1,0:T(8,128)S(1)}, f32[12,8,128]{2,1,0:T(8,128)S(1)}, u32[]{:S(2)}, u32[]{:S(2)}) %collective-permute-start.1) | collective-permute-done | bytes 49184 | tf_op jit(solution)/shard_map/ppermute | solution.py:556
  11.5 0.1 shard_map.105
  11.6 0.1 collective-permute-start.5
  11.7 2.5 %collective-permute-start.2 = (f32[144,128]{1,0:T(8,128)S(1)}, f32[144,128]{1,0:T(8,128)S(1)}, u32[]{:S(2)}, u32[]{:S(2)}) collective-permute-start(f32[144,128]{1,0:T(8,128)S(1)} %get-tuple-element.31.own_first), channel_id=1, source_target_pairs={{8,16},{16,8},{24,0},{0,24},{9,17},{17,9},{25,1},{1,25},{10,18},{1... | collective-permute-start | bytes 221192 | tf_op jit(solution)/shard_map/ppermute | solution.py:555
  14.2 0.5 %collective-permute-start.3 = (f32[144,128]{1,0:T(8,128)S(1)}, f32[144,128]{1,0:T(8,128)S(1)}, u32[]{:S(2)}, u32[]{:S(2)}) collective-permute-start(f32[144,128]{1,0:T(8,128)S(1)} %get-tuple-element.32.own_second), channel_id=1, source_target_pairs={{0,8},{8,0},{16,24},{24,16},{1,9},{9,1},{17,25},{25,17},{2,10},{10... | collective-permute-start | bytes 221192 | tf_op jit(solution)/shard_map/ppermute | solution.py:556
  14.7 2.9 %collective-permute-done.2.got_first = f32[144,128]{1,0:T(8,128)S(1)} collective-permute-done((f32[144,128]{1,0:T(8,128)S(1)}, f32[144,128]{1,0:T(8,128)S(1)}, u32[]{:S(2)}, u32[]{:S(2)}) %collective-permute-start.2) | collective-permute-done | bytes 73760 | tf_op jit(solution)/shard_map/ppermute | solution.py:555
  17.6 1.3 %collective-permute-done.3.got_second = f32[144,128]{1,0:T(8,128)S(1)} collective-permute-done((f32[144,128]{1,0:T(8,128)S(1)}, f32[144,128]{1,0:T(8,128)S(1)}, u32[]{:S(2)}, u32[]{:S(2)}) %collective-permute-start.3) | collective-permute-done | bytes 73760 | tf_op jit(solution)/shard_map/ppermute | solution.py:556
  18.9 0.6 %shard_map.106 = (f32[2,144,128]{2,1,0:T(8,128)S(1)}, f32[2,144,128]{2,1,0:T(8,128)S(1)}) custom-call(f32[10,8,128]{2,1,0:T(8,128)S(1)} %get-tuple-element.24.weights, f32[144,128]{1,0:T(8,128)S(1)} %get-tuple-element.31.own_first, f32[144,128]{1,0:T(8,128)S(1)} %get-tuple-element.32.own_second, f32[144,128]{1,0:T(8,128)S(1)} %collective-permute-done.2.got_first, ...), custom_call_target="tpu_custom_call" | custom-call | tf_op jit(solution)/shard_map/pallas_call | solution.py:628
  19.5 0.1 collective-permute-start.4
  19.6 0.8 %shard_map.107.base = f32[2,8,128,128]{3,2,1,0:T(8,128)S(1)} custom-call(f32[2,144,128]{2,1,0:T(8,128)S(1)} %get-tuple-element.33.column_flux, f32[2,2,8,128]{3,2,1,0:T(8,128)S(1)} %get-tuple-element.34.row_flux, f32[2,8,128,128]{3,2,1,0:T(8,128)S(1)} %get-tuple-element.35.base_in), custom_call_target="tpu_custom_call", output_to_operand_aliasing={{}: (2, {})} | custom-call | flops 10000000 | tf_op jit(solution)/shard_map/pallas_call | solution.py:639
  20.4 0.0 collective-permute-done.5.other
  20.4 0.1 shard_map.108
  20.5 0.4 %collective-permute-done.4.other = f32[2,144,128]{2,1,0:T(8,128)S(1)} collective-permute-done((f32[2,144,128]{2,1,0:T(8,128)S(1)}, f32[2,144,128]{2,1,0:T(8,128)S(1)}, u32[]{:S(2)}, u32[]{:S(2)}) %collective-permute-start.4) | collective-permute-done | bytes 147488 | tf_op jit(solution)/shard_map/ppermute | solution.py:635
  20.9 2.1 %shard_map.109 = (f32[128,128]{1,0:T(8,128)}, f32[8,128,128]{2,1,0:T(8,128)}, f32[8,128,128]{2,1,0:T(8,128)}, f32[2,3,160,128]{3,2,1,0:T(8,128)S(1)}, f32[2,5,16...) custom-call(f32[2,8,128,128]{3,2,1,0:T(8,128)S(1)} %shard_map.107.bas, ...), custom_call_target="tpu_custom_call", output_to_operand_aliasing={{3}: (4, {}), {4}: (5, {}), {5}: (6, {})} | custom-call | tf_op jit(solution)/shard_map/pallas_call | solution.py:649
  (1 shorter events, 0.0 us)
Async XLA Ops:
  0.6 6.7 %copy-start.6 = (f32[128,128]{1,0:T(8,128)S(1)}, f32[128,128]{1,0:T(8,128)}, u32[]{:S(2)}) copy-start(f32[128,128]{1,0:T(8,128)} %coriolis.3) | copy-start | bytes 196612
  0.6 6.7 %copy-start.5 = (s32[128,128]{1,0:T(8,128)S(1)}, s32[128,128]{1,0:T(8,128)}, u32[]{:S(2)}) copy-start(s32[128,128]{1,0:T(8,128)} %bottom.3) | copy-start | bytes 196612
  0.7 6.7 %copy-start.4 = (s32[128,128]{1,0:T(8,128)S(1)}, s32[128,128]{1,0:T(8,128)}, u32[]{:S(2)}) copy-start(s32[128,128]{1,0:T(8,128)} %land.3) | copy-start | bytes 196612
  0.7 6.7 %copy-start.3 = (f32[128,128]{1,0:T(8,128)S(1)}, f32[128,128]{1,0:T(8,128)}, u32[]{:S(2)}) copy-start(f32[128,128]{1,0:T(8,128)} %surface.3) | copy-start | bytes 196612
  0.7 6.7 %copy-start.2 = (f32[8,128,128]{2,1,0:T(8,128)S(1)}, f32[8,128,128]{2,1,0:T(8,128)}, u32[]{:S(2)}) copy-start(f32[8,128,128]{2,1,0:T(8,128)} %press.3) | copy-start | bytes 1572868
  0.7 6.7 %copy-start.1 = (f32[8,128,128]{2,1,0:T(8,128)S(1)}, f32[8,128,128]{2,1,0:T(8,128)}, u32[]{:S(2)}) copy-start(f32[8,128,128]{2,1,0:T(8,128)} %north.3) | copy-start | bytes 1572868
  0.7 6.7 %copy-start = (f32[8,128,128]{2,1,0:T(8,128)S(1)}, f32[8,128,128]{2,1,0:T(8,128)}, u32[]{:S(2)}) copy-start(f32[8,128,128]{2,1,0:T(8,128)} %east.3) | copy-start | bytes 1572868
  2.2 7.4 %collective-permute-start = (f32[12,8,128]{2,1,0:T(8,128)S(1)}, f32[12,8,128]{2,1,0:T(8,128)S(1)}, u32[]{:S(2)}, u32[]{:S(2)}) collective-permute-start(f32[12,8,128]{2,1,0:T(8,128)S(1)} %get-tuple-element.25.own_first), channel_id=1, source_target_pairs={{2,4},{4,2},{6,0},{0,6},{3,5},{5,3},{7,1},{1,7},{10,12},{12,10},{1... | collective-permute-start | bytes 147464 | tf_op jit(solution)/shard_map/ppermute | solution.py:555
  7.4 4.1 %collective-permute-start.1 = (f32[12,8,128]{2,1,0:T(8,128)S(1)}, f32[12,8,128]{2,1,0:T(8,128)S(1)}, u32[]{:S(2)}, u32[]{:S(2)}) collective-permute-start(f32[12,8,128]{2,1,0:T(8,128)S(1)} %get-tuple-element.26.own_second), channel_id=1, source_target_pairs={{0,2},{2,0},{4,6},{6,4},{1,3},{3,1},{5,7},{7,5},{8,10},{10,8},{12,... | collective-permute-start | bytes 147464 | tf_op jit(solution)/shard_map/ppermute | solution.py:556
  11.6 8.8 %collective-permute-start.5 = (f32[5,144,128]{2,1,0:T(8,128)S(1)}, f32[5,144,128]{2,1,0:T(8,128)S(1)}, u32[]{:S(2)}, u32[]{:S(2)}) collective-permute-start(f32[5,144,128]{2,1,0:T(8,128)S(1)} %get-tuple-element.38.mine), channel_id=1, source_target_pairs={{1,0},{0,1},{3,2},{2,3},{5,4},{4,5},{7,6},{6,7},{9,8},{8,9},{11,10... | collective-permute-start | bytes 1105928 | tf_op jit(solution)/shard_map/ppermute | solution.py:622
  11.7 5.9 %collective-permute-start.2 = (f32[144,128]{1,0:T(8,128)S(1)}, f32[144,128]{1,0:T(8,128)S(1)}, u32[]{:S(2)}, u32[]{:S(2)}) collective-permute-start(f32[144,128]{1,0:T(8,128)S(1)} %get-tuple-element.31.own_first), channel_id=1, source_target_pairs={{8,16},{16,8},{24,0},{0,24},{9,17},{17,9},{25,1},{1,25},{10,18},{1... | collective-permute-start | bytes 221192 | tf_op jit(solution)/shard_map/ppermute | solution.py:555
  14.2 4.7 %collective-permute-start.3 = (f32[144,128]{1,0:T(8,128)S(1)}, f32[144,128]{1,0:T(8,128)S(1)}, u32[]{:S(2)}, u32[]{:S(2)}) collective-permute-start(f32[144,128]{1,0:T(8,128)S(1)} %get-tuple-element.32.own_second), channel_id=1, source_target_pairs={{0,8},{8,0},{16,24},{24,16},{1,9},{9,1},{17,25},{25,17},{2,10},{10... | collective-permute-start | bytes 221192 | tf_op jit(solution)/shard_map/ppermute | solution.py:556
  19.5 1.4 %collective-permute-start.4 = (f32[2,144,128]{2,1,0:T(8,128)S(1)}, f32[2,144,128]{2,1,0:T(8,128)S(1)}, u32[]{:S(2)}, u32[]{:S(2)}) collective-permute-start(f32[2,144,128]{2,1,0:T(8,128)S(1)} %get-tuple-element.37.ends.mine), channel_id=1, source_target_pairs={{1,0},{0,1},{3,2},{2,3},{5,4},{4,5},{7,6},{6,7},{9,8},{8,9},{11,10... | collective-permute-start | bytes 442376 | tf_op jit(solution)/shard_map/ppermute | solution.py:635

commit v5 on v4

--- a/solution.py
+++ b/solution.py
@@ -19,6 +19,8 @@
 F32 = jnp.float32
 
 FIELDS = 8
+GAINS = 95
+BLOCKS = 2
 SURFACE, COUNT, CORIOLIS = 5, 6, 7
 SUMS = 5
 
@@ -233,19 +235,43 @@
 
 def tile_kernel(
     size, weights, east, north, press, surface, land, bottom, coriolis,
-    base, sums, statics, x_first, x_second,
+    base, sums, statics, x_first, x_second, tile, whole, sems,
 ):
     levels, rows, cols = size.levels, size.rows, size.cols
     first_level = (lax.axis_index("gz") * levels).astype(F32)
-    span = slice(REACH, REACH + rows)
-    statics[0, span, :] = surface[...]
-    statics[1, span, :] = land[...].astype(F32) * bottom[...].astype(F32)
-    statics[2, span, :] = coriolis[...]
-    fields = (east, north, press)
+    span = pl.ds(REACH, rows)
+    flat = [
+        pltpu.make_async_copy(land, whole.at[0], sems.at[0]),
+        pltpu.make_async_copy(bottom, whole.at[1], sems.at[1]),
+        pltpu.make_async_copy(surface, statics.at[0, span, :], sems.at[2]),
+        pltpu.make_async_copy(coriolis, statics.at[2, span, :], sems.at[3]),
+    ]
+    for copy in flat:
+        copy.start()
+    deep = rows // BLOCKS
+    blocks = []
+    for block in range(BLOCKS):
+        blocks.append([])
+        for slot, field in enumerate((east, north, press)):
+            at = pl.ds(block * deep, deep)
+            copy = pltpu.make_async_copy(
+                field.at[:, at, :], tile.at[slot, :, at, :], sems.at[4 + 3 * block + slot]
+            )
+            copy.start()
+            blocks[-1].append(copy)
+    for copy in flat:
+        copy.wait()
+    statics[1, REACH : REACH + rows, :] = whole[0].astype(F32) * whole[1].astype(F32)
+    fields = [tile.at[slot] for slot in range(3)]
+    arrived = 0
     x_flag, _ = roles("gx")
     like = (CHUNK, cols)
     weight = [jnp.concatenate([weights[2 + k]] * (CHUNK // REACH)) for k in range(levels)]
     for start in range(0, rows, CHUNK):
+        while arrived < BLOCKS and arrived * deep < min(start + CHUNK + 1, rows):
+            for copy in blocks[arrived]:
+                copy.wait()
+            arrived += 1
 
         def load(move):
             at = start + move
@@ -335,7 +361,7 @@
 
 
 def column_kernel(
-    size, weights, own_first, own_second, got_first, got_second, ends, flux,
+    size, weights, own_first, own_second, got_first, got_second, ends, strips, flux,
 ):
     wide, cols, half = size.wide, size.cols, size.half
     first_level = (lax.axis_index("gz") * size.levels).astype(F32)
@@ -364,15 +390,16 @@
     total = weight * to_east + turned(weight * to_west, 4 * REACH)
     for shift in (1, 2, 4):
         total = total + turned(total, shift)
-    sources = [(2 * index + 1) * REACH + end for index in range(2)]
-    ends[1] = jnp.where(
-        among(lane, sources), total, turned(total, -half - 4 * REACH - 1)
-    )
     outer_west = among(lane, (end, 2 * REACH + end))
     outer_east = among(lane, (REACH, 3 * REACH))
     gain = jnp.where(outer_west, turned(total, -5 * REACH), 0.0)
     gain = gain + jnp.where(outer_east, turned(total, -half - end), 0.0)
-    ends[0] = jnp.where(slot_of % 2 == 0, west, east) + gain
+    strips[...] = jnp.where(slot_of % 2 == 0, west, east)
+    for_west = among(lane, [GAINS + 2 * index * REACH for index in range(2)])
+    forces = jnp.where(
+        for_west, turned(total, GAINS - REACH - end), turned(total, GAINS - half - 6 * REACH)
+    )
+    ends[...] = jnp.where(lane < 2 * SUMS * REACH, strips[...] + gain, forces)
 
 
 def finish_kernel(size, column_flux, row_flux, base_in, base):
@@ -414,7 +441,7 @@
     return jnp.where((lane < REACH) | (lane >= size.cols - REACH), moved, 0.0)
 
 
-def blend_kernel(size, mine, other, statics, ends, state, fixed, drive):
+def blend_kernel(size, mine, other, statics, strips, state, fixed, drive):
     here = slice(REACH, REACH + size.wide)
     total = [mine[index] + other[index] for index in range(SUMS)]
     ocean = jnp.where(statics[1] > 0, 1.0, 0.0)
@@ -426,7 +453,7 @@
     drive[0] = total[2] + TIMESTEP * total[0]
     drive[1] = total[3] + TIMESTEP * total[1]
     drive[2] = total[4] + (1.0 - ocean)
-    strips = ends[0]
+    strips = strips[...]
     ocean = jnp.where(strip_field(size, strips, COUNT) > 0, 1.0, 0.0)
     fixed[1, STEP, here, :] = 0.5 * COURANT * ocean
     fixed[1, TURN, here, :] = COURANT * ocean * strip_field(size, strips, CORIOLIS)
@@ -444,7 +471,7 @@
     first_level = (lax.axis_index("gz") * levels).astype(F32)
 
     here, lane = slice(REACH, REACH + wide), lane_ids(wide, cols)
-    strips = mine[0] + other[0]
+    strips = mine[...] + other[...]
     force_east, force_north, sum_east, sum_north, depth = (
         strip_field(size, strips, index) for index in range(SUMS)
     )
@@ -454,9 +481,8 @@
     fixed[1, PUSH_N, here, :] = 2.0 * step * force_north
     state[1, TE, here, :] = sum_east
     state[1, TN, here, :] = sum_north
-    gains = mine[1] + other[1]
     for index, push in ((0, PUSH_E), (1, PUSH_N)):
-        gain = turned(gains, -((2 * index + 1) * REACH + REACH - 1))
+        gain = turned(strips, -GAINS - 2 * index * REACH)
         gain = jnp.where((lane == 0) | (lane == cols - 1), gain, 0.0)
         fixed[0, push, here, :] = (
             fixed[0, push, here, :] + 2.0 * fixed[0, STEP, here, :] * gain
@@ -590,7 +616,7 @@
     base, sums, statics, x_first, x_second = call(
         tile_kernel,
         size,
-        [VMEM] * 8,
+        [VMEM] + [HBM] * 7,
         [VMEM] * 5,
         [
             shaped(2, levels, rows, cols),
@@ -599,11 +625,13 @@
             packed,
             packed,
         ],
+        [
+            pltpu.VMEM((3, levels, rows, cols), F32),
+            pltpu.VMEM((2, rows, cols), jnp.int32),
+            pltpu.SemaphoreType.DMA((4 + 3 * BLOCKS,)),
+        ],
         flops=10**7,
-    )(
-        weights, layer_east, layer_north, layer_press,
-        surface, land_sea, bottom_level, coriolis,
-    )
+    )(weights, *inputs[1:])
     sums, statics, x_first, x_second, row_flux = call(
         row_kernel,
         size,
@@ -625,16 +653,16 @@
         shaped(2, 5, wide + 2 * REACH, cols),
         shaped(3, wide, cols),
     ]
-    ends, column_flux = call(
+    ends, strips, column_flux = call(
         column_kernel,
         size,
         [VMEM] * 5,
-        [VMEM] * 2,
-        [shaped(2, wide, cols), shaped(2, wide, cols)],
+        [VMEM] * 3,
+        [packed, packed, shaped(2, wide, cols)],
     )(weights, x_first, x_second, *got_x)
     other_ends = lax.ppermute(ends, "gz", pairing("gz")[0])
     blended = call(blend_kernel, size, [VMEM] * 4, [VMEM] * 3, scratch, flops=10**6)(
-        sums, other_sums, statics, ends
+        sums, other_sums, statics, strips
     )
     base = call(
         finish_kernel,

time: 23.2 us -> 23.1 us (level)
  waiting for transfers between devices: 6.56 us -> 5.31 us
  Pallas kernels: 7.34 us -> 8.54 us
    pallas_call x2, Pallas kernels: 2.64 us -> 3.87 us  [the longest x1 3.21 us: on_device(): call(tile_kernel, size, [VMEM] + [HBM] * 7, [VMEM] * 5, [shaped(2, levels...]
    ppermute x2, waiting for transfers between devices: 3.08 us -> 2.13 us  [swapped(): second = lax.ppermute(second, axis, pairs[1])]
  transfers between devices with their start and end apart: 6 -> 6, of which waited for: 5 -> 4; matrix products, arithmetic and copies ran while one was open for 0% -> 0% of each run, Pallas kernels for 15% -> 21%
where the time goes in v5:
time: 23.1 us; the launch traced here: 22.9 us
  Pallas kernels  8.54 us (37%)
  starting transfers between devices  8.33 us (36%)
  waiting for transfers between devices  5.31 us (23%)
  between operations  0.71 us (3%)
    ppermute x2, starting transfers between devices, swapped(): first = lax.ppermute(first, axis, pairs[0])  7.65 us
    pallas_call x1, Pallas kernels, on_device(): call(tile_kernel, size, [VMEM] + [HBM] * 7, [VMEM] * 5, [shaped(2, levels...  3.21 us
    ppermute x2, waiting for transfers between devices, swapped(): first = lax.ppermute(first, axis, pairs[0])  2.89 us
    pallas_call x1, Pallas kernels, on_device(): call(surface_kernel, size, [VMEM] * 7, [HBM] * 3 + [VMEM] * 3, [shaped(ro...  2.23 us
    ppermute x2, waiting for transfers between devices, swapped(): second = lax.ppermute(second, axis, pairs[1])  2.13 us
    pallas_call x1, Pallas kernels, on_device(): call(edge_kernel, size, [HBM] * 8, [VMEM] * 3, [side, side, shaped(2 + le...  1.39 us
    pallas_call x1, Pallas kernels, on_device(): call(finish_kernel, size, [VMEM] * 3, [VMEM], [shaped(2, levels, rows, co...  0.79 us
    pallas_call x1, Pallas kernels, on_device(): call(column_kernel, size, [VMEM] * 5, [VMEM] * 3, [packed, packed, shaped...  0.66 us
  transfers between devices with their start and end apart: 6, of which 4 were waited for; matrix products, arithmetic and copies ran while one was open for 0% of the time, Pallas kernels for 21%

profile of v5, /device:TPU:0, one launch (start us, length us, event | category | flops | bytes accessed | tf_op | source)
XLA Modules:
  0.0 22.9 jit_solution(14911542566405286883)
XLA Ops:
  0.6 1.4 %shard_map.103 = (f32[12,8,128]{2,1,0:T(8,128)S(1)}, f32[12,8,128]{2,1,0:T(8,128)S(1)}, f32[10,8,128]{2,1,0:T(8,128)S(1)}) custom-call(f32[8]{0:T(128)} %thick_hbm.1, f32[8,128,128]{2,1,0:T(8,128)} %east.3, f32[8,128,128]{2,1,0:T(8,128)} %north.3, f32[8,128,128]{2,1,0:T(8,128)} %press.3, f32[128,128]{1,0:T(8,128)} %surface.3, s32[128,128]{1,0:T(8,128)} %land.3, ...), custom_call_target="tpu_custom_call" | custom-call | tf_op jit(solution)/shard_map/pallas_call | solution.py:600
  2.0 5.1 %collective-permute-start = (f32[12,8,128]{2,1,0:T(8,128)S(1)}, f32[12,8,128]{2,1,0:T(8,128)S(1)}, u32[]{:S(2)}, u32[]{:S(2)}) collective-permute-start(f32[12,8,128]{2,1,0:T(8,128)S(1)} %get-tuple-element.26.own_first), channel_id=1, source_target_pairs={{2,4},{4,2},{6,0},{0,6},{3,5},{5,3},{7,1},{1,7},{10,12},{12,10},{1... | collective-permute-start | bytes 147464 | tf_op jit(solution)/shard_map/ppermute | solution.py:581
  7.2 0.0 collective-permute-start.1
  7.2 3.2 %shard_map.104 = (f32[2,8,128,128]{3,2,1,0:T(8,128)S(1)}, f32[5,144,128]{2,1,0:T(8,128)S(1)}, f32[3,144,128]{2,1,0:T(8,128)S(1)}, f32[144,128]{1,0:T(8,128)S(1)}, f32[144,128]{1,0:T(8,128)S(1)}) custom-call(f32[10,8,128]{2,1,0:T(8,128)S(1)} %get-tuple-element.25.weights, f32[8,128,128]{2,1,0:T(8,128)} %east.3, f32[8,128,128]{2,1,0:T(8,128)} %north.3, ...), custom_call_target="tpu_custom_call" | custom-call | flops 10000000 | tf_op jit(solution)/shard_map/pallas_call | solution.py:616
  10.4 0.0 collective-permute-done.got_first
  10.4 0.9 %collective-permute-done.1.got_second = f32[12,8,128]{2,1,0:T(8,128)S(1)} collective-permute-done((f32[12,8,128]{2,1,0:T(8,128)S(1)}, f32[12,8,128]{2,1,0:T(8,128)S(1)}, u32[]{:S(2)}, u32[]{:S(2)}) %collective-permute-start.1) | collective-permute-done | bytes 49184 | tf_op jit(solution)/shard_map/ppermute | solution.py:582
  11.3 0.1 shard_map.105
  11.4 0.1 collective-permute-start.5
  11.5 2.5 %collective-permute-start.2 = (f32[144,128]{1,0:T(8,128)S(1)}, f32[144,128]{1,0:T(8,128)S(1)}, u32[]{:S(2)}, u32[]{:S(2)}) collective-permute-start(f32[144,128]{1,0:T(8,128)S(1)} %get-tuple-element.32.own_first), channel_id=1, source_target_pairs={{8,16},{16,8},{24,0},{0,24},{9,17},{17,9},{25,1},{1,25},{10,18},{1... | collective-permute-start | bytes 221192 | tf_op jit(solution)/shard_map/ppermute | solution.py:581
  14.0 0.5 %collective-permute-start.3 = (f32[144,128]{1,0:T(8,128)S(1)}, f32[144,128]{1,0:T(8,128)S(1)}, u32[]{:S(2)}, u32[]{:S(2)}) collective-permute-start(f32[144,128]{1,0:T(8,128)S(1)} %get-tuple-element.33.own_second), channel_id=1, source_target_pairs={{0,8},{8,0},{16,24},{24,16},{1,9},{9,1},{17,25},{25,17},{2,10},{10... | collective-permute-start | bytes 221192 | tf_op jit(solution)/shard_map/ppermute | solution.py:582
  14.5 2.9 %collective-permute-done.2.got_first = f32[144,128]{1,0:T(8,128)S(1)} collective-permute-done((f32[144,128]{1,0:T(8,128)S(1)}, f32[144,128]{1,0:T(8,128)S(1)}, u32[]{:S(2)}, u32[]{:S(2)}) %collective-permute-start.2) | collective-permute-done | bytes 73760 | tf_op jit(solution)/shard_map/ppermute | solution.py:581
  17.4 1.3 %collective-permute-done.3.got_second = f32[144,128]{1,0:T(8,128)S(1)} collective-permute-done((f32[144,128]{1,0:T(8,128)S(1)}, f32[144,128]{1,0:T(8,128)S(1)}, u32[]{:S(2)}, u32[]{:S(2)}) %collective-permute-start.3) | collective-permute-done | bytes 73760 | tf_op jit(solution)/shard_map/ppermute | solution.py:582
  18.7 0.7 %shard_map.106 = (f32[144,128]{1,0:T(8,128)S(1)}, f32[144,128]{1,0:T(8,128)S(1)}, f32[2,144,128]{2,1,0:T(8,128)S(1)}) custom-call(f32[10,8,128]{2,1,0:T(8,128)S(1)} %get-tuple-element.25.weights, f32[144,128]{1,0:T(8,128)S(1)} %get-tuple-element.32.own_first, f32[144,128]{1,0:T(8,128)S(1)} %get-tuple-element.33.own_second, ...), custom_call_target="tpu_custom_call" | custom-call | tf_op jit(solution)/shard_map/pallas_call | solution.py:656
  19.3 0.1 collective-permute-start.4
  19.4 0.8 %shard_map.107.base = f32[2,8,128,128]{3,2,1,0:T(8,128)S(1)} custom-call(f32[2,144,128]{2,1,0:T(8,128)S(1)} %get-tuple-element.34.column_flux, f32[2,2,8,128]{3,2,1,0:T(8,128)S(1)} %get-tuple-element.35.row_flux, f32[2,8,128,128]{3,2,1,0:T(8,128)S(1)} %get-tuple-element.36.base_in), custom_call_target="tpu_custom_call", output_to_operand_aliasing={{}: (2, {})} | custom-call | flops 10000000 | tf_op jit(solution)/shard_map/pallas_call | solution.py:667
  20.2 0.0 collective-permute-done.5.other
  20.2 0.1 shard_map.108
  20.4 0.3 %collective-permute-done.4.other = f32[144,128]{1,0:T(8,128)S(1)} collective-permute-done((f32[144,128]{1,0:T(8,128)S(1)}, f32[144,128]{1,0:T(8,128)S(1)}, u32[]{:S(2)}, u32[]{:S(2)}) %collective-permute-start.4) | collective-permute-done | bytes 73760 | tf_op jit(solution)/shard_map/ppermute | solution.py:663
  20.7 2.2 %shard_map.109 = (f32[128,128]{1,0:T(8,128)}, f32[8,128,128]{2,1,0:T(8,128)}, f32[8,128,128]{2,1,0:T(8,128)}, f32[2,3,160,128]{3,2,1,0:T(8,128)S(1)}, f32[2,5,16...) custom-call(f32[2,8,128,128]{3,2,1,0:T(8,128)S(1)} %shard_map.107.bas, ...), custom_call_target="tpu_custom_call", output_to_operand_aliasing={{3}: (4, {}), {4}: (5, {}), {5}: (6, {})} | custom-call | tf_op jit(solution)/shard_map/pallas_call | solution.py:677
Async XLA Ops:
  2.0 8.4 %collective-permute-start = (f32[12,8,128]{2,1,0:T(8,128)S(1)}, f32[12,8,128]{2,1,0:T(8,128)S(1)}, u32[]{:S(2)}, u32[]{:S(2)}) collective-permute-start(f32[12,8,128]{2,1,0:T(8,128)S(1)} %get-tuple-element.26.own_first), channel_id=1, source_target_pairs={{2,4},{4,2},{6,0},{0,6},{3,5},{5,3},{7,1},{1,7},{10,12},{12,10},{1... | collective-permute-start | bytes 147464 | tf_op jit(solution)/shard_map/ppermute | solution.py:581
  7.2 4.1 %collective-permute-start.1 = (f32[12,8,128]{2,1,0:T(8,128)S(1)}, f32[12,8,128]{2,1,0:T(8,128)S(1)}, u32[]{:S(2)}, u32[]{:S(2)}) collective-permute-start(f32[12,8,128]{2,1,0:T(8,128)S(1)} %get-tuple-element.27.own_second), channel_id=1, source_target_pairs={{0,2},{2,0},{4,6},{6,4},{1,3},{3,1},{5,7},{7,5},{8,10},{10,8},{12,... | collective-permute-start | bytes 147464 | tf_op jit(solution)/shard_map/ppermute | solution.py:582
  11.4 8.8 %collective-permute-start.5 = (f32[5,144,128]{2,1,0:T(8,128)S(1)}, f32[5,144,128]{2,1,0:T(8,128)S(1)}, u32[]{:S(2)}, u32[]{:S(2)}) collective-permute-start(f32[5,144,128]{2,1,0:T(8,128)S(1)} %get-tuple-element.39.mine), channel_id=1, source_target_pairs={{1,0},{0,1},{3,2},{2,3},{5,4},{4,5},{7,6},{6,7},{9,8},{8,9},{11,10... | collective-permute-start | bytes 1105928 | tf_op jit(solution)/shard_map/ppermute | solution.py:650
  11.5 5.9 %collective-permute-start.2 = (f32[144,128]{1,0:T(8,128)S(1)}, f32[144,128]{1,0:T(8,128)S(1)}, u32[]{:S(2)}, u32[]{:S(2)}) collective-permute-start(f32[144,128]{1,0:T(8,128)S(1)} %get-tuple-element.32.own_first), channel_id=1, source_target_pairs={{8,16},{16,8},{24,0},{0,24},{9,17},{17,9},{25,1},{1,25},{10,18},{1... | collective-permute-start | bytes 221192 | tf_op jit(solution)/shard_map/ppermute | solution.py:581
  14.0 4.7 %collective-permute-start.3 = (f32[144,128]{1,0:T(8,128)S(1)}, f32[144,128]{1,0:T(8,128)S(1)}, u32[]{:S(2)}, u32[]{:S(2)}) collective-permute-start(f32[144,128]{1,0:T(8,128)S(1)} %get-tuple-element.33.own_second), channel_id=1, source_target_pairs={{0,8},{8,0},{16,24},{24,16},{1,9},{9,1},{17,25},{25,17},{2,10},{10... | collective-permute-start | bytes 221192 | tf_op jit(solution)/shard_map/ppermute | solution.py:582
  19.3 1.3 %collective-permute-start.4 = (f32[144,128]{1,0:T(8,128)S(1)}, f32[144,128]{1,0:T(8,128)S(1)}, u32[]{:S(2)}, u32[]{:S(2)}) collective-permute-start(f32[144,128]{1,0:T(8,128)S(1)} %get-tuple-element.38.mine), channel_id=1, source_target_pairs={{1,0},{0,1},{3,2},{2,3},{5,4},{4,5},{7,6},{6,7},{9,8},{8,9},{11,10... | collective-permute-start | bytes 221192 | tf_op jit(solution)/shard_map/ppermute | solution.py:663

commit v6 on v4

--- a/solution.py
+++ b/solution.py
@@ -19,6 +19,7 @@
 F32 = jnp.float32
 
 FIELDS = 8
+GAINS = 95
 SURFACE, COUNT, CORIOLIS = 5, 6, 7
 SUMS = 5
 
@@ -335,7 +336,7 @@
 
 
 def column_kernel(
-    size, weights, own_first, own_second, got_first, got_second, ends, flux,
+    size, weights, own_first, own_second, got_first, got_second, ends, strips, flux,
 ):
     wide, cols, half = size.wide, size.cols, size.half
     first_level = (lax.axis_index("gz") * size.levels).astype(F32)
@@ -364,15 +365,16 @@
     total = weight * to_east + turned(weight * to_west, 4 * REACH)
     for shift in (1, 2, 4):
         total = total + turned(total, shift)
-    sources = [(2 * index + 1) * REACH + end for index in range(2)]
-    ends[1] = jnp.where(
-        among(lane, sources), total, turned(total, -half - 4 * REACH - 1)
-    )
     outer_west = among(lane, (end, 2 * REACH + end))
     outer_east = among(lane, (REACH, 3 * REACH))
     gain = jnp.where(outer_west, turned(total, -5 * REACH), 0.0)
     gain = gain + jnp.where(outer_east, turned(total, -half - end), 0.0)
-    ends[0] = jnp.where(slot_of % 2 == 0, west, east) + gain
+    strips[...] = jnp.where(slot_of % 2 == 0, west, east)
+    for_west = among(lane, [GAINS + 2 * index * REACH for index in range(2)])
+    forces = jnp.where(
+        for_west, turned(total, GAINS - REACH - end), turned(total, GAINS - half - 6 * REACH)
+    )
+    ends[...] = jnp.where(lane < 2 * SUMS * REACH, strips[...] + gain, forces)
 
 
 def finish_kernel(size, column_flux, row_flux, base_in, base):
@@ -414,7 +416,7 @@
     return jnp.where((lane < REACH) | (lane >= size.cols - REACH), moved, 0.0)
 
 
-def blend_kernel(size, mine, other, statics, ends, state, fixed, drive):
+def blend_kernel(size, mine, other, statics, strips, state, fixed, drive):
     here = slice(REACH, REACH + size.wide)
     total = [mine[index] + other[index] for index in range(SUMS)]
     ocean = jnp.where(statics[1] > 0, 1.0, 0.0)
@@ -426,7 +428,7 @@
     drive[0] = total[2] + TIMESTEP * total[0]
     drive[1] = total[3] + TIMESTEP * total[1]
     drive[2] = total[4] + (1.0 - ocean)
-    strips = ends[0]
+    strips = strips[...]
     ocean = jnp.where(strip_field(size, strips, COUNT) > 0, 1.0, 0.0)
     fixed[1, STEP, here, :] = 0.5 * COURANT * ocean
     fixed[1, TURN, here, :] = COURANT * ocean * strip_field(size, strips, CORIOLIS)
@@ -444,7 +446,7 @@
     first_level = (lax.axis_index("gz") * levels).astype(F32)
 
     here, lane = slice(REACH, REACH + wide), lane_ids(wide, cols)
-    strips = mine[0] + other[0]
+    strips = mine[...] + other[...]
     force_east, force_north, sum_east, sum_north, depth = (
         strip_field(size, strips, index) for index in range(SUMS)
     )
@@ -454,9 +456,8 @@
     fixed[1, PUSH_N, here, :] = 2.0 * step * force_north
     state[1, TE, here, :] = sum_east
     state[1, TN, here, :] = sum_north
-    gains = mine[1] + other[1]
     for index, push in ((0, PUSH_E), (1, PUSH_N)):
-        gain = turned(gains, -((2 * index + 1) * REACH + REACH - 1))
+        gain = turned(strips, -GAINS - 2 * index * REACH)
         gain = jnp.where((lane == 0) | (lane == cols - 1), gain, 0.0)
         fixed[0, push, here, :] = (
             fixed[0, push, here, :] + 2.0 * fixed[0, STEP, here, :] * gain
@@ -625,16 +626,16 @@
         shaped(2, 5, wide + 2 * REACH, cols),
         shaped(3, wide, cols),
     ]
-    ends, column_flux = call(
+    ends, strips, column_flux = call(
         column_kernel,
         size,
         [VMEM] * 5,
-        [VMEM] * 2,
-        [shaped(2, wide, cols), shaped(2, wide, cols)],
+        [VMEM] * 3,
+        [packed, packed, shaped(2, wide, cols)],
     )(weights, x_first, x_second, *got_x)
     other_ends = lax.ppermute(ends, "gz", pairing("gz")[0])
     blended = call(blend_kernel, size, [VMEM] * 4, [VMEM] * 3, scratch, flops=10**6)(
-        sums, other_sums, statics, ends
+        sums, other_sums, statics, strips
     )
     base = call(
         finish_kernel,

time: 23.2 us -> 23.3 us (level)
  transfers between devices with their start and end apart: 6 -> 6, of which waited for: 5 -> 5; matrix products, arithmetic and copies ran while one was open for 0% -> 0% of each run, Pallas kernels for 15% -> 16%
where the time goes in v6:
time: 23.3 us; the launch traced here: 23.1 us
  starting transfers between devices  8.33 us (36%)
  Pallas kernels  7.49 us (32%)
  waiting for transfers between devices  6.44 us (28%)
  between operations  0.81 us (3%)
    ppermute x2, starting transfers between devices, swapped(): first = lax.ppermute(first, axis, pairs[0])  7.65 us
    ppermute x2, waiting for transfers between devices, swapped(): second = lax.ppermute(second, axis, pairs[1])  3.08 us
    ppermute x2, waiting for transfers between devices, swapped(): first = lax.ppermute(first, axis, pairs[0])  3.07 us
    pallas_call x1, Pallas kernels, on_device(): call(surface_kernel, size, [VMEM] * 7, [HBM] * 3 + [VMEM] * 3, [shaped(ro...  2.25 us
    pallas_call x1, Pallas kernels, on_device(): call(tile_kernel, size, [VMEM] * 8, [VMEM] * 5, [shaped(2, levels, rows,...  2.02 us
    pallas_call x1, Pallas kernels, on_device(): call(edge_kernel, size, [HBM] * 8, [VMEM] * 3, [side, side, shaped(2 + le...  1.51 us
    pallas_call x1, Pallas kernels, on_device(): call(finish_kernel, size, [VMEM] * 3, [VMEM], [shaped(2, levels, rows, co...  0.79 us
    pallas_call x1, Pallas kernels, on_device(): call(column_kernel, size, [VMEM] * 5, [VMEM] * 3, [packed, packed, shaped...  0.66 us
  transfers between devices with their start and end apart: 6, of which 5 were waited for; matrix products, arithmetic and copies ran while one was open for 0% of the time, Pallas kernels for 16%

profile of v6, /device:TPU:0, one launch (start us, length us, event | category | flops | bytes accessed | tf_op | source)
XLA Modules:
  0.0 23.1 jit_solution(10097004175875123281)
XLA Ops:
  0.6 0.0 copy-start.6
  0.6 0.0 copy-start.5
  0.7 0.0 copy-start.4
  0.7 0.0 copy-start.3
  0.7 0.0 copy-start.2
  0.7 0.0 copy-start.1
  0.7 0.0 copy-start
  0.7 1.5 %shard_map.103 = (f32[12,8,128]{2,1,0:T(8,128)S(1)}, f32[12,8,128]{2,1,0:T(8,128)S(1)}, f32[10,8,128]{2,1,0:T(8,128)S(1)}) custom-call(f32[8]{0:T(128)} %thick_hbm.1, f32[8,128,128]{2,1,0:T(8,128)} %east.3, f32[8,128,128]{2,1,0:T(8,128)} %north.3, f32[8,128,128]{2,1,0:T(8,128)} %press.3, f32[128,128]{1,0:T(8,128)} %surface.3, s32[128,128]{1,0:T(8,128)} %land.3, ...), custom_call_target="tpu_custom_call" | custom-call | tf_op jit(solution)/shard_map/pallas_call | solution.py:575
  2.2 5.1 %collective-permute-start = (f32[12,8,128]{2,1,0:T(8,128)S(1)}, f32[12,8,128]{2,1,0:T(8,128)S(1)}, u32[]{:S(2)}, u32[]{:S(2)}) collective-permute-start(f32[12,8,128]{2,1,0:T(8,128)S(1)} %get-tuple-element.26.own_first), channel_id=1, source_target_pairs={{2,4},{4,2},{6,0},{0,6},{3,5},{5,3},{7,1},{1,7},{10,12},{12,10},{1... | collective-permute-start | bytes 147464 | tf_op jit(solution)/shard_map/ppermute | solution.py:556
  7.4 0.0 collective-permute-start.1
  7.4 0.0 copy-done.6
  7.4 0.0 copy-done.4
  7.4 0.0 copy-done.3
  7.4 0.0 copy-done.2
  7.4 0.0 copy-done.1
  7.4 0.0 copy-done
  7.4 2.0 %shard_map.104 = (f32[2,8,128,128]{3,2,1,0:T(8,128)S(1)}, f32[5,144,128]{2,1,0:T(8,128)S(1)}, f32[3,144,128]{2,1,0:T(8,128)S(1)}, f32[144,128]{1,0:T(8,128)S(1)}, f32[144,128]{1,0:T(8,128)S(1)}) custom-call(f32[10,8,128]{2,1,0:T(8,128)S(1)} %get-tuple-element.25.weights, f32[8,128,128]{2,1,0:T(8,128)S(1)} %copy-done, f32[8,128,128]{2,1,0:T(8,128)S(1)} %copy-done.1, ...), custom_call_target="tpu_custom_call" | custom-call | flops 10000000 | tf_op jit(solution)/shard_map/pallas_call | solution.py:591
  9.5 0.2 collective-permute-done.got_first
  9.6 1.8 %collective-permute-done.1.got_second = f32[12,8,128]{2,1,0:T(8,128)S(1)} collective-permute-done((f32[12,8,128]{2,1,0:T(8,128)S(1)}, f32[12,8,128]{2,1,0:T(8,128)S(1)}, u32[]{:S(2)}, u32[]{:S(2)}) %collective-permute-start.1) | collective-permute-done | bytes 49184 | tf_op jit(solution)/shard_map/ppermute | solution.py:557
  11.5 0.1 shard_map.105
  11.6 0.1 collective-permute-start.5
  11.7 2.5 %collective-permute-start.2 = (f32[144,128]{1,0:T(8,128)S(1)}, f32[144,128]{1,0:T(8,128)S(1)}, u32[]{:S(2)}, u32[]{:S(2)}) collective-permute-start(f32[144,128]{1,0:T(8,128)S(1)} %get-tuple-element.32.own_first), channel_id=1, source_target_pairs={{8,16},{16,8},{24,0},{0,24},{9,17},{17,9},{25,1},{1,25},{10,18},{1... | collective-permute-start | bytes 221192 | tf_op jit(solution)/shard_map/ppermute | solution.py:556
  14.2 0.5 %collective-permute-start.3 = (f32[144,128]{1,0:T(8,128)S(1)}, f32[144,128]{1,0:T(8,128)S(1)}, u32[]{:S(2)}, u32[]{:S(2)}) collective-permute-start(f32[144,128]{1,0:T(8,128)S(1)} %get-tuple-element.33.own_second), channel_id=1, source_target_pairs={{0,8},{8,0},{16,24},{24,16},{1,9},{9,1},{17,25},{25,17},{2,10},{10... | collective-permute-start | bytes 221192 | tf_op jit(solution)/shard_map/ppermute | solution.py:557
  14.7 2.9 %collective-permute-done.2.got_first = f32[144,128]{1,0:T(8,128)S(1)} collective-permute-done((f32[144,128]{1,0:T(8,128)S(1)}, f32[144,128]{1,0:T(8,128)S(1)}, u32[]{:S(2)}, u32[]{:S(2)}) %collective-permute-start.2) | collective-permute-done | bytes 73760 | tf_op jit(solution)/shard_map/ppermute | solution.py:556
  17.6 1.3 %collective-permute-done.3.got_second = f32[144,128]{1,0:T(8,128)S(1)} collective-permute-done((f32[144,128]{1,0:T(8,128)S(1)}, f32[144,128]{1,0:T(8,128)S(1)}, u32[]{:S(2)}, u32[]{:S(2)}) %collective-permute-start.3) | collective-permute-done | bytes 73760 | tf_op jit(solution)/shard_map/ppermute | solution.py:557
  18.9 0.7 %shard_map.106 = (f32[144,128]{1,0:T(8,128)S(1)}, f32[144,128]{1,0:T(8,128)S(1)}, f32[2,144,128]{2,1,0:T(8,128)S(1)}) custom-call(f32[10,8,128]{2,1,0:T(8,128)S(1)} %get-tuple-element.25.weights, f32[144,128]{1,0:T(8,128)S(1)} %get-tuple-element.32.own_first, f32[144,128]{1,0:T(8,128)S(1)} %get-tuple-element.33.own_second, ...), custom_call_target="tpu_custom_call" | custom-call | tf_op jit(solution)/shard_map/pallas_call | solution.py:629
  19.5 0.1 collective-permute-start.4
  19.6 0.8 %shard_map.107.base = f32[2,8,128,128]{3,2,1,0:T(8,128)S(1)} custom-call(f32[2,144,128]{2,1,0:T(8,128)S(1)} %get-tuple-element.34.column_flux, f32[2,2,8,128]{3,2,1,0:T(8,128)S(1)} %get-tuple-element.35.row_flux, f32[2,8,128,128]{3,2,1,0:T(8,128)S(1)} %get-tuple-element.36.base_in), custom_call_target="tpu_custom_call", output_to_operand_aliasing={{}: (2, {})} | custom-call | flops 10000000 | tf_op jit(solution)/shard_map/pallas_call | solution.py:640
  20.4 0.0 collective-permute-done.5.other
  20.4 0.1 shard_map.108
  20.6 0.3 %collective-permute-done.4.other = f32[144,128]{1,0:T(8,128)S(1)} collective-permute-done((f32[144,128]{1,0:T(8,128)S(1)}, f32[144,128]{1,0:T(8,128)S(1)}, u32[]{:S(2)}, u32[]{:S(2)}) %collective-permute-start.4) | collective-permute-done | bytes 73760 | tf_op jit(solution)/shard_map/ppermute | solution.py:636
  20.9 2.2 %shard_map.109 = (f32[128,128]{1,0:T(8,128)}, f32[8,128,128]{2,1,0:T(8,128)}, f32[8,128,128]{2,1,0:T(8,128)}, f32[2,3,160,128]{3,2,1,0:T(8,128)S(1)}, f32[2,5,16...) custom-call(f32[2,8,128,128]{3,2,1,0:T(8,128)S(1)} %shard_map.107.bas, ...), custom_call_target="tpu_custom_call", output_to_operand_aliasing={{3}: (4, {}), {4}: (5, {}), {5}: (6, {})} | custom-call | tf_op jit(solution)/shard_map/pallas_call | solution.py:650
  (1 shorter events, 0.0 us)
Async XLA Ops:
  0.6 6.7 %copy-start.6 = (f32[128,128]{1,0:T(8,128)S(1)}, f32[128,128]{1,0:T(8,128)}, u32[]{:S(2)}) copy-start(f32[128,128]{1,0:T(8,128)} %coriolis.3) | copy-start | bytes 196612
  0.6 6.7 %copy-start.5 = (s32[128,128]{1,0:T(8,128)S(1)}, s32[128,128]{1,0:T(8,128)}, u32[]{:S(2)}) copy-start(s32[128,128]{1,0:T(8,128)} %bottom.3) | copy-start | bytes 196612
  0.7 6.7 %copy-start.4 = (s32[128,128]{1,0:T(8,128)S(1)}, s32[128,128]{1,0:T(8,128)}, u32[]{:S(2)}) copy-start(s32[128,128]{1,0:T(8,128)} %land.3) | copy-start | bytes 196612
  0.7 6.7 %copy-start.3 = (f32[128,128]{1,0:T(8,128)S(1)}, f32[128,128]{1,0:T(8,128)}, u32[]{:S(2)}) copy-start(f32[128,128]{1,0:T(8,128)} %surface.3) | copy-start | bytes 196612
  0.7 6.7 %copy-start.2 = (f32[8,128,128]{2,1,0:T(8,128)S(1)}, f32[8,128,128]{2,1,0:T(8,128)}, u32[]{:S(2)}) copy-start(f32[8,128,128]{2,1,0:T(8,128)} %press.3) | copy-start | bytes 1572868
  0.7 6.7 %copy-start.1 = (f32[8,128,128]{2,1,0:T(8,128)S(1)}, f32[8,128,128]{2,1,0:T(8,128)}, u32[]{:S(2)}) copy-start(f32[8,128,128]{2,1,0:T(8,128)} %north.3) | copy-start | bytes 1572868
  0.7 6.7 %copy-start = (f32[8,128,128]{2,1,0:T(8,128)S(1)}, f32[8,128,128]{2,1,0:T(8,128)}, u32[]{:S(2)}) copy-start(f32[8,128,128]{2,1,0:T(8,128)} %east.3) | copy-start | bytes 1572868
  2.2 7.4 %collective-permute-start = (f32[12,8,128]{2,1,0:T(8,128)S(1)}, f32[12,8,128]{2,1,0:T(8,128)S(1)}, u32[]{:S(2)}, u32[]{:S(2)}) collective-permute-start(f32[12,8,128]{2,1,0:T(8,128)S(1)} %get-tuple-element.26.own_first), channel_id=1, source_target_pairs={{2,4},{4,2},{6,0},{0,6},{3,5},{5,3},{7,1},{1,7},{10,12},{12,10},{1... | collective-permute-start | bytes 147464 | tf_op jit(solution)/shard_map/ppermute | solution.py:556
  7.4 4.1 %collective-permute-start.1 = (f32[12,8,128]{2,1,0:T(8,128)S(1)}, f32[12,8,128]{2,1,0:T(8,128)S(1)}, u32[]{:S(2)}, u32[]{:S(2)}) collective-permute-start(f32[12,8,128]{2,1,0:T(8,128)S(1)} %get-tuple-element.27.own_second), channel_id=1, source_target_pairs={{0,2},{2,0},{4,6},{6,4},{1,3},{3,1},{5,7},{7,5},{8,10},{10,8},{12,... | collective-permute-start | bytes 147464 | tf_op jit(solution)/shard_map/ppermute | solution.py:557
  11.6 8.8 %collective-permute-start.5 = (f32[5,144,128]{2,1,0:T(8,128)S(1)}, f32[5,144,128]{2,1,0:T(8,128)S(1)}, u32[]{:S(2)}, u32[]{:S(2)}) collective-permute-start(f32[5,144,128]{2,1,0:T(8,128)S(1)} %get-tuple-element.39.mine), channel_id=1, source_target_pairs={{1,0},{0,1},{3,2},{2,3},{5,4},{4,5},{7,6},{6,7},{9,8},{8,9},{11,10... | collective-permute-start | bytes 1105928 | tf_op jit(solution)/shard_map/ppermute | solution.py:623
  11.7 5.9 %collective-permute-start.2 = (f32[144,128]{1,0:T(8,128)S(1)}, f32[144,128]{1,0:T(8,128)S(1)}, u32[]{:S(2)}, u32[]{:S(2)}) collective-permute-start(f32[144,128]{1,0:T(8,128)S(1)} %get-tuple-element.32.own_first), channel_id=1, source_target_pairs={{8,16},{16,8},{24,0},{0,24},{9,17},{17,9},{25,1},{1,25},{10,18},{1... | collective-permute-start | bytes 221192 | tf_op jit(solution)/shard_map/ppermute | solution.py:556
  14.2 4.7 %collective-permute-start.3 = (f32[144,128]{1,0:T(8,128)S(1)}, f32[144,128]{1,0:T(8,128)S(1)}, u32[]{:S(2)}, u32[]{:S(2)}) collective-permute-start(f32[144,128]{1,0:T(8,128)S(1)} %get-tuple-element.33.own_second), channel_id=1, source_target_pairs={{0,8},{8,0},{16,24},{24,16},{1,9},{9,1},{17,25},{25,17},{2,10},{10... | collective-permute-start | bytes 221192 | tf_op jit(solution)/shard_map/ppermute | solution.py:557
  19.5 1.3 %collective-permute-start.4 = (f32[144,128]{1,0:T(8,128)S(1)}, f32[144,128]{1,0:T(8,128)S(1)}, u32[]{:S(2)}, u32[]{:S(2)}) collective-permute-start(f32[144,128]{1,0:T(8,128)S(1)} %get-tuple-element.38.mine), channel_id=1, source_target_pairs={{1,0},{0,1},{3,2},{2,3},{5,4},{4,5},{7,6},{6,7},{9,8},{8,9},{11,10... | collective-permute-start | bytes 221192 | tf_op jit(solution)/shard_map/ppermute | solution.py:636
